TPU v7x, 32 devices: a whole 2x2x4 slice. The times are simulated.
32 devices in a mesh: lon: 8 (over z, y), lat: 4 (over x, core).
Axes of the slice: x: 2, y: 2, z: 4, core: 2. Of those that a mesh axis runs over, the one named last changes fastest.
Arguments:
- inputs: bfloat16 [32, 1024, 512], P('lat', 'lon'), may hold values from -6 to 6
- d_out: bfloat16 [32, 1024, 512], P('lat', 'lon'), may hold values from -6 to 6
- w_qkv: bfloat16 [512, 1536], replicated, may hold values from -0.25 to 0.25
- w_proj: bfloat16 [512, 512], replicated, may hold values from -0.25 to 0.25
- gain: float32 [512], replicated, may hold values from 0.1 to 1.9
- bias_table: float32 [465, 16], replicated, may hold values from -400 to 400
- rel_index: int32 [128, 128], replicated, may hold values from 0 to 464, as said below
- shifts: int32 [4], P('lat'), may hold values from 1 to 15, as said below
Outputs:
- d_inputs: bfloat16 [32, 1024, 512], P('lat', 'lon')
- g_qkv: float32 [512, 1536], P(('lon', 'lat'))
- g_proj: float32 [512, 512], P(('lon', 'lat'))
- g_gain: float32 [512], P(('lon', 'lat'))
- g_table: float32 [465, 16], replicated
Inputs may be any that keep to these rules, and one draw needn't show every extreme that they name: `rel_index`: entry (i, j) depends only on the row and column offsets between window positions i and j, and distinct offsets give distinct entries. `shifts`: some band is shifted by 16 - 1.
All inputs are finite; a program needn't handle non-finite values.
Results may differ from a plain program's by a relative error of at most 0.0095.
Values may be sent and summed in bfloat16 or wider, within the bound.
No kernel may reach another device: no remote copies, remote signals or barrier semaphores. Data moves between devices by JAX's collectives and lax.ppermute only.
A program may use at most 128 MiB of HBM per device.

v0:
```python
import math

import jax
import jax.numpy as jnp
from jax import lax
from jax.experimental import pallas as pl
from jax.experimental.pallas import tpu as pltpu
from jax.sharding import PartitionSpec as P

H = 16
HD = 32
WH = 8
WW = 16
WIN = WH * WW
LANES = 128
SLAB = LANES // HD
SPANS = WH + 1
EPSILON = 1e-05
LOG2E = math.log2(math.e)
BF = jnp.bfloat16
F32 = jnp.float32


def dot(left, right):
    return lax.dot_general(left, right, (((1,), (0,)), ((), ())), preferred_element_type=F32)


def dot_nt(left, right):
    return lax.dot_general(left, right, (((1,), (1,)), ((), ())), preferred_element_type=F32)


def split3(value):
    high = value.astype(BF)
    rest = value - high.astype(F32)
    middle = rest.astype(BF)
    low = (rest - middle.astype(F32)).astype(BF)
    return jnp.concatenate([high, middle, low], axis=0)


def joined3(value):
    rows = value.shape[0] // 3
    return (value[:rows] + value[rows : 2 * rows]) + value[2 * rows :]


def odd_lanes(rows):
    lane = lax.broadcasted_iota(jnp.int32, (rows, LANES), 1)
    return (lane // WW) % 2 == 1


def bias_kernel(code_ref, table_ref, hot_ref, bias_ref, span_ref):
    entries, width = hot_ref.shape
    entry = lax.broadcasted_iota(jnp.int32, (entries, width), 0)
    hot = jnp.where(entry == code_ref[...], 1.0, 0.0).astype(BF)
    hot_ref[...] = hot
    spans = joined3(dot(split3(table_ref[...]), hot)) * LOG2E
    span_ref[...] = spans
    odd = odd_lanes(WW)

    for h in range(H):
        for row in range(WH):
            halves = []
            for parity in range(2):
                first = parity - row + WH - 1
                line = span_ref[h : h + 1, first * LANES : (first + 1) * LANES]
                line = jnp.broadcast_to(line, (WW, LANES))
                turn = (LANES - (WW - 1) + WW * parity) % LANES
                halves.append(pltpu.roll(line, turn, 1, stride=1, stride_axis=0))
            bias_ref[h, row * WW : (row + 1) * WW, :] = jnp.where(odd, halves[1], halves[0])


def expand_bias(code, table):
    entries, width = table.shape[1], code.shape[1]
    return pl.pallas_call(
        bias_kernel,
        out_shape=(
            jax.ShapeDtypeStruct((entries, width), BF),
            jax.ShapeDtypeStruct((H, WIN, WIN), F32),
        ),
        scratch_shapes=[pltpu.VMEM((H, width), F32)],
        name="expand_bias",
    )(code, table)


def norm_stats(rows):
    centred = rows - jnp.mean(rows, axis=-1, keepdims=True)
    inv_std = lax.rsqrt(jnp.mean(centred * centred, axis=-1, keepdims=True) + EPSILON)
    return centred * inv_std, inv_std


def pair_rows(first, second):
    both = jnp.concatenate([first, second], axis=1)
    return both.reshape(both.shape[0] * both.shape[1], both.shape[2])


def shift_matrix(offset):
    row = lax.broadcasted_iota(jnp.int32, (WIN, 2 * WIN), 0)
    col = lax.broadcasted_iota(jnp.int32, (WIN, 2 * WIN), 1)
    same = (row // WW) == (col // (2 * WW))
    hit = same & ((col % (2 * WW)) == (row % WW) + offset)
    return jnp.where(hit, 1.0, 0.0).astype(BF)


def project_kernel(
    shift_ref, xprev_ref, xcur_ref, dprev_ref, dcur_ref, wq_ref, wp_ref, gain_ref, *rest
):
    x_ref, d_ref, nt_ref, qkv_ref, dh_ref, wpt_ref = rest[-6:]

    @pl.when(pl.program_id(0) == 0)
    def _():
        wpt_ref[...] = wp_ref[...].T

    select = shift_matrix(WW - shift_ref[0])
    rows = dot(select, pair_rows(xprev_ref[...], xcur_ref[...]))
    x_ref[0] = rows.astype(BF)
    normal, _ = norm_stats(rows)
    normed = (normal * gain_ref[...]).astype(BF)
    nt_ref[...] = normed.T
    qkv_ref[0] = dot(normed, wq_ref[...]).astype(BF)
    grads = dot(select, pair_rows(dprev_ref[...], dcur_ref[...])).astype(BF)
    d_ref[0] = grads
    dh_ref[0] = dot(grads, wpt_ref[...]).astype(BF)


def project(shift, x, d, w_qkv, w_proj, gain, halo=None, carried=None):
    c = x.shape[-1]
    count = x.shape[1] // WW
    block = (WH, WW, c)
    if carried is None:
        base, steps = 1, count - 1
        prev_x, prev_d = x, d
        more, alias = (), {}
    else:
        base, steps = 0, 1
        prev_x, prev_d = halo
        more, alias = carried, {8 + n: n for n in range(5)}
    full = pl.BlockSpec(memory_space=pl.ANY)
    return pl.pallas_call(
        project_kernel,
        grid=(steps,),
        in_specs=[
            pl.BlockSpec(memory_space=pltpu.SMEM),
            pl.BlockSpec(block, lambda w: (0, w, 0)),
            pl.BlockSpec(block, lambda w: (0, w + base, 0)),
            pl.BlockSpec(block, lambda w: (0, w, 0)),
            pl.BlockSpec(block, lambda w: (0, w + base, 0)),
            pl.BlockSpec(w_qkv.shape, lambda w: (0, 0)),
            pl.BlockSpec(w_proj.shape, lambda w: (0, 0)),
            pl.BlockSpec(gain.shape, lambda w: (0, 0)),
        ]
        + [full for _ in more],
        out_specs=[
            pl.BlockSpec((1, WIN, c), lambda w: (w + base, 0, 0)),
            pl.BlockSpec((1, WIN, c), lambda w: (w + base, 0, 0)),
            pl.BlockSpec((c, WIN), lambda w: (0, w + base)),
            pl.BlockSpec((1, WIN, 3 * c), lambda w: (w + base, 0, 0)),
            pl.BlockSpec((1, WIN, c), lambda w: (w + base, 0, 0)),
        ],
        out_shape=[
            jax.ShapeDtypeStruct((count, WIN, c), BF),
            jax.ShapeDtypeStruct((count, WIN, c), BF),
            jax.ShapeDtypeStruct((c, count * WIN), BF),
            jax.ShapeDtypeStruct((count, WIN, 3 * c), BF),
            jax.ShapeDtypeStruct((count, WIN, c), BF),
        ],
        scratch_shapes=[pltpu.VMEM(w_proj.shape, BF)],
        input_output_aliases=alias,
        name="project_rest" if carried is None else "project_rim",
    )(shift, prev_x, x, prev_d, d, w_qkv, w_proj, gain, *more)


def own_blocks(turned):
    rows = []
    for a in range(SLAB):
        part = turned[a * HD : (a + 1) * HD]
        gap = jnp.zeros_like(part)
        rows.append(jnp.concatenate([part if b == a else gap for b in range(SLAB)], axis=1))
    return jnp.concatenate(rows, axis=0)


def own_lanes(slab):
    lane = lax.broadcasted_iota(jnp.int32, slab.shape, 1)
    return jnp.concatenate(
        [jnp.where(lane // HD == a, slab, jnp.zeros_like(slab)) for a in range(SLAB)], axis=0
    )


def attend_slab(q, k, v, dh, bias_ref, sum_ref, first):
    factor = HD ** (-0.5)
    k_turned, v_turned = k.T, v.T
    scores = dot(k, own_blocks(q.T))
    d_soft = dot(v, own_blocks(dh.T))
    soft_all, d_all, att, dq = [], [], [], []
    for a in range(SLAB):
        lanes = slice(a * WIN, (a + 1) * WIN)
        part = slice(a * HD, (a + 1) * HD)
        score = scores[:, lanes] * (factor * LOG2E) + bias_ref[first + a]
        raised = jnp.exp2(score - jnp.max(score, axis=0, keepdims=True))
        attention = raised * (1.0 / jnp.sum(raised, axis=0, keepdims=True))
        soft_low = attention.astype(BF)
        soft = d_soft[:, lanes]
        d_score = attention * (soft - jnp.sum(attention * soft, axis=0, keepdims=True))
        sum_ref[first + a] += d_score
        d_low = d_score.astype(BF)
        soft_all.append(soft_low)
        d_all.append(d_low)
        att.append(dot(v_turned[part], soft_low))
        dq.append(dot(k_turned[part], d_low))
    att = jnp.concatenate(att, axis=0).astype(BF)
    dq = (jnp.concatenate(dq, axis=0) * factor).astype(BF).T
    dk = (dot(jnp.concatenate(d_all, axis=1), own_lanes(q)) * factor).astype(BF)
    dv = dot(jnp.concatenate(soft_all, axis=1), own_lanes(dh)).astype(BF)
    return att, dq, dk, dv


def fold_table(sum_ref, hot_ref, row_ref, heads):
    odd = odd_lanes(WH)
    for h in range(heads):
        sums = [None, None]
        for col in range(WW):
            tile = sum_ref[h, pl.ds(col, WH, stride=WW), :]
            for parity in range(2):
                kept = jnp.where(odd, tile, 0.0) if parity else jnp.where(odd, 0.0, tile)
                moved = pltpu.roll(kept, (WW - 1 - col - WW * parity) % LANES, 1)
                sums[parity] = moved if col == 0 else sums[parity] + moved
        for parity in range(2):
            row_ref[h, parity * WH : (parity + 1) * WH, :] = sums[parity]
    spans = []
    for first in range(SPANS):
        span = None
        for parity in range(2):
            row = parity + WH - 1 - first
            if 0 <= row < WH:
                part = row_ref[:, parity * WH + row, :]
                span = part if span is None else span + part
        spans.append(span)
    return joined3(dot_nt(split3(jnp.concatenate(spans, axis=1)), hot_ref[...]))


def attend_kernel(scales, last, *refs):
    q_ref, k_ref, v_ref, dh_ref, bias_ref, hot_ref, nt_ref, d_ref = refs[:8]
    if last:
        att0_ref = refs[8]
        dp_ref, grad_ref, table_ref = refs[9:12]
    else:
        dp_ref, att_out_ref, grad_ref, table_ref = refs[8:12]
    att_ref, sum_ref, row_ref = refs[12:]
    w = pl.program_id(0)
    heads = bias_ref.shape[0]
    slabs = heads // SLAB
    wide = slabs * LANES

    @pl.when(w == 0)
    def _():
        sum_ref[...] = jnp.zeros_like(sum_ref)

    for s in range(slabs):
        lanes = slice(s * LANES, (s + 1) * LANES)
        att, dq, dk, dv = attend_slab(
            q_ref[0, :, lanes],
            k_ref[0, :, lanes],
            v_ref[0, :, lanes],
            dh_ref[0, :, lanes],
            bias_ref,
            sum_ref,
            s * SLAB,
        )
        att_ref[lanes, pl.ds(pl.multiple_of(w * WIN, WIN), WIN)] = att
        for n, part in enumerate((dq, dk, dv)):
            dp_ref[w, :, n * wide + s * LANES : n * wide + (s + 1) * LANES] = part

    @pl.when(w == pl.num_programs(0) - 1)
    def _():
        grad_scale, table_scale = scales
        count = dp_ref.shape[0]
        tokens = count * WIN
        c = nt_ref.shape[0]
        grad = dot(nt_ref[...], dp_ref[...].reshape(tokens, 3 * wide))
        grad_ref[:, : 3 * wide] = (grad * grad_scale).astype(BF)
        if last:
            d_rows = d_ref[...].reshape(tokens, c)
            grad = dot(att0_ref[...], d_rows)
            grad_ref[: c - wide, 3 * wide :] = (grad * grad_scale).astype(BF)
            grad = dot(att_ref[...], d_rows)
            grad_ref[c - wide :, 3 * wide :] = (grad * grad_scale).astype(BF)
        else:
            att_out_ref[...] = att_ref[...]
        table_ref[...] = fold_table(sum_ref, hot_ref, row_ref, heads) * table_scale


def attend(group, groups, qkv, dh, bias, hot, nt, d, scales, att0=None):
    count, _, c = dh.shape
    heads = H // groups
    wide = heads * HD
    tokens = count * WIN
    last = att0 is not None
    entries = hot.shape[0]

    def lane_block(n):
        return pl.BlockSpec((1, WIN, wide), lambda w: (w, 0, n))

    def whole(array):
        return pl.BlockSpec(array.shape, lambda w: (0,) * array.ndim)

    columns = 3 * wide + (c if last else 0)
    outs = [jax.ShapeDtypeStruct((count, WIN, 3 * wide), BF)]
    if not last:
        outs.append(jax.ShapeDtypeStruct((wide, tokens), BF))
    outs.append(jax.ShapeDtypeStruct((c, columns), BF))
    outs.append(jax.ShapeDtypeStruct((heads, entries), F32))
    args = [qkv, qkv, qkv, dh, bias, hot, nt, d] + ([att0] if last else [])
    return pl.pallas_call(
        lambda *refs: attend_kernel(scales, last, *refs),
        grid=(count,),
        in_specs=[
            lane_block(group),
            lane_block(groups + group),
            lane_block(2 * groups + group),
            lane_block(group),
            pl.BlockSpec((heads, WIN, WIN), lambda w: (group, 0, 0)),
            whole(hot),
            whole(nt),
            whole(d),
        ]
        + ([whole(att0)] if last else []),
        out_specs=[whole(o) for o in outs],
        out_shape=outs,
        scratch_shapes=[
            pltpu.VMEM((wide, tokens), BF),
            pltpu.VMEM((heads, WIN, WIN), F32),
            pltpu.VMEM((heads, 2 * WH, LANES), F32),
        ],
        name=f"attend_{group}",
    )(*args)


def input_kernel(groups, *refs):
    dp_refs = refs[:groups]
    x_ref, d_ref, w_ref, gain_ref, out_ref, wt_ref = refs[groups:]
    c = x_ref.shape[-1]

    @pl.when(pl.program_id(0) == 0)
    def _():
        wt_ref[...] = w_ref[...].T

    wide = dp_refs[0].shape[-1] // 3
    d_normed = None
    for n in range(3):
        for g in range(groups):
            part = dot(
                dp_refs[g][0, :, n * wide : (n + 1) * wide],
                wt_ref[n * c + g * wide : n * c + (g + 1) * wide, :],
            )
            d_normed = part if d_normed is None else d_normed + part
    normal, inv_std = norm_stats(x_ref[0].astype(F32))
    scaled = d_normed * gain_ref[...]
    branch = inv_std * (
        scaled
        - jnp.mean(scaled, axis=-1, keepdims=True)
        - normal * jnp.mean(scaled * normal, axis=-1, keepdims=True)
    )
    out_ref[0] = (d_ref[0].astype(F32) + branch).astype(BF)


def input_grad(dps, x, d, w_qkv, gain):
    count, _, c = x.shape
    groups = len(dps)
    return pl.pallas_call(
        lambda *refs: input_kernel(groups, *refs),
        grid=(count,),
        in_specs=[pl.BlockSpec((1, WIN, dp.shape[-1]), lambda w: (w, 0, 0)) for dp in dps]
        + [
            pl.BlockSpec((1, WIN, c), lambda w: (w, 0, 0)),
            pl.BlockSpec((1, WIN, c), lambda w: (w, 0, 0)),
            pl.BlockSpec(w_qkv.shape, lambda w: (0, 0)),
            pl.BlockSpec(gain.shape, lambda w: (0, 0)),
        ],
        out_specs=pl.BlockSpec((1, WIN, c), lambda w: (w, 0, 0)),
        out_shape=jax.ShapeDtypeStruct((count, WIN, c), BF),
        scratch_shapes=[pltpu.VMEM(w_qkv.shape[::-1], BF)],
        name="input_grad",
    )(*dps, x, d, w_qkv, gain)


def place_kernel(shift_ref, cur_ref, next_ref, rim_ref, out_ref):
    w = pl.program_id(0)
    final = w == pl.num_programs(0) - 1
    cur = cur_ref[0].reshape(WH, WW, cur_ref.shape[-1])
    after = jnp.where(final, rim_ref[0], next_ref[0]).reshape(WH, WW, cur_ref.shape[-1])
    moved = dot(shift_matrix(shift_ref[0]), pair_rows(cur, after)).astype(BF)
    out_ref[...] = moved.reshape(WH, WW, cur_ref.shape[-1])


def place(shift, windows, rim):
    count, _, c = windows.shape
    return pl.pallas_call(
        place_kernel,
        grid=(count,),
        in_specs=[
            pl.BlockSpec(memory_space=pltpu.SMEM),
            pl.BlockSpec((1, WIN, c), lambda w: (w, 0, 0)),
            pl.BlockSpec((1, WIN, c), lambda w: (jnp.minimum(w + 1, count - 1), 0, 0)),
            pl.BlockSpec((1, WIN, c), lambda w: (0, 0, 0)),
        ],
        out_specs=pl.BlockSpec((WH, WW, c), lambda w: (0, w, 0)),
        out_shape=jax.ShapeDtypeStruct((WH, count * WW, c), BF),
        name="place",
    )(shift, windows, windows, rim)


def flat_permute(value, mask):
    total = lax.axis_size("lon") * lax.axis_size("lat")
    return lax.ppermute(value, ("lon", "lat"), [(n, n ^ mask) for n in range(total)])


def bit_groups(total):
    bits = total.bit_length() - 1
    sizes = [1]
    while sum(sizes) < bits:
        sizes.append(min(2, bits - sum(sizes)))
    return sizes


def scatter_sum(matrix):
    n_lat = lax.axis_size("lat")
    total = lax.axis_size("lon") * n_lat
    me = lax.axis_index("lon") * n_lat + lax.axis_index("lat")
    rows, cols = matrix.shape
    blocks = matrix.reshape(total, rows // total, cols)
    low = 0
    sizes = bit_groups(total)
    for size in sizes:
        ways = 1 << size
        mine = (me >> low) & (ways - 1)
        view = blocks.reshape(blocks.shape[0] // ways, ways, rows // total, cols)
        kept = lax.dynamic_index_in_dim(view, mine, 1, keepdims=False).astype(F32)
        for n in range(1, ways):
            sent = lax.dynamic_index_in_dim(view, mine ^ n, 1, keepdims=False)
            kept = kept + flat_permute(sent, n << low).astype(F32)
        low += size
        blocks = kept if low == sum(sizes) else kept.astype(BF)
    return blocks.reshape(rows // total, cols)


def full_sum(value):
    total = lax.axis_size("lon") * lax.axis_size("lat")
    low = 0
    for size in bit_groups(total):
        parts = [flat_permute(value, n << low) for n in range(1, 1 << size)]
        for part in parts:
            value = value + part
        low += size
    return value


def ring_shift(value, steps):
    count = lax.axis_size("lon")
    return lax.ppermute(value, "lon", [(n, (n + steps) % count) for n in range(count)])


def span_codes(rel_index):
    rel = rel_index.reshape(WH, WW, WH, WW)
    upper = jnp.concatenate([rel[0, 0, ::-1, ::-1], rel[0, 1:, ::-1, 0].T], axis=1)
    lower = jnp.concatenate([rel[1:, 0, 0, ::-1], rel[1:, 1:, 0, 0]], axis=1)
    grid = jnp.concatenate([upper, lower], axis=0)
    grid = jnp.pad(grid, ((0, 0), (0, 1)), constant_values=-1)
    slots = WH // 2
    lines = [grid[n : n + 2 * slots - 1 : 2].reshape(1, slots * 2 * WW) for n in range(SPANS)]
    return jnp.concatenate(lines, axis=1)


def shards(inputs, d_out, w_qkv, w_proj, gain, bias_table, rel_index, shifts):
    n_lon = lax.axis_size("lon")
    n_lat = lax.axis_size("lat")
    n_dev = n_lon * n_lat
    _, columns, c = inputs.shape
    tokens = inputs.shape[0] * columns * n_dev
    scales = (tokens ** (-0.5), (tokens // WIN) ** (-0.5))
    groups = 2
    gain_row = gain.reshape(1, c)

    rim = (inputs[:, columns - WW :], d_out[:, columns - WW :])
    halo = (ring_shift(rim[0], 1), ring_shift(rim[1], 1))

    relations, _ = bias_table.shape
    entries = -(-relations // LANES) * LANES
    table = jnp.pad(bias_table.T, ((0, 0), (0, entries - relations)))
    hot, bias = expand_bias(span_codes(rel_index), table)

    carried = project(shifts, inputs, d_out, w_qkv, w_proj, gain_row)
    x, d, nt, qkv, dh = project(
        shifts, inputs, d_out, w_qkv, w_proj, gain_row, halo=halo, carried=tuple(carried)
    )

    dp0, att0, grad0, table0 = attend(0, groups, qkv, dh, bias, hot, nt, d, scales)
    own0 = scatter_sum(grad0)
    dp1, grad1, table1 = attend(1, groups, qkv, dh, bias, hot, nt, d, scales, att0=att0)
    own1 = scatter_sum(grad1)

    windows = input_grad((dp0, dp1), x, d, w_qkv, gain_row)
    returned = ring_shift(windows[:1], -1)
    d_inputs = place(shifts, windows, returned)

    g_table = full_sum(jnp.concatenate([table0, table1], axis=0))[:, :relations].T

    wide = c // groups
    parts = []
    for n in range(3):
        parts += [own0[:, n * wide : (n + 1) * wide], own1[:, n * wide : (n + 1) * wide]]
    g_qkv = jnp.concatenate(parts, axis=1)
    g_proj = own1[:, 3 * wide :]
    rows = c // n_dev
    start = (lax.axis_index("lon") * n_lat + lax.axis_index("lat")) * rows
    w_rows = lax.dynamic_slice_in_dim(w_qkv, start, rows, 0).astype(F32)
    gain_rows = lax.dynamic_slice_in_dim(gain, start, rows, 0)
    g_gain = jnp.sum(w_rows * g_qkv, axis=1) / gain_rows
    return (d_inputs, g_qkv, g_proj, g_gain, g_table)


def solution(mesh):
    return jax.shard_map(
        shards,
        mesh=mesh,
        in_specs=(P("lat", "lon", None), P("lat", "lon", None), P(), P(), P(), P(), P(), P("lat")),
        out_specs=(
            P("lat", "lon", None),
            P(("lon", "lat"), None),
            P(("lon", "lat"), None),
            P(("lon", "lat")),
            P(),
        ),
        check_vma=False,
    )
```

profile of v0, /device:TPU:0, one launch (start us, length us, event | category | flops | bytes accessed | tf_op | source)
XLA Modules:
  0.0 119.7 jit_solution(2439276442569597510)
XLA Ops:
  1.6 3.0 %collective-permute-start = (bf16[8,16,512]{2,1,0:T(8,128)(2,1)S(1)}, bf16[8,16,512]{2,1,0:T(8,128)(2,1)S(1)}, u32[]{:S(2)}, u32[]{:S(2)}) collective-permute-start(bf16[8,16,512]{2,1,0:T(8,128)(2,1)S(1)} %slice.72), channel_id=1, source_target_pairs={{0,4},{4,8},{8,12},{12,16},{16,20},{20,24},{24,28},{28,0},{1,5},{5... | collective-permute-start | bytes 393224 | tf_op jit(solution)/shard_map/ppermute | solution.py:457
  5.5 1.6 %collective-permute-start.1 = (bf16[8,16,512]{2,1,0:T(8,128)(2,1)S(1)}, bf16[8,16,512]{2,1,0:T(8,128)(2,1)S(1)}, u32[]{:S(2)}, u32[]{:S(2)}) collective-permute-start(bf16[8,16,512]{2,1,0:T(8,128)(2,1)S(1)} %slice.73), channel_id=1, source_target_pairs={{0,4},{4,8},{8,12},{12,16},{16,20},{20,24},{24,28},{28,0},{1,5},{5... | collective-permute-start | bytes 393224 | tf_op jit(solution)/shard_map/ppermute | solution.py:457
  8.1 1.9 %slice_reduce_fusion = s32[7,15]{1,0:T(8,128)S(1)} fusion(s32[8,16,8,16]{3,2,1,0:T(8,128)S(1)} %reshape.86), kind=kLoop, calls=%fused_computation.22 | loop fusion | bytes 840 | tf_op jit(solution)/shard_map/slice | solution.py:463
  13.5 2.6 %expand_bias.1 = (bf16[512,1152]{1,0:T(8,128)(2,1)}, f32[16,128,128]{2,1,0:T(8,128)}) custom-call(s32[1,1152]{1,0:T(1,128)} %copy-done.9, f32[16,512]{1,0:T(8,128)} %pad.9.table_ref), custom_call_target="tpu_custom_call" | custom-call | tf_op jit(solution)/shard_map/expand_bias/pallas_call | solution.py:73
  16.1 10.2 %project_rest.1 = (bf16[8,128,512]{2,1,0:T(8,128)(2,1)}, bf16[8,128,512]{2,1,0:T(8,128)(2,1)}, bf16[512,1024]{1,0:T(8,128)(2,1)}, bf16[8,128,1536]{2,1,0:T(8,128)(2,1)}, bf16[8,128,512]{2,1,0:T(8,128)(2,1)}) custom-call(s32[1]{0:T(128)S(6)} %copy.48.shift_ref, bf16[8,128,512]{2,1,0:T(8,128)(2,1)} %xcur_ref.3, bf16[8,128,512]{2,1,0:T(8,128)(2,1)} %xcur_ref.3, ...), custom_call_target="tpu_custom_call" | custom-call | tf_op jit(solution)/shard_map/project_rest/pallas_call | solution.py:137
  26.9 3.4 %project_rim.1 = (bf16[8,128,512]{2,1,0:T(8,128)(2,1)}, bf16[8,128,512]{2,1,0:T(8,128)(2,1)}, bf16[512,1024]{1,0:T(8,128)(2,1)}, bf16[8,128,1536]{2,1,0:T(8,128)(2,1)}, bf16[8,128,512]{2,1,0:T(8,128)(2,1)}) custom-call(s32[1]{0:T(128)S(6)} %copy.48.shift_ref, ...), custom_call_target="tpu_custom_call", output_to_operand_aliasing={{0}: (8, {}), {1}: (9, {}), {2}: (10, {}), {3}: (11, {}), {... | custom-call | tf_op jit(solution)/shard_map/project_rim/pallas_call | solution.py:137
  30.3 13.1 %attend_0.1 = (bf16[8,128,768]{2,1,0:T(8,128)(2,1)}, bf16[256,1024]{1,0:T(8,128)(2,1)}, bf16[512,768]{1,0:T(8,128)(2,1)}, f32[8,512]{1,0:T(8,128)}) custom-call(bf16[8,128,1536]{2,1,0:T(8,128)(2,1)} %get-tuple-element.29.refs_0_.refs_1_.refs_2_, bf16[8,128,1536]{2,1,0:T(8,128)(2,1)} %get-tuple-element.29.refs_0_.refs_1_.refs_2_, ...), custom_call_target="tpu_custom_call" | custom-call | tf_op jit(solution)/shard_map/attend_0/pallas_call | solution.py:311
  43.5 13.9 %attend_1.1 = (bf16[8,128,768]{2,1,0:T(8,128)(2,1)}, bf16[512,1280]{1,0:T(8,128)(2,1)}, f32[8,512]{1,0:T(8,128)}) custom-call(bf16[8,128,1536]{2,1,0:T(8,128)(2,1)} %get-tuple-element.29.refs_0_.refs_1_.refs_2_, bf16[8,128,1536]{2,1,0:T(8,128)(2,1)} %get-tuple-element.29.refs_0_.refs_1_.refs_2_, ...), custom_call_target="tpu_custom_call" | custom-call | tf_op jit(solution)/shard_map/attend_1/pallas_call | solution.py:311
  57.4 9.2 %input_grad.1.cur_ref.next_ref = bf16[8,128,512]{2,1,0:T(8,128)(2,1)} custom-call(bf16[8,128,768]{2,1,0:T(8,128)(2,1)} %get-tuple-element.35.refs_0_, bf16[8,128,768]{2,1,0:T(8,128)(2,1)} %get-tuple-element.37.refs_1_, bf16[8,128,512]{2,1,0:T(8,128)(2,1)} %get-tuple-element.38.refs_2_, bf16[8,128,512]{2,1,0:T(8,128)(2,1)} %get-tuple-element.34.refs_7_.refs_3_, ...), custom_call_target="tpu_custom_call" | custom-call | tf_op jit(solution)/shard_map/input_grad/pallas_call | solution.py:367
  67.5 3.4 %collective-permute-start.2 = (bf16[1,128,512]{2,1,0:T(8,128)(2,1)S(1)}, bf16[1,128,512]{2,1,0:T(8,128)(2,1)S(1)}, u32[]{:S(2)}, u32[]{:S(2)}) collective-permute-start(bf16[1,128,512]{2,1,0:T(8,128)(2,1)S(1)} %slice.100), channel_id=1, source_target_pairs={{0,28},{4,0},{8,4},{12,8},{16,12},{20,16},{24,20},{28,24},{1,29},{... | collective-permute-start | bytes 393224 | tf_op jit(solution)/shard_map/ppermute | solution.py:457
  72.3 2.9 %collective-permute-start.19 = (f32[16,512]{1,0:T(8,128)S(1)}, f32[16,512]{1,0:T(8,128)S(1)}, u32[]{:S(2)}, u32[]{:S(2)}) collective-permute-start(f32[16,512]{1,0:T(8,128)S(1)} %add.148), channel_id=1, source_target_pairs={{0,4},{1,5},{2,6},{3,7},{4,0},{5,1},{6,2},{7,3},{8,12},{9,13},{10,... | collective-permute-start | bytes 98312 | tf_op jit(solution)/shard_map/ppermute | solution.py:412
  77.4 1.7 %collective-permute-done.18 = f32[16,512]{1,0:T(8,128)S(1)} collective-permute-done((f32[16,512]{1,0:T(8,128)S(1)}, f32[16,512]{1,0:T(8,128)S(1)}, u32[]{:S(2)}, u32[]{:S(2)}) %collective-permute-start.18) | collective-permute-done | bytes 32800 | tf_op jit(solution)/shard_map/ppermute | solution.py:412
  79.2 1.9 %collective-permute-start.23 = (f32[16,512]{1,0:T(8,128)S(1)}, f32[16,512]{1,0:T(8,128)S(1)}, u32[]{:S(2)}, u32[]{:S(2)}) collective-permute-start(f32[16,512]{1,0:T(8,128)S(1)} %add_add_fusion), channel_id=1, source_target_pairs={{0,24},{1,25},{2,26},{3,27},{4,28},{5,29},{6,30},{7,31},{8,16},{9,... | collective-permute-start | bytes 98312 | tf_op jit(solution)/shard_map/ppermute | solution.py:412
  81.0 2.6 %collective-permute-start.21 = (f32[16,512]{1,0:T(8,128)S(1)}, f32[16,512]{1,0:T(8,128)S(1)}, u32[]{:S(2)}, u32[]{:S(2)}) collective-permute-start(f32[16,512]{1,0:T(8,128)S(1)} %add_add_fusion), channel_id=1, source_target_pairs={{0,8},{1,9},{2,10},{3,11},{4,12},{5,13},{6,14},{7,15},{8,0},{9,1},... | collective-permute-start | bytes 98312 | tf_op jit(solution)/shard_map/ppermute | solution.py:412
  87.0 1.4 %collective-permute-start.4 = (bf16[4,16,768]{2,1,0:T(8,128)(2,1)S(1)}, bf16[4,16,768]{2,1,0:T(8,128)(2,1)S(1)}, u32[]{:S(2)}, u32[]{:S(2)}) collective-permute-start(bf16[4,16,768]{2,1,0:T(8,128)(2,1)S(1)} %get-tuple-element.46), channel_id=1, source_target_pairs={{0,2},{1,3},{2,0},{3,1},{4,6},{5,7},{6,4},{7,5},{8,10},{9,11},{10,... | collective-permute-start | bytes 294920 | tf_op jit(solution)/shard_map/ppermute | solution.py:412
  89.7 6.2 %place.1 = bf16[8,128,512]{2,1,0:T(8,128)(2,1)} custom-call(s32[1]{0:T(128)S(6)} %copy.48.shift_ref, bf16[8,128,512]{2,1,0:T(8,128)(2,1)} %input_grad.1.cur_ref.next_ref, bf16[8,128,512]{2,1,0:T(8,128)(2,1)} %input_grad.1.cur_ref.next_ref, bf16[1,128,512]{2,1,0:T(8,128)(2,1)} %copy-done.5), custom_call_target="tpu_custom_call" | custom-call | tf_op jit(solution)/shard_map/place/pallas_call | solution.py:395
  96.0 1.9 %collective-permute-start.9 = (bf16[1,16,768]{2,1,0:T(8,128)(2,1)S(1)}, bf16[1,16,768]{2,1,0:T(8,128)(2,1)S(1)}, u32[]{:S(2)}, u32[]{:S(2)}) collective-permute-start(bf16[1,16,768]{2,1,0:T(8,128)(2,1)S(1)} %get-tuple-element.53), channel_id=1, source_target_pairs={{0,24},{1,25},{2,26},{3,27},{4,28},{5,29},{6,30},{7,31},{8,16},{9,... | collective-permute-start | bytes 73736 | tf_op jit(solution)/shard_map/ppermute | solution.py:412
  97.9 2.6 %collective-permute-start.7 = (bf16[1,16,768]{2,1,0:T(8,128)(2,1)S(1)}, bf16[1,16,768]{2,1,0:T(8,128)(2,1)S(1)}, u32[]{:S(2)}, u32[]{:S(2)}) collective-permute-start(bf16[1,16,768]{2,1,0:T(8,128)(2,1)S(1)} %get-tuple-element.52), channel_id=1, source_target_pairs={{0,8},{1,9},{2,10},{3,11},{4,12},{5,13},{6,14},{7,15},{8,0},{9,1},... | collective-permute-start | bytes 73736 | tf_op jit(solution)/shard_map/ppermute | solution.py:412
  103.9 1.4 %collective-permute-start.11 = (bf16[4,16,1280]{2,1,0:T(8,128)(2,1)S(1)}, bf16[4,16,1280]{2,1,0:T(8,128)(2,1)S(1)}, u32[]{:S(2)}, u32[]{:S(2)}) collective-permute-start(bf16[4,16,1280]{2,1,0:T(8,128)(2,1)S(1)} %get-tuple-element.43), channel_id=1, source_target_pairs={{0,2},{1,3},{2,0},{3,1},{4,6},{5,7},{6,4},{7,5},{8,10},{9,11},{10,... | collective-permute-start | bytes 491528 | tf_op jit(solution)/shard_map/ppermute | solution.py:412
  105.3 2.8 %collective-permute-done.13 = bf16[4,16,1280]{2,1,0:T(8,128)(2,1)S(1)} collective-permute-done((bf16[4,16,1280]{2,1,0:T(8,128)(2,1)S(1)}, bf16[4,16,1280]{2,1,0:T(8,128)(2,1)S(1)}, u32[]{:S(2)}, u32[]{:S(2)}) %collective-permute-start.13) | collective-permute-done | bytes 163872 | tf_op jit(solution)/shard_map/ppermute | solution.py:412
  108.1 1.7 %collective-permute-done.12 = bf16[4,16,1280]{2,1,0:T(8,128)(2,1)S(1)} collective-permute-done((bf16[4,16,1280]{2,1,0:T(8,128)(2,1)S(1)}, bf16[4,16,1280]{2,1,0:T(8,128)(2,1)S(1)}, u32[]{:S(2)}, u32[]{:S(2)}) %collective-permute-start.12) | collective-permute-done | bytes 163872 | tf_op jit(solution)/shard_map/ppermute | solution.py:412
  109.9 1.9 %collective-permute-start.16 = (bf16[1,16,1280]{2,1,0:T(8,128)(2,1)S(1)}, bf16[1,16,1280]{2,1,0:T(8,128)(2,1)S(1)}, u32[]{:S(2)}, u32[]{:S(2)}) collective-permute-start(bf16[1,16,1280]{2,1,0:T(8,128)(2,1)S(1)} %get-tuple-element.50), channel_id=1, source_target_pairs={{0,24},{1,25},{2,26},{3,27},{4,28},{5,29},{6,30},{7,31},{8,16},{9,... | collective-permute-start | bytes 122888 | tf_op jit(solution)/shard_map/ppermute | solution.py:412
  111.8 2.6 %collective-permute-start.14 = (bf16[1,16,1280]{2,1,0:T(8,128)(2,1)S(1)}, bf16[1,16,1280]{2,1,0:T(8,128)(2,1)S(1)}, u32[]{:S(2)}, u32[]{:S(2)}) collective-permute-start(bf16[1,16,1280]{2,1,0:T(8,128)(2,1)S(1)} %get-tuple-element.49), channel_id=1, source_target_pairs={{0,8},{1,9},{2,10},{3,11},{4,12},{5,13},{6,14},{7,15},{8,0},{9,1},... | collective-permute-start | bytes 122888 | tf_op jit(solution)/shard_map/ppermute | solution.py:412
  114.4 1.4 %collective-permute-done.16 = bf16[1,16,1280]{2,1,0:T(8,128)(2,1)S(1)} collective-permute-done((bf16[1,16,1280]{2,1,0:T(8,128)(2,1)S(1)}, bf16[1,16,1280]{2,1,0:T(8,128)(2,1)S(1)}, u32[]{:S(2)}, u32[]{:S(2)}) %collective-permute-start.16) | collective-permute-done | bytes 40992 | tf_op jit(solution)/shard_map/ppermute | solution.py:412
  (120 shorter events, 22.8 us)
Async XLA Ops:
  1.6 24.7 %collective-permute-start = (bf16[8,16,512]{2,1,0:T(8,128)(2,1)S(1)}, bf16[8,16,512]{2,1,0:T(8,128)(2,1)S(1)}, u32[]{:S(2)}, u32[]{:S(2)}) collective-permute-start(bf16[8,16,512]{2,1,0:T(8,128)(2,1)S(1)} %slice.72), channel_id=1, source_target_pairs={{0,4},{4,8},{8,12},{12,16},{16,20},{20,24},{24,28},{28,0},{1,5},{5... | collective-permute-start | bytes 393224 | tf_op jit(solution)/shard_map/ppermute | solution.py:457
  5.5 20.7 %collective-permute-start.1 = (bf16[8,16,512]{2,1,0:T(8,128)(2,1)S(1)}, bf16[8,16,512]{2,1,0:T(8,128)(2,1)S(1)}, u32[]{:S(2)}, u32[]{:S(2)}) collective-permute-start(bf16[8,16,512]{2,1,0:T(8,128)(2,1)S(1)} %slice.73), channel_id=1, source_target_pairs={{0,4},{4,8},{8,12},{12,16},{16,20},{20,24},{24,28},{28,0},{1,5},{5... | collective-permute-start | bytes 393224 | tf_op jit(solution)/shard_map/ppermute | solution.py:457
  67.5 21.5 %collective-permute-start.2 = (bf16[1,128,512]{2,1,0:T(8,128)(2,1)S(1)}, bf16[1,128,512]{2,1,0:T(8,128)(2,1)S(1)}, u32[]{:S(2)}, u32[]{:S(2)}) collective-permute-start(bf16[1,128,512]{2,1,0:T(8,128)(2,1)S(1)} %slice.100), channel_id=1, source_target_pairs={{0,28},{4,0},{8,4},{12,8},{16,12},{20,16},{24,20},{28,24},{1,29},{... | collective-permute-start | bytes 393224 | tf_op jit(solution)/shard_map/ppermute | solution.py:457
  71.0 1.3 %collective-permute-start.17 = (f32[16,512]{1,0:T(8,128)S(1)}, f32[16,512]{1,0:T(8,128)S(1)}, u32[]{:S(2)}, u32[]{:S(2)}) collective-permute-start(f32[16,512]{1,0:T(8,128)S(1)} %constant_dynamic-update-slice_fusion.15), channel_id=1, source_target_pairs={{0,1},{1,0},{2,3},{3,2},{4,5},{5,4},{6,7},{7,6},{8,9},{9,8},{10,11... | collective-permute-start | bytes 98312 | tf_op jit(solution)/shard_map/ppermute | solution.py:412
  71.1 9.9 %collective-permute-start.3 = (bf16[16,16,768]{2,1,0:T(8,128)(2,1)S(1)}, bf16[16,16,768]{2,1,0:T(8,128)(2,1)S(1)}, u32[]{:S(2)}, u32[]{:S(2)}) collective-permute-start(bf16[16,16,768]{2,1,0:T(8,128)(2,1)S(1)} %dynamic-slice_bitcast_fusion.1), channel_id=1, source_target_pairs={{0,1},{1,0},{2,3},{3,2},{4,5},{5,4},{6,7},{7,6},{8,9},{9,8},{10,11... | collective-permute-start | bytes 1179656 | tf_op jit(solution)/shard_map/ppermute | solution.py:412
  72.3 4.8 %collective-permute-start.20 = (f32[16,512]{1,0:T(8,128)S(1)}, f32[16,512]{1,0:T(8,128)S(1)}, u32[]{:S(2)}, u32[]{:S(2)}) collective-permute-start(f32[16,512]{1,0:T(8,128)S(1)} %add.148), channel_id=1, source_target_pairs={{0,6},{1,7},{2,4},{3,5},{4,2},{5,3},{6,0},{7,1},{8,14},{9,15},{10,... | collective-permute-start | bytes 98312 | tf_op jit(solution)/shard_map/ppermute | solution.py:412
  72.3 5.2 %collective-permute-start.19 = (f32[16,512]{1,0:T(8,128)S(1)}, f32[16,512]{1,0:T(8,128)S(1)}, u32[]{:S(2)}, u32[]{:S(2)}) collective-permute-start(f32[16,512]{1,0:T(8,128)S(1)} %add.148), channel_id=1, source_target_pairs={{0,4},{1,5},{2,6},{3,7},{4,0},{5,1},{6,2},{7,3},{8,12},{9,13},{10,... | collective-permute-start | bytes 98312 | tf_op jit(solution)/shard_map/ppermute | solution.py:412
  75.2 3.9 %collective-permute-start.18 = (f32[16,512]{1,0:T(8,128)S(1)}, f32[16,512]{1,0:T(8,128)S(1)}, u32[]{:S(2)}, u32[]{:S(2)}) collective-permute-start(f32[16,512]{1,0:T(8,128)S(1)} %add.148), channel_id=1, source_target_pairs={{0,2},{1,3},{2,0},{3,1},{4,6},{5,7},{6,4},{7,5},{8,10},{9,11},{10,... | collective-permute-start | bytes 98312 | tf_op jit(solution)/shard_map/ppermute | solution.py:412
  77.1 23.4 %collective-permute-start.10 = (bf16[16,16,1280]{2,1,0:T(8,128)(2,1)S(1)}, bf16[16,16,1280]{2,1,0:T(8,128)(2,1)}, u32[]{:S(2)}, u32[]{:S(2)}) collective-permute-start(bf16[16,16,1280]{2,1,0:T(8,128)(2,1)S(1)} %dynamic-slice_bitcast_fusion), channel_id=1, source_target_pairs={{0,1},{1,0},{2,3},{3,2},{4,5},{5,4},{6,7},{7,6},{8,9},{9,8},{10,11... | collective-permute-start | bytes 1966088 | tf_op jit(solution)/shard_map/ppermute | solution.py:412
  79.2 5.8 %collective-permute-start.23 = (f32[16,512]{1,0:T(8,128)S(1)}, f32[16,512]{1,0:T(8,128)S(1)}, u32[]{:S(2)}, u32[]{:S(2)}) collective-permute-start(f32[16,512]{1,0:T(8,128)S(1)} %add_add_fusion), channel_id=1, source_target_pairs={{0,24},{1,25},{2,26},{3,27},{4,28},{5,29},{6,30},{7,31},{8,16},{9,... | collective-permute-start | bytes 98312 | tf_op jit(solution)/shard_map/ppermute | solution.py:412
  81.0 4.8 %collective-permute-start.22 = (f32[16,512]{1,0:T(8,128)S(1)}, f32[16,512]{1,0:T(8,128)S(1)}, u32[]{:S(2)}, u32[]{:S(2)}) collective-permute-start(f32[16,512]{1,0:T(8,128)S(1)} %add_add_fusion), channel_id=1, source_target_pairs={{0,16},{1,17},{2,18},{3,19},{4,20},{5,21},{6,22},{7,23},{8,24},{9,... | collective-permute-start | bytes 98312 | tf_op jit(solution)/shard_map/ppermute | solution.py:412
  81.0 6.0 %collective-permute-start.21 = (f32[16,512]{1,0:T(8,128)S(1)}, f32[16,512]{1,0:T(8,128)S(1)}, u32[]{:S(2)}, u32[]{:S(2)}) collective-permute-start(f32[16,512]{1,0:T(8,128)S(1)} %add_add_fusion), channel_id=1, source_target_pairs={{0,8},{1,9},{2,10},{3,11},{4,12},{5,13},{6,14},{7,15},{8,0},{9,1},... | collective-permute-start | bytes 98312 | tf_op jit(solution)/shard_map/ppermute | solution.py:412
  84.9 10.9 %collective-permute-start.6 = (bf16[4,16,768]{2,1,0:T(8,128)(2,1)S(1)}, bf16[4,16,768]{2,1,0:T(8,128)(2,1)S(1)}, u32[]{:S(2)}, u32[]{:S(2)}) collective-permute-start(bf16[4,16,768]{2,1,0:T(8,128)(2,1)S(1)} %get-tuple-element.47), channel_id=1, source_target_pairs={{0,6},{1,7},{2,4},{3,5},{4,2},{5,3},{6,0},{7,1},{8,14},{9,15},{10,... | collective-permute-start | bytes 294920 | tf_op jit(solution)/shard_map/ppermute | solution.py:412
  85.9 10.0 %collective-permute-start.5 = (bf16[4,16,768]{2,1,0:T(8,128)(2,1)S(1)}, bf16[4,16,768]{2,1,0:T(8,128)(2,1)S(1)}, u32[]{:S(2)}, u32[]{:S(2)}) collective-permute-start(bf16[4,16,768]{2,1,0:T(8,128)(2,1)S(1)} %get-tuple-element.48), channel_id=1, source_target_pairs={{0,4},{1,5},{2,6},{3,7},{4,0},{5,1},{6,2},{7,3},{8,12},{9,13},{10,... | collective-permute-start | bytes 294920 | tf_op jit(solution)/shard_map/ppermute | solution.py:412
  87.0 8.9 %collective-permute-start.4 = (bf16[4,16,768]{2,1,0:T(8,128)(2,1)S(1)}, bf16[4,16,768]{2,1,0:T(8,128)(2,1)S(1)}, u32[]{:S(2)}, u32[]{:S(2)}) collective-permute-start(bf16[4,16,768]{2,1,0:T(8,128)(2,1)S(1)} %get-tuple-element.46), channel_id=1, source_target_pairs={{0,2},{1,3},{2,0},{3,1},{4,6},{5,7},{6,4},{7,5},{8,10},{9,11},{10,... | collective-permute-start | bytes 294920 | tf_op jit(solution)/shard_map/ppermute | solution.py:412
  96.0 7.9 %collective-permute-start.9 = (bf16[1,16,768]{2,1,0:T(8,128)(2,1)S(1)}, bf16[1,16,768]{2,1,0:T(8,128)(2,1)S(1)}, u32[]{:S(2)}, u32[]{:S(2)}) collective-permute-start(bf16[1,16,768]{2,1,0:T(8,128)(2,1)S(1)} %get-tuple-element.53), channel_id=1, source_target_pairs={{0,24},{1,25},{2,26},{3,27},{4,28},{5,29},{6,30},{7,31},{8,16},{9,... | collective-permute-start | bytes 73736 | tf_op jit(solution)/shard_map/ppermute | solution.py:412
  97.9 7.5 %collective-permute-start.8 = (bf16[1,16,768]{2,1,0:T(8,128)(2,1)S(1)}, bf16[1,16,768]{2,1,0:T(8,128)(2,1)S(1)}, u32[]{:S(2)}, u32[]{:S(2)}) collective-permute-start(bf16[1,16,768]{2,1,0:T(8,128)(2,1)S(1)} %get-tuple-element.54), channel_id=1, source_target_pairs={{0,16},{1,17},{2,18},{3,19},{4,20},{5,21},{6,22},{7,23},{8,24},{9,... | collective-permute-start | bytes 73736 | tf_op jit(solution)/shard_map/ppermute | solution.py:412
  97.9 7.5 %collective-permute-start.7 = (bf16[1,16,768]{2,1,0:T(8,128)(2,1)S(1)}, bf16[1,16,768]{2,1,0:T(8,128)(2,1)S(1)}, u32[]{:S(2)}, u32[]{:S(2)}) collective-permute-start(bf16[1,16,768]{2,1,0:T(8,128)(2,1)S(1)} %get-tuple-element.52), channel_id=1, source_target_pairs={{0,8},{1,9},{2,10},{3,11},{4,12},{5,13},{6,14},{7,15},{8,0},{9,1},... | collective-permute-start | bytes 73736 | tf_op jit(solution)/shard_map/ppermute | solution.py:412
  101.7 6.4 %collective-permute-start.13 = (bf16[4,16,1280]{2,1,0:T(8,128)(2,1)S(1)}, bf16[4,16,1280]{2,1,0:T(8,128)(2,1)S(1)}, u32[]{:S(2)}, u32[]{:S(2)}) collective-permute-start(bf16[4,16,1280]{2,1,0:T(8,128)(2,1)S(1)} %get-tuple-element.44), channel_id=1, source_target_pairs={{0,6},{1,7},{2,4},{3,5},{4,2},{5,3},{6,0},{7,1},{8,14},{9,15},{10,... | collective-permute-start | bytes 491528 | tf_op jit(solution)/shard_map/ppermute | solution.py:412
  102.7 7.1 %collective-permute-start.12 = (bf16[4,16,1280]{2,1,0:T(8,128)(2,1)S(1)}, bf16[4,16,1280]{2,1,0:T(8,128)(2,1)S(1)}, u32[]{:S(2)}, u32[]{:S(2)}) collective-permute-start(bf16[4,16,1280]{2,1,0:T(8,128)(2,1)S(1)} %get-tuple-element.45), channel_id=1, source_target_pairs={{0,4},{1,5},{2,6},{3,7},{4,0},{5,1},{6,2},{7,3},{8,12},{9,13},{10,... | collective-permute-start | bytes 491528 | tf_op jit(solution)/shard_map/ppermute | solution.py:412
  103.9 5.9 %collective-permute-start.11 = (bf16[4,16,1280]{2,1,0:T(8,128)(2,1)S(1)}, bf16[4,16,1280]{2,1,0:T(8,128)(2,1)S(1)}, u32[]{:S(2)}, u32[]{:S(2)}) collective-permute-start(bf16[4,16,1280]{2,1,0:T(8,128)(2,1)S(1)} %get-tuple-element.43), channel_id=1, source_target_pairs={{0,2},{1,3},{2,0},{3,1},{4,6},{5,7},{6,4},{7,5},{8,10},{9,11},{10,... | collective-permute-start | bytes 491528 | tf_op jit(solution)/shard_map/ppermute | solution.py:412
  109.9 5.9 %collective-permute-start.16 = (bf16[1,16,1280]{2,1,0:T(8,128)(2,1)S(1)}, bf16[1,16,1280]{2,1,0:T(8,128)(2,1)S(1)}, u32[]{:S(2)}, u32[]{:S(2)}) collective-permute-start(bf16[1,16,1280]{2,1,0:T(8,128)(2,1)S(1)} %get-tuple-element.50), channel_id=1, source_target_pairs={{0,24},{1,25},{2,26},{3,27},{4,28},{5,29},{6,30},{7,31},{8,16},{9,... | collective-permute-start | bytes 122888 | tf_op jit(solution)/shard_map/ppermute | solution.py:412
  111.8 5.0 %collective-permute-start.15 = (bf16[1,16,1280]{2,1,0:T(8,128)(2,1)S(1)}, bf16[1,16,1280]{2,1,0:T(8,128)(2,1)S(1)}, u32[]{:S(2)}, u32[]{:S(2)}) collective-permute-start(bf16[1,16,1280]{2,1,0:T(8,128)(2,1)S(1)} %get-tuple-element.51), channel_id=1, source_target_pairs={{0,16},{1,17},{2,18},{3,19},{4,20},{5,21},{6,22},{7,23},{8,24},{9,... | collective-permute-start | bytes 122888 | tf_op jit(solution)/shard_map/ppermute | solution.py:412
  111.8 5.0 %collective-permute-start.14 = (bf16[1,16,1280]{2,1,0:T(8,128)(2,1)S(1)}, bf16[1,16,1280]{2,1,0:T(8,128)(2,1)S(1)}, u32[]{:S(2)}, u32[]{:S(2)}) collective-permute-start(bf16[1,16,1280]{2,1,0:T(8,128)(2,1)S(1)} %get-tuple-element.49), channel_id=1, source_target_pairs={{0,8},{1,9},{2,10},{3,11},{4,12},{5,13},{6,14},{7,15},{8,0},{9,1},... | collective-permute-start | bytes 122888 | tf_op jit(solution)/shard_map/ppermute | solution.py:412
  (10 other events, 75.7 us)
where the time goes:
time: 121 us; the launch traced here: 120 us
  Pallas kernels  58.6 us (48%)
  starting transfers between devices  31.8 us (26%)
  waiting for transfers between devices  12.7 us (10%)
  local copies, waits for them, and re-layouts  10.4 us (9%)
  other arithmetic  4.5 us (4%)
  between operations  1.62 us (1%)
    pallas_call x2, Pallas kernels, attend(): pl.pallas_call(lambda *refs: attend_kernel(scales, last, *refs), grid=(co...  27 us
    ppermute x21, starting transfers between devices, flat_permute(): lax.ppermute(value, ('lon', 'lat'), [(n, n ^ mask) for n in range(total)])  23.8 us
    pallas_call x2, Pallas kernels, project(): pl.pallas_call(project_kernel, grid=(steps,), in_specs=[pl.BlockSpec(memo...  13.6 us
    ppermute x21, waiting for transfers between devices, flat_permute(): lax.ppermute(value, ('lon', 'lat'), [(n, n ^ mask) for n in range(total)])  12.7 us
    pallas_call x1, Pallas kernels, input_grad(): pl.pallas_call(lambda *refs: input_kernel(groups, *refs), grid=(count,),...  9.21 us
    ppermute x3, starting transfers between devices, ring_shift(): lax.ppermute(value, 'lon', [(n, (n + steps) % count) for n in range(count)])  8.06 us
    pallas_call x1, Pallas kernels, place(): pl.pallas_call(place_kernel, grid=(count,), in_specs=[pl.BlockSpec(memory...  6.17 us
    pallas_call x1, Pallas kernels, expand_bias(): pl.pallas_call(bias_kernel, out_shape=(jax.ShapeDtypeStruct((entries, wid...  2.61 us
  transfers between devices with their start and end apart: 24, of which 10 were waited for; matrix products, arithmetic and copies ran while one was open for 7% of the time, Pallas kernels for 16%

commit v1 on v0

v1 whole, which is shorter than its diff:
```python
import math

import jax
import jax.numpy as jnp
from jax import lax
from jax.experimental import pallas as pl
from jax.experimental.pallas import tpu as pltpu
from jax.sharding import PartitionSpec as P


H = 16
HD = 32
WH = 8
WW = 16
WIN = WH * WW
LANES = 128
SLAB = LANES // HD
SPANS = WH + 1
UNIT = 16
EPSILON = 1e-05
LOG2E = math.log2(math.e)
BF = jnp.bfloat16
F32 = jnp.float32
PARAMS = pltpu.CompilerParams(vmem_limit_bytes=24 * 2**20)


def dot(left, right):
    return lax.dot_general(left, right, (((1,), (0,)), ((), ())), preferred_element_type=F32)


def dot_nt(left, right):
    return lax.dot_general(left, right, (((1,), (1,)), ((), ())), preferred_element_type=F32)


def split3(value):
    high = value.astype(BF)
    rest = value - high.astype(F32)
    middle = rest.astype(BF)
    low = (rest - middle.astype(F32)).astype(BF)
    return jnp.concatenate([high, middle, low], axis=0)


def joined3(value):
    rows = value.shape[0] // 3
    return (value[:rows] + value[rows : 2 * rows]) + value[2 * rows :]


def bits_of(me_ref, low, size):
    return lax.shift_right_logical(me_ref[0], low) & ((1 << size) - 1)


def odd_lanes(rows):
    lane = lax.broadcasted_iota(jnp.int32, (rows, LANES), 1)
    return (lane // WW) % 2 == 1


def bias_kernel(me_ref, rel_ref, table_ref, hot_ref, bias_ref, line_ref, span_ref):
    line_ref[...] = rel_ref[...].astype(F32).T
    slot = lax.broadcasted_iota(jnp.int32, (1, LANES), 1) % (2 * WW)
    codes = []
    for first in range(SPANS):
        row = max(WH - 1 - first, 0)
        parity = first + row - (WH - 1)
        near = line_ref[row * WW + WW - 1 : row * WW + WW, :]
        far = line_ref[row * WW : row * WW + 1, :]
        if parity:
            near = pltpu.roll(near, LANES - WW, 1)
        far = pltpu.roll(far, (WW - 1 - WW * parity) % LANES, 1)
        code = jnp.where(slot < WW, near, far)
        codes.append(jnp.where(slot == 2 * WW - 1, -1.0, code))
    code = jnp.concatenate(codes, axis=1).astype(jnp.int32)
    entry = lax.broadcasted_iota(jnp.int32, hot_ref.shape, 0)
    hot = jnp.where(entry == code, 1.0, 0.0).astype(BF)
    hot_ref[...] = hot
    span_ref[...] = joined3(dot(split3(table_ref[...]), hot)) * LOG2E
    odd = odd_lanes(WW)
    for h in range(H):
        for row in range(WH):
            halves = []
            for parity in range(2):
                first = parity - row + WH - 1
                line = span_ref[h : h + 1, first * LANES : (first + 1) * LANES]
                line = jnp.broadcast_to(line, (WW, LANES))
                turn = (LANES - (WW - 1) + WW * parity) % LANES
                halves.append(pltpu.roll(line, turn, 1, stride=1, stride_axis=0))
            bias_ref[h, row * WW : (row + 1) * WW, :] = jnp.where(odd, halves[1], halves[0])


def expand_bias(me, rel_index, table):
    width = SPANS * LANES
    whole = pl.BlockSpec(memory_space=pltpu.VMEM)
    return pl.pallas_call(
        bias_kernel,
        in_specs=[pl.BlockSpec(memory_space=pltpu.SMEM), whole, whole],
        out_shape=(
            jax.ShapeDtypeStruct((table.shape[1], width), BF),
            jax.ShapeDtypeStruct((H, WIN, WIN), F32),
        ),
        scratch_shapes=[pltpu.VMEM((WIN, WIN), F32), pltpu.VMEM((H, width), F32)],
        compiler_params=PARAMS,
        name="expand_bias",
    )(me, rel_index, table)


def norm_stats(rows):
    centred = rows - jnp.mean(rows, axis=-1, keepdims=True)
    inv_std = lax.rsqrt(jnp.mean(centred * centred, axis=-1, keepdims=True) + EPSILON)
    return centred * inv_std, inv_std


def pair_rows(first, second):
    both = jnp.concatenate([first, second], axis=1)
    return both.reshape(both.shape[0] * both.shape[1], both.shape[2])


def shift_matrix(offset):
    row = lax.broadcasted_iota(jnp.int32, (WIN, 2 * WIN), 0)
    col = lax.broadcasted_iota(jnp.int32, (WIN, 2 * WIN), 1)
    same = (row // WW) == (col // (2 * WW))
    hit = same & ((col % (2 * WW)) == (row % WW) + offset)
    return jnp.where(hit, 1.0, 0.0).astype(BF)


def project_kernel(
    shift_ref, rim_ref, x_ref, d_ref, wq_ref, wp_ref, gain_ref, *rest
):
    xw_ref, dw_ref, nt_ref, qkv_ref, dh_ref, norm_ref = rest[-6:]
    rim = rim_ref is not None
    count = 1 if rim else x_ref.shape[1] // WW - 1
    c = x_ref.shape[-1]
    tokens = count * WIN
    select = shift_matrix(WW - shift_ref[0])

    def spans(ref, n, halo):
        if rim:
            return pair_rows(rim_ref[halo], ref[...])
        return pair_rows(ref[:, n * WW : (n + 1) * WW, :], ref[:, (n + 1) * WW : (n + 2) * WW, :])

    first = 0 if rim else 1
    for n in range(count):
        rows = slice(n * WIN, (n + 1) * WIN)
        values = dot(select, spans(x_ref, n, 0))
        xw_ref[first + n] = values.astype(BF)
        normal, _ = norm_stats(values)
        normed = (normal * gain_ref[...]).astype(BF)
        norm_ref[rows, :] = normed
        nt_ref[:, (first + n) * WIN : (first + n + 1) * WIN] = normed.T
        dw_ref[first + n] = dot(select, spans(d_ref, n, 1)).astype(BF)
    step = 2 * LANES
    for n in range(3 * c // step):
        cols = slice(n * step, (n + 1) * step)
        part = dot(norm_ref[...], wq_ref[:, cols]).astype(BF)
        qkv_ref[first:, :, cols] = part.reshape(count, WIN, step)
    grads = dw_ref[first:].reshape(tokens, c)
    for n in range(c // step):
        cols = slice(n * step, (n + 1) * step)
        part = dot_nt(grads, wp_ref[cols, :]).astype(BF)
        dh_ref[first:, :, cols] = part.reshape(count, WIN, step)


def project(shift, x, d, w_qkv, w_proj, gain, halo=None, carried=None):
    c = x.shape[-1]
    count = x.shape[1] // WW
    outs = [
        jax.ShapeDtypeStruct((count, WIN, c), BF),
        jax.ShapeDtypeStruct((count, WIN, c), BF),
        jax.ShapeDtypeStruct((c, count * WIN), BF),
        jax.ShapeDtypeStruct((count, WIN, 3 * c), BF),
        jax.ShapeDtypeStruct((count, WIN, c), BF),
    ]
    scalar = pl.BlockSpec(memory_space=pltpu.SMEM)
    if carried is None:
        whole = pl.BlockSpec(memory_space=pltpu.VMEM)
        return pl.pallas_call(
            lambda shift_ref, *refs: project_kernel(shift_ref, None, *refs),
            in_specs=[scalar] + [whole] * 5,
            out_shape=outs,
            scratch_shapes=[pltpu.VMEM(((count - 1) * WIN, c), BF)],
            compiler_params=PARAMS,
            name="project_rest",
        )(shift, x, d, w_qkv, w_proj, gain)
    block = pl.BlockSpec((WH, WW, c), lambda w: (0, 0, 0))

    def one(array):
        return pl.BlockSpec(array.shape, lambda w: (0,) * array.ndim)

    return pl.pallas_call(
        project_kernel,
        grid=(1,),
        in_specs=[scalar, one(halo), block, block, one(w_qkv), one(w_proj), one(gain)]
        + [pl.BlockSpec(memory_space=pl.ANY) for _ in carried],
        out_specs=[
            pl.BlockSpec((1, WIN, c), lambda w: (0, 0, 0)),
            pl.BlockSpec((1, WIN, c), lambda w: (0, 0, 0)),
            pl.BlockSpec((c, WIN), lambda w: (0, 0)),
            pl.BlockSpec((1, WIN, 3 * c), lambda w: (0, 0, 0)),
            pl.BlockSpec((1, WIN, c), lambda w: (0, 0, 0)),
        ],
        out_shape=outs,
        scratch_shapes=[pltpu.VMEM((WIN, c), BF)],
        input_output_aliases={7 + n: n for n in range(5)},
        compiler_params=PARAMS,
        name="project_rim",
    )(shift, halo, x, d, w_qkv, w_proj, gain, *carried)


def own_blocks(turned):
    rows = []
    for a in range(SLAB):
        part = turned[a * HD : (a + 1) * HD]
        gap = jnp.zeros_like(part)
        rows.append(jnp.concatenate([part if b == a else gap for b in range(SLAB)], axis=1))
    return jnp.concatenate(rows, axis=0)


def own_lanes(slab):
    lane = lax.broadcasted_iota(jnp.int32, slab.shape, 1)
    return jnp.concatenate(
        [jnp.where(lane // HD == a, slab, jnp.zeros_like(slab)) for a in range(SLAB)], axis=0
    )


def attend_slab(q, k, v, dh, bias_ref, sum_ref, head, first):
    factor = HD ** (-0.5)
    k_turned, v_turned = k.T, v.T
    scores = dot(k, own_blocks(q.T))
    d_soft = dot(v, own_blocks(dh.T))
    soft_all, d_all, att, dq = [], [], [], []
    for a in range(SLAB):
        lanes = slice(a * WIN, (a + 1) * WIN)
        part = slice(a * HD, (a + 1) * HD)
        score = scores[:, lanes] * (factor * LOG2E) + bias_ref[head + first + a]
        raised = jnp.exp2(score - jnp.max(score, axis=0, keepdims=True))
        attention = raised * (1.0 / jnp.sum(raised, axis=0, keepdims=True))
        soft_low = attention.astype(BF)
        soft = d_soft[:, lanes]
        d_score = attention * (soft - jnp.sum(attention * soft, axis=0, keepdims=True))
        sum_ref[first + a] += d_score
        d_low = d_score.astype(BF)
        soft_all.append(soft_low)
        d_all.append(d_low)
        att.append(dot(v_turned[part], soft_low))
        dq.append(dot(k_turned[part], d_low))
    att = jnp.concatenate(att, axis=0).astype(BF)
    dq = (jnp.concatenate(dq, axis=0) * factor).astype(BF).T
    dk = (dot(jnp.concatenate(d_all, axis=1), own_lanes(q)) * factor).astype(BF)
    dv = dot(jnp.concatenate(soft_all, axis=1), own_lanes(dh)).astype(BF)
    return att, dq, dk, dv


def fold_table(sum_ref, hot_ref, row_ref, heads):
    odd = odd_lanes(WH)
    for h in range(heads):
        sums = [None, None]
        for col in range(WW):
            tile = sum_ref[h, pl.ds(col, WH, stride=WW), :]
            for parity in range(2):
                kept = jnp.where(odd, tile, 0.0) if parity else jnp.where(odd, 0.0, tile)
                moved = pltpu.roll(kept, (WW - 1 - col - WW * parity) % LANES, 1)
                sums[parity] = moved if col == 0 else sums[parity] + moved
        for parity in range(2):
            row_ref[h, parity * WH : (parity + 1) * WH, :] = sums[parity]
    spans = []
    for first in range(SPANS):
        span = None
        for parity in range(2):
            row = parity + WH - 1 - first
            if 0 <= row < WH:
                part = row_ref[:, parity * WH + row, :]
                span = part if span is None else span + part
        spans.append(span)
    return joined3(dot_nt(split3(jnp.concatenate(spans, axis=1)), hot_ref[...]))


def attend_kernel(scales, slabs, base, split, *refs):
    core_ref, qkv_ref, dh_ref, bias_ref, hot_ref, nt_ref, d_ref = refs[:7]
    dp_ref, att_ref, sum_ref, row_ref = refs[7], refs[-3], refs[-2], refs[-1]
    count, _, c = dh_ref.shape
    heads = slabs * SLAB
    wide = slabs * LANES
    tokens = count * WIN
    sum_ref[...] = jnp.zeros_like(sum_ref)

    def window(w, carry):
        for s in range(slabs):
            at = (base + s) * LANES
            att, dq, dk, dv = attend_slab(
                qkv_ref[w, :, at : at + LANES],
                qkv_ref[w, :, c + at : c + at + LANES],
                qkv_ref[w, :, 2 * c + at : 2 * c + at + LANES],
                dh_ref[w, :, at : at + LANES],
                bias_ref,
                sum_ref,
                base * SLAB,
                s * SLAB,
            )
            lanes = slice(s * LANES, (s + 1) * LANES)
            att_ref[lanes, pl.ds(pl.multiple_of(w * WIN, WIN), WIN)] = att
            for n, part in enumerate((dq, dk, dv)):
                dp_ref[w, :, n * wide + s * LANES : n * wide + (s + 1) * LANES] = part
        return carry

    lax.fori_loop(0, count, window, 0)
    grad_scale, table_scale = scales
    table = fold_table(sum_ref, hot_ref, row_ref, heads) * table_scale
    d_rows = d_ref[...].reshape(tokens, c)
    if not split:
        grad_ref, proj_ref, table_ref = refs[8:11]
        for n in range(3 * slabs):
            cols = slice(n * LANES, (n + 1) * LANES)
            part = dp_ref[:, :, cols].reshape(tokens, LANES)
            grad_ref[:, cols] = (dot(nt_ref[...], part) * grad_scale).astype(BF)
        proj_ref[...] = (dot(att_ref[...], d_rows) * grad_scale).astype(BF)
        table_ref[...] = table
        return
    kept_ref, sent_ref, table_ref, both_ref = refs[8:12]
    core = bits_of(core_ref, 0, 1)
    low = 2 * kept_ref.shape[0]
    top = c // (low * UNIT)
    per_top = 3 * slabs
    for n in range(0, per_top, 2):
        wide_n = min(2, per_top - n)
        part = dp_ref[:, :, n * LANES : (n + wide_n) * LANES].reshape(tokens, wide_n * LANES)
        grad = (dot(nt_ref[...], part) * grad_scale).astype(BF)
        for t in range(top):
            for b in range(low):
                row = (t * low + b) * UNIT
                for m in range(wide_n):
                    both_ref[(b % 2) ^ core, b // 2, t * per_top + n + m] = grad[
                        row : row + UNIT, m * LANES : (m + 1) * LANES
                    ]
    tiles = c // LANES
    grad = (dot(att_ref[...], d_rows) * grad_scale).astype(BF)
    for s in range(slabs):
        for b in range(low):
            row = (s * low + b) * UNIT
            for m in range(tiles):
                both_ref[(b % 2) ^ core, b // 2, top * per_top + s * tiles + m] = grad[
                    row : row + UNIT, m * LANES : (m + 1) * LANES
                ]
    table_ref[...] = jnp.zeros_like(table_ref)
    rows = slice(base * SLAB, base * SLAB + heads)
    entries = table.shape[1]
    for n in range(table_ref.shape[0]):
        lanes = min(LANES, entries - n * LANES)
        table_ref[n, rows, :lanes] = table[:, n * LANES : n * LANES + lanes]
    kept_ref[...] = both_ref[0]
    units = kept_ref.shape[0] * kept_ref.shape[1]
    sent_ref[:units] = both_ref[1].reshape(units, UNIT, LANES)
    sent_ref[units:] = table_ref[...].astype(BF)


def attend(base, slabs, qkv, dh, bias, hot, nt, d, scales, core, n_dev):
    count, _, c = dh.shape
    heads = slabs * SLAB
    wide = heads * HD
    tokens = count * WIN
    entries = hot.shape[0]
    split = c // n_dev == UNIT
    outs = [jax.ShapeDtypeStruct((count, WIN, 3 * wide), BF)]
    scratch = []
    if split:
        top = c // LANES
        low = n_dev // top
        units = top * 3 * slabs + slabs * (c // LANES)
        tables = -(-entries // LANES)
        outs += [
            jax.ShapeDtypeStruct((low // 2, units, UNIT, LANES), BF),
            jax.ShapeDtypeStruct((low // 2 * units + tables, UNIT, LANES), BF),
            jax.ShapeDtypeStruct((tables, UNIT, LANES), F32),
        ]
        scratch = [pltpu.VMEM((2, low // 2, units, UNIT, LANES), BF)]
    else:
        outs += [
            jax.ShapeDtypeStruct((c, 3 * wide), BF),
            jax.ShapeDtypeStruct((wide, c), BF),
            jax.ShapeDtypeStruct((heads, entries), F32),
        ]
    whole = pl.BlockSpec(memory_space=pltpu.VMEM)
    return pl.pallas_call(
        lambda *refs: attend_kernel(scales, slabs, base, split, *refs),
        in_specs=[pl.BlockSpec(memory_space=pltpu.SMEM)] + [whole] * 6,
        out_shape=outs,
        scratch_shapes=scratch
        + [
            pltpu.VMEM((wide, tokens), BF),
            pltpu.VMEM((heads, WIN, WIN), F32),
            pltpu.VMEM((heads, 2 * WH, LANES), F32),
        ],
        compiler_params=PARAMS,
    )(core, qkv, dh, bias, hot, nt, d)


def input_rows(dp_refs, windows, x_ref, d_ref, w_ref, gain_ref, store):
    c = x_ref.shape[-1]
    start, stop = windows
    d_normed = None
    for n in range(3):
        parts = []
        for dp_ref in dp_refs:
            wide = dp_ref.shape[-1] // 3
            part = dp_ref[start:stop, :, n * wide : (n + 1) * wide]
            parts.append(part.reshape((stop - start) * WIN, wide))
        part = dot_nt(jnp.concatenate(parts, axis=1), w_ref[:, n * c : (n + 1) * c])
        d_normed = part if d_normed is None else d_normed + part
    for w in range(start, stop):
        grad = d_normed[(w - start) * WIN : (w - start + 1) * WIN]
        normal, inv_std = norm_stats(x_ref[w].astype(F32))
        scaled = grad * gain_ref[...]
        branch = inv_std * (
            scaled
            - jnp.mean(scaled, axis=-1, keepdims=True)
            - normal * jnp.mean(scaled * normal, axis=-1, keepdims=True)
        )
        store(w, (d_ref[w].astype(F32) + branch).astype(BF))


def input_rim_kernel(dp0_ref, dp1_ref, x_ref, d_ref, w_ref, gain_ref, out_ref):
    def store(w, value):
        out_ref[...] = value

    input_rows((dp0_ref, dp1_ref), (0, 1), x_ref, d_ref, w_ref, gain_ref, store)


def placed(select, first, second):
    c = first.shape[-1]
    pair = pair_rows(first.reshape(WH, WW, c), second.reshape(WH, WW, c))
    return dot(select, pair).astype(BF).reshape(WH, WW, c)


def input_rest_kernel(
    shift_ref, dp0_ref, dp1_ref, x_ref, d_ref, w_ref, gain_ref, rim_ref, out_ref, end_ref, row_ref
):
    count = x_ref.shape[0]
    select = shift_matrix(shift_ref[0])
    row_ref[0] = rim_ref[...]

    def store(w, value):
        row_ref[w] = value

    half = (count + 1) // 2
    for windows in ((1, half), (half, count)):
        input_rows((dp0_ref, dp1_ref), windows, x_ref, d_ref, w_ref, gain_ref, store)
        for w in range(windows[0], windows[1]):
            out_ref[:, (w - 1) * WW : w * WW, :] = placed(select, row_ref[w - 1], row_ref[w])
    end_ref[...] = row_ref[count - 1]


def place_kernel(shift_ref, end_ref, rim_ref, grid_ref, out_ref):
    out_ref[...] = placed(shift_matrix(shift_ref[0]), end_ref[...], rim_ref[...])


def input_rim(dps, x, d, w_qkv, gain):
    return pl.pallas_call(
        input_rim_kernel,
        out_shape=jax.ShapeDtypeStruct(x.shape[1:], BF),
        compiler_params=PARAMS,
        name="input_rim",
    )(*dps, x, d, w_qkv, gain)


def input_rest(shift, dps, x, d, w_qkv, gain, rim):
    count, _, c = x.shape
    whole = pl.BlockSpec(memory_space=pltpu.VMEM)
    return pl.pallas_call(
        input_rest_kernel,
        in_specs=[pl.BlockSpec(memory_space=pltpu.SMEM)] + [whole] * 7,
        out_shape=(
            jax.ShapeDtypeStruct((WH, count * WW, c), BF),
            jax.ShapeDtypeStruct((WIN, c), BF),
        ),
        scratch_shapes=[pltpu.VMEM((count, WIN, c), BF)],
        compiler_params=PARAMS,
        name="input_rest",
    )(shift, *dps, x, d, w_qkv, gain, rim)


def place_last(shift, end, rim, grid):
    last = grid.shape[1] // WW - 1
    c = grid.shape[2]
    one = pl.BlockSpec((WIN, c), lambda n: (0, 0))
    return pl.pallas_call(
        place_kernel,
        grid=(1,),
        in_specs=[
            pl.BlockSpec(memory_space=pltpu.SMEM),
            one,
            one,
            pl.BlockSpec(memory_space=pl.ANY),
        ],
        out_specs=pl.BlockSpec((WH, WW, c), lambda n: (0, last, 0)),
        out_shape=jax.ShapeDtypeStruct(grid.shape, BF),
        input_output_aliases={3: 0},
        compiler_params=PARAMS,
        name="place_last",
    )(shift, end, rim, grid)


def pair_sum(own, parts):
    if len(parts) == 1:
        return own + parts[0]
    return (own + parts[0]) + (parts[1] + parts[2])


def low_kernel(me_ref, kept_ref, got_ref, table_ref, own_ref, sent1_ref, sent2_ref, sent3_ref, out_ref):
    blocks, units = kept_ref.shape[:2]
    table = table_ref[...].astype(BF).astype(F32) + got_ref[blocks * units :].astype(F32)
    out_ref[...] = table
    mine = bits_of(me_ref, 1, 2)
    for n, sent_ref in enumerate((None, sent1_ref, sent2_ref, sent3_ref)):
        b = mine ^ n
        total = kept_ref[b].astype(F32) + got_ref[pl.ds(b * units, units)].astype(F32)
        if n == 0:
            own_ref[...] = total
        else:
            sent_ref[:units] = total.astype(BF)
            sent_ref[units:] = table.astype(BF)


def low_stage(mine, kept, got, table):
    _, units = kept.shape[:2]
    tables = table.shape[0]
    whole = pl.BlockSpec(memory_space=pltpu.VMEM)
    sent = jax.ShapeDtypeStruct((units + tables, UNIT, LANES), BF)
    return pl.pallas_call(
        low_kernel,
        in_specs=[pl.BlockSpec(memory_space=pltpu.SMEM)] + [whole] * 3,
        out_shape=(
            jax.ShapeDtypeStruct((units, UNIT, LANES), F32),
            sent,
            sent,
            sent,
            jax.ShapeDtypeStruct(table.shape, F32),
        ),
        compiler_params=PARAMS,
    )(mine, kept, got, table)


def top_kernel(me_ref, *refs):
    (own0, table0), got0 = refs[:2], refs[2:5]
    (own1, table1), got1 = refs[5:7], refs[7:10]
    own_ref, sent_refs, out_ref, sum0_ref, sum1_ref = refs[10], refs[11:14], refs[14], refs[15], refs[16]
    table = None
    for own, gots, sum_ref, part in ((own0, got0, sum0_ref, table0), (own1, got1, sum1_ref, table1)):
        units = own.shape[0]
        sum_ref[...] = pair_sum(own[...], [g[:units].astype(F32) for g in gots])
        part = pair_sum(part[...].astype(BF).astype(F32), [g[units:].astype(F32) for g in gots])
        table = part if table is None else table + part
    out_ref[...] = table
    top = 1 + len(sent_refs)
    slabs0, slabs1 = (s.shape[0] // (4 * 4) for s in (own0, own1))
    proj0 = own0.shape[0] - slabs0 * 4
    proj1 = own1.shape[0] - slabs1 * 4
    n0, n1 = proj0 // top, proj1 // top
    mine = bits_of(me_ref, 3, 2)
    for n in range(top):
        t = mine ^ n
        target = own_ref if n == 0 else sent_refs[n - 1]
        kind = F32 if n == 0 else BF
        target[:n0] = sum0_ref[pl.ds(t * n0, n0)].astype(kind)
        target[n0 : n0 + n1] = sum1_ref[pl.ds(t * n1, n1)].astype(kind)

        @pl.when(t < slabs0)
        def _():
            target[n0 + n1 : n0 + n1 + 4] = sum0_ref[pl.ds(proj0 + t * 4, 4)].astype(kind)

        @pl.when(t >= slabs0)
        def _():
            target[n0 + n1 : n0 + n1 + 4] = sum1_ref[pl.ds(proj1 + (t - slabs0) * 4, 4)].astype(kind)

        if n:
            target[n0 + n1 + 4 :] = table.astype(BF)


def top_stage(mine, first, second):
    own0, got0, table0 = first
    own1, got1, table1 = second
    tables = table0.shape[0]
    units = (own0.shape[0] + own1.shape[0]) // 4
    whole = pl.BlockSpec(memory_space=pltpu.VMEM)
    sent = jax.ShapeDtypeStruct((units + tables, UNIT, LANES), BF)
    return pl.pallas_call(
        top_kernel,
        in_specs=[pl.BlockSpec(memory_space=pltpu.SMEM)] + [whole] * 10,
        out_shape=(
            jax.ShapeDtypeStruct((units, UNIT, LANES), F32),
            sent,
            sent,
            sent,
            jax.ShapeDtypeStruct(table0.shape, F32),
        ),
        scratch_shapes=[pltpu.VMEM(own0.shape, F32), pltpu.VMEM(own1.shape, F32)],
        compiler_params=PARAMS,
        name="top_stage",
    )(mine, own0, table0, *got0, own1, table1, *got1)


def finish_kernel(
    slabs, me_ref, own_ref, table_ref, got1, got2, got3, w_ref, gain_ref, qkv_ref, proj_ref, g_ref, t_ref
):
    gots = (got1, got2, got3)
    units = own_ref.shape[0]
    total = pair_sum(own_ref[...], [g[:units].astype(F32) for g in gots])
    table = pair_sum(table_ref[...].astype(BF).astype(F32), [g[units:].astype(F32) for g in gots])
    c = proj_ref.shape[1]
    tiles = c // LANES
    unit = 0
    for base, count in ((0, slabs[0]), (slabs[0], slabs[1])):
        for n in range(3):
            for s in range(count):
                at = n * c + (base + s) * LANES
                qkv_ref[:, at : at + LANES] = total[unit]
                unit += 1
    for m in range(tiles):
        proj_ref[:, m * LANES : (m + 1) * LANES] = total[unit + m]
    start = pl.multiple_of(me_ref[0] * UNIT, UNIT)
    rows = w_ref[pl.ds(start, UNIT), :].astype(F32)
    products = jnp.sum(rows * qkv_ref[...], axis=1, keepdims=True)
    lane = lax.broadcasted_iota(jnp.int32, (UNIT, c), 1)
    row = lax.broadcasted_iota(jnp.int32, (UNIT, c), 0)
    gains = jnp.where(lane == start + row, gain_ref[...], 0.0)
    column = products / jnp.sum(gains, axis=1, keepdims=True)
    g_ref[...] = jnp.broadcast_to(column, (UNIT, LANES)).T[:1, :]
    entries = t_ref.shape[1]
    for n in range(table.shape[0]):
        lanes = min(LANES, entries - n * LANES)
        t_ref[:, n * LANES : n * LANES + lanes] = table[n, :, :lanes]


def finish(slabs, me, own, table, gots, w_qkv, gain, entries):
    c = w_qkv.shape[0]
    whole = pl.BlockSpec(memory_space=pltpu.VMEM)
    return pl.pallas_call(
        lambda *refs: finish_kernel(slabs, *refs),
        in_specs=[pl.BlockSpec(memory_space=pltpu.SMEM)] + [whole] * 7,
        out_shape=(
            jax.ShapeDtypeStruct((UNIT, 3 * c), F32),
            jax.ShapeDtypeStruct((UNIT, c), F32),
            jax.ShapeDtypeStruct((1, UNIT), F32),
            jax.ShapeDtypeStruct((H, entries), F32),
        ),
        compiler_params=PARAMS,
        name="finish",
    )(me, own, table, *gots, w_qkv, gain)


def flat_permute(value, mask):
    total = lax.axis_size("lon") * lax.axis_size("lat")
    return lax.ppermute(value, ("lon", "lat"), [(n, n ^ mask) for n in range(total)])


def bit_groups(total):
    bits = total.bit_length() - 1
    sizes = [1]
    while sum(sizes) < bits:
        sizes.append(min(2, bits - sum(sizes)))
    return sizes


def scatter_sum(matrix):
    n_lat = lax.axis_size("lat")
    total = lax.axis_size("lon") * n_lat
    me = lax.axis_index("lon") * n_lat + lax.axis_index("lat")
    rows, cols = matrix.shape
    blocks = matrix.reshape(total, rows // total, cols)
    low = 0
    sizes = bit_groups(total)
    for size in sizes:
        ways = 1 << size
        mine = (me >> low) & (ways - 1)
        view = blocks.reshape(blocks.shape[0] // ways, ways, rows // total, cols)
        kept = lax.dynamic_index_in_dim(view, mine, 1, keepdims=False).astype(F32)
        for n in range(1, ways):
            sent = lax.dynamic_index_in_dim(view, mine ^ n, 1, keepdims=False)
            kept = kept + flat_permute(sent, n << low).astype(F32)
        low += size
        blocks = kept if low == sum(sizes) else kept.astype(BF)
    return blocks.reshape(rows // total, cols)


def full_sum(value):
    total = lax.axis_size("lon") * lax.axis_size("lat")
    low = 0
    for size in bit_groups(total):
        value = pair_sum(value, [flat_permute(value, n << low) for n in range(1, 1 << size)])
        low += size
    return value


def ring_shift(value, steps):
    count = lax.axis_size("lon")
    return lax.ppermute(value, "lon", [(n, (n + steps) % count) for n in range(count)])


def step(inputs, d_out, w_qkv, w_proj, gain, bias_table, rel_index, shifts):
    n_lon = lax.axis_size("lon")
    n_lat = lax.axis_size("lat")
    n_dev = n_lon * n_lat
    _, columns, c = inputs.shape
    tokens = inputs.shape[0] * columns * n_dev
    scales = (tokens ** (-0.5), (tokens // WIN) ** (-0.5))
    entries = bias_table.shape[0]
    gain_row = gain.reshape(1, c)
    me = (lax.axis_index("lon") * n_lat + lax.axis_index("lat")).astype(jnp.int32).reshape(1)
    split = c // n_dev == UNIT and n_lat == 4
    total = c // LANES
    slabs = (total - 1, 1)

    rim = jnp.stack([inputs[:, columns - WW :], d_out[:, columns - WW :]])
    halo = ring_shift(rim, 1)
    hot, bias = expand_bias(me, rel_index, bias_table.T)
    carried = project(shifts, inputs, d_out, w_qkv, w_proj, gain_row)
    x, d, nt, qkv, dh = project(
        shifts, inputs, d_out, w_qkv, w_proj, gain_row, halo=halo, carried=tuple(carried)
    )

    def three(values, low):
        return [flat_permute(value, n << low) for n, value in enumerate(values, 1)]

    shared = (qkv, dh, bias, hot, nt, d, scales, me, n_dev)
    dp0, *out0 = attend(0, slabs[0], *shared)
    if split:
        got0 = flat_permute(out0[1], 1)
    dp1, *out1 = attend(slabs[0], slabs[1], *shared)
    if split:
        got1 = flat_permute(out1[1], 1)
        own0, *sent0, table0 = low_stage(me, out0[0], got0, out0[2])
        got0 = three(sent0, 1)
    first = input_rim((dp0, dp1), x, d, w_qkv, gain_row)
    returned = ring_shift(first, -1)
    if split:
        own1, *sent1, table1 = low_stage(me, out1[0], got1, out1[2])
        got1 = three(sent1, 1)
    grid, end = input_rest(shifts, (dp0, dp1), x, d, w_qkv, gain_row, first)
    if split:
        own, *sent, table = top_stage(me, (own0, got0, table0), (own1, got1, table1))
        got = three(sent, 3)
    d_inputs = place_last(shifts, end, returned, grid)
    if split:
        g_qkv, g_proj, g_gain, g_table = finish(
            slabs, me, own, table, got, w_qkv, gain_row, entries
        )
        return (d_inputs, g_qkv, g_proj, g_gain.reshape(UNIT), g_table.T)

    parts = []
    for n in range(3):
        for out, count in ((out0, slabs[0]), (out1, slabs[1])):
            parts.append(out[0][:, n * count * LANES : (n + 1) * count * LANES])
    parts.append(jnp.concatenate([out0[1], out1[1]], axis=0))
    own = scatter_sum(jnp.concatenate(parts, axis=1))
    g_qkv, g_proj = own[:, : 3 * c], own[:, 3 * c :]
    g_table = full_sum(jnp.concatenate([out0[2], out1[2]], axis=0)).T
    rows = c // n_dev
    w_rows = lax.dynamic_slice_in_dim(w_qkv, me[0] * rows, rows, 0).astype(F32)
    gain_rows = lax.dynamic_slice_in_dim(gain, me[0] * rows, rows, 0)
    g_gain = jnp.sum(w_rows * g_qkv, axis=1) / gain_rows
    return (d_inputs, g_qkv, g_proj, g_gain, g_table)


def solution(mesh):
    return jax.shard_map(
        step,
        mesh=mesh,
        in_specs=(P("lat", "lon", None), P("lat", "lon", None), P(), P(), P(), P(), P(), P("lat")),
        out_specs=(
            P("lat", "lon", None),
            P(("lon", "lat"), None),
            P(("lon", "lat"), None),
            P(("lon", "lat")),
            P(),
        ),
        check_vma=False,
    )
```

time: 121 us -> 69 us (0.57)
  Pallas kernels: 58.6 us -> 31 us
  starting transfers between devices: 31.8 us -> 20.8 us
  waiting for transfers between devices: 12.7 us -> 7.14 us
  other arithmetic: 4.5 us -> 0.03 us
  local copies, waits for them, and re-layouts: 10.4 us -> 8.17 us
    pallas_call x7 -> x12, Pallas kernels: 58.6 us -> 31 us  [the longest x2 19.6 us: attend(): pl.pallas_call(lambda *refs: attend_kernel(scales, slabs, base, split, *r...]
    ppermute x21 -> x11, starting transfers between devices: 23.8 us -> 14.1 us  [flat_permute(): lax.ppermute(value, ('lon', 'lat'), [(n, n ^ mask) for n in range(total)])]
    ppermute x21 -> x11, waiting for transfers between devices: 12.7 us -> 7.13 us  [flat_permute(): lax.ppermute(value, ('lon', 'lat'), [(n, n ^ mask) for n in range(total)])]
    slice x17 -> x0, local copies, waits for them, and re-layouts: 5.5 us -> none  [the longest x2 1.95 us: span_codes(): lower = jnp.concatenate([rel[1:, 0, 0, ::-1], rel[1:, 1:, 0, 0]], axis=1)]
    unnamed x35 -> x16, local copies, waits for them, and re-layouts: 2.01 us -> 7.17 us
    reshape x10 -> x0, local copies, waits for them, and re-layouts: 1.76 us -> none  [the longest x1 1.02 us: span_codes(): rel = rel_index.reshape(WH, WW, WH, WW)]
    convert_element_type x4 -> x0, other arithmetic: 1.5 us -> none  [scatter_sum(): blocks = kept if low == sum(sizes) else kept.astype(BF)]
    ppermute x3 -> x2, starting transfers between devices: 8.06 us -> 6.66 us  [ring_shift(): lax.ppermute(value, 'lon', [(n, (n + steps) % count) for n in range(count)])]
  transfers between devices with their start and end apart: 24 -> 13, of which waited for: 10 -> 2; matrix products, arithmetic and copies ran while one was open for 7% -> 0% of each run, Pallas kernels for 16% -> 23%
where the time goes in v1:
time: 69 us; the launch traced here: 68.5 us
  Pallas kernels  31 us (45%)
  starting transfers between devices  20.8 us (30%)
  local copies, waits for them, and re-layouts  8.17 us (12%)
  waiting for transfers between devices  7.14 us (10%)
  between operations  1.43 us (2%)
    pallas_call x2, Pallas kernels, attend(): pl.pallas_call(lambda *refs: attend_kernel(scales, slabs, base, split, *r...  19.6 us
    ppermute x11, starting transfers between devices, flat_permute(): lax.ppermute(value, ('lon', 'lat'), [(n, n ^ mask) for n in range(total)])  14.1 us
    unnamed x16, local copies, waits for them, and re-layouts  7.17 us
    ppermute x11, waiting for transfers between devices, flat_permute(): lax.ppermute(value, ('lon', 'lat'), [(n, n ^ mask) for n in range(total)])  7.13 us
    ppermute x2, starting transfers between devices, ring_shift(): lax.ppermute(value, 'lon', [(n, (n + steps) % count) for n in range(count)])  6.66 us
    pallas_call x1, Pallas kernels, input_rest(): pl.pallas_call(input_rest_kernel, in_specs=[pl.BlockSpec(memory_space=plt...  3.66 us
    pallas_call x1, Pallas kernels, project(): pl.pallas_call(lambda shift_ref, *refs: project_kernel(shift_ref, None, *...  2.69 us
  transfers between devices with their start and end apart: 13, of which 2 were waited for; matrix products, arithmetic and copies ran while one was open for 0% of the time, Pallas kernels for 23%

profile of v1, /device:TPU:0, one launch (start us, length us, event | category | flops | bytes accessed | tf_op | source)
XLA Modules:
  0.0 68.5 jit_solution(13026046543196469103)
XLA Ops:
  0.6 1.0 %slice_bitcast_fusion = (bf16[1,8,16,512]{3,2,1,0:T(8,128)(2,1)S(1)}, bf16[1,8,16,512]{3,2,1,0:T(8,128)(2,1)S(1)}) fusion(bf16[8,128,512]{2,1,0:T(8,128)(2,1)} %d_ref.1, bf16[8,128,512]{2,1,0:T(8,128)(2,1)} %x_ref.1), kind=kLoop, calls=%fused_computation.1 | loop fusion | bytes 524288 | tf_op jit(solution)/shard_map/stack | solution.py:709
  1.7 3.0 %collective-permute-start = (bf16[2,8,16,512]{3,2,1,0:T(8,128)(2,1)S(1)}, bf16[2,8,16,512]{3,2,1,0:T(8,128)(2,1)S(1)}, u32[]{:S(2)}, u32[]{:S(2)}) collective-permute-start(bf16[2,8,16,512]{3,2,1,0:T(8,128)(2,1)S(1)} %pad_maximum_fusion), channel_id=1, source_target_pairs={{0,4},{4,8},{8,12},{12,16},{16,20},{20,24},{24,28},{28,0},{1,5},{5... | collective-permute-start | bytes 786440 | tf_op jit(solution)/shard_map/ppermute | solution.py:692
  5.4 0.8 %copy-done.5 = s32[128,128]{1,0:T(8,128)S(1)} copy-done((s32[128,128]{1,0:T(8,128)S(1)}, s32[128,128]{1,0:T(8,128)}, u32[]{:S(2)}) %copy-start.5) | copy-done | bytes 65560
  7.0 1.1 %expand_bias.1 = (bf16[465,1152]{1,0:T(8,128)(2,1)S(1)}, f32[16,128,128]{2,1,0:T(8,128)S(1)}) custom-call(s32[1]{0:T(128)} %bitcast.me_ref.refs_0_, s32[128,128]{1,0:T(8,128)S(1)} %copy-done.5, f32[16,465]{1,0:T(8,128)S(1)} %bitcast.14), custom_call_target="tpu_custom_call" | custom-call | tf_op jit(solution)/shard_map/expand_bias/pallas_call | solution.py:92
  8.0 1.4 %copy-done = bf16[512,1536]{1,0:T(8,128)(2,1)S(1)} copy-done((bf16[512,1536]{1,0:T(8,128)(2,1)S(1)}, bf16[512,1536]{1,0:T(8,128)(2,1)}, u32[]{:S(2)}) %copy-start) | copy-done | bytes 1572888
  9.4 1.2 %copy-done.2 = bf16[8,128,512]{2,1,0:T(8,128)(2,1)S(1)} copy-done((bf16[8,128,512]{2,1,0:T(8,128)(2,1)S(1)}, bf16[8,128,512]{2,1,0:T(8,128)(2,1)}, u32[]{:S(2)}) %copy-start.2) | copy-done | bytes 1048600
  10.7 1.2 %copy-done.3 = bf16[8,128,512]{2,1,0:T(8,128)(2,1)S(1)} copy-done((bf16[8,128,512]{2,1,0:T(8,128)(2,1)S(1)}, bf16[8,128,512]{2,1,0:T(8,128)(2,1)}, u32[]{:S(2)}) %copy-start.3) | copy-done | bytes 1048600
  11.9 1.0 %copy-done.4 = bf16[512,512]{1,0:T(8,128)(2,1)S(1)} copy-done((bf16[512,512]{1,0:T(8,128)(2,1)S(1)}, bf16[512,512]{1,0:T(8,128)(2,1)}, u32[]{:S(2)}) %copy-start.4) | copy-done | bytes 524312
  13.6 2.7 %project_rest.1 = (bf16[8,128,512]{2,1,0:T(8,128)(2,1)S(1)}, bf16[8,128,512]{2,1,0:T(8,128)(2,1)S(1)}, bf16[512,1024]{1,0:T(8,128)(2,1)S(1)}, bf16[8,128,1536]{2,1,0:T(8,128)(2,1)S(1)}, bf16[8,128,512]{2,1,0:T(8,128)(2,1)S(1)}) custom-call(s32[1]{0:T(128)S(6)} %copy.25.shift_ref, bf16[8,128,512]{2,1,0:T(8,128)(2,1)S(1)} %copy-done.3, ...), custom_call_target="tpu_custom_call" | custom-call | tf_op jit(solution)/shard_map/project_rest/pallas_call | solution.py:174
  16.3 0.9 %project_rim.1 = (bf16[8,128,512]{2,1,0:T(8,128)(2,1)S(1)}, bf16[8,128,512]{2,1,0:T(8,128)(2,1)S(1)}, bf16[512,1024]{1,0:T(8,128)(2,1)S(1)}, bf16[8,128,1536]{2,1,0:T(8,128)(2,1)S(1)}, bf16[8,128,512]{2,1,0:T(8,128)(2,1)S(1)}) custom-call(s32[1]{0:T(128)S(6)} %copy.25.shift_ref, ...), custom_call_target="tpu_custom_call", output_to_operand_aliasing={{0}: (7, {}), {1}: (8, {}), {2}: (9, {}), {3}: (10, {}), {4... | custom-call | tf_op jit(solution)/shard_map/project_rim/pallas_call | solution.py:187
  17.2 13.6 %shard_map.119 = (bf16[8,128,1152]{2,1,0:T(8,128)(2,1)S(1)}, bf16[4,48,16,128]{3,2,1,0:T(8,128)(2,1)S(1)}, bf16[196,16,128]{2,1,0:T(8,128)(2,1)S(1)}, f32[4,16,128]{2,1,0:T(8,128)S(1)}) custom-call(s32[1]{0:T(128)} %bitcast.me_ref.refs_0_, bf16[8,128,1536]{2,1,0:T(8,128)(2,1)S(1)} %get-tuple-element.51.refs_1_, ...), custom_call_target="tpu_custom_call" | custom-call | tf_op jit(solution)/shard_map/pallas_call | solution.py:380
  30.9 6.0 %shard_map.120 = (bf16[8,128,384]{2,1,0:T(8,128)(2,1)S(1)}, bf16[4,16,16,128]{3,2,1,0:T(8,128)(2,1)S(1)}, bf16[68,16,128]{2,1,0:T(8,128)(2,1)S(1)}, f32[4,16,128]{2,1,0:T(8,128)S(1)}) custom-call(s32[1]{0:T(128)} %bitcast.me_ref.refs_0_, bf16[8,128,1536]{2,1,0:T(8,128)(2,1)S(1)} %get-tuple-element.51.refs_1_, ...), custom_call_target="tpu_custom_call" | custom-call | tf_op jit(solution)/shard_map/pallas_call | solution.py:380
  37.7 1.6 %collective-permute-start.3 = (bf16[52,16,128]{2,1,0:T(8,128)(2,1)S(1)}, bf16[52,16,128]{2,1,0:T(8,128)(2,1)S(1)}, u32[]{:S(2)}, u32[]{:S(2)}) collective-permute-start(bf16[52,16,128]{2,1,0:T(8,128)(2,1)S(1)} %get-tuple-element.67), channel_id=1, source_target_pairs={{0,2},{1,3},{2,0},{3,1},{4,6},{5,7},{6,4},{7,5},{8,10},{9,11},{10,... | collective-permute-start | bytes 638984 | tf_op jit(solution)/shard_map/ppermute | solution.py:649
  39.2 1.5 %collective-permute-start.4 = (bf16[52,16,128]{2,1,0:T(8,128)(2,1)S(1)}, bf16[52,16,128]{2,1,0:T(8,128)(2,1)S(1)}, u32[]{:S(2)}, u32[]{:S(2)}) collective-permute-start(bf16[52,16,128]{2,1,0:T(8,128)(2,1)S(1)} %get-tuple-element.68), channel_id=1, source_target_pairs={{0,4},{1,5},{2,6},{3,7},{4,0},{5,1},{6,2},{7,3},{8,12},{9,13},{10,... | collective-permute-start | bytes 638984 | tf_op jit(solution)/shard_map/ppermute | solution.py:649
  41.3 1.6 %collective-permute-start.7 = (bf16[20,16,128]{2,1,0:T(8,128)(2,1)S(1)}, bf16[20,16,128]{2,1,0:T(8,128)(2,1)S(1)}, u32[]{:S(2)}, u32[]{:S(2)}) collective-permute-start(bf16[20,16,128]{2,1,0:T(8,128)(2,1)S(1)} %get-tuple-element.75), channel_id=1, source_target_pairs={{0,2},{1,3},{2,0},{3,1},{4,6},{5,7},{6,4},{7,5},{8,10},{9,11},{10,... | collective-permute-start | bytes 245768 | tf_op jit(solution)/shard_map/ppermute | solution.py:649
  42.9 1.5 %collective-permute-start.8 = (bf16[20,16,128]{2,1,0:T(8,128)(2,1)S(1)}, bf16[20,16,128]{2,1,0:T(8,128)(2,1)S(1)}, u32[]{:S(2)}, u32[]{:S(2)}) collective-permute-start(bf16[20,16,128]{2,1,0:T(8,128)(2,1)S(1)} %get-tuple-element.76), channel_id=1, source_target_pairs={{0,4},{1,5},{2,6},{3,7},{4,0},{5,1},{6,2},{7,3},{8,12},{9,13},{10,... | collective-permute-start | bytes 245768 | tf_op jit(solution)/shard_map/ppermute | solution.py:649
  44.4 6.9 %collective-permute-done.7.refs_7_ = bf16[20,16,128]{2,1,0:T(8,128)(2,1)S(1)} collective-permute-done((bf16[20,16,128]{2,1,0:T(8,128)(2,1)S(1)}, bf16[20,16,128]{2,1,0:T(8,128)(2,1)S(1)}, u32[]{:S(2)}, u32[]{:S(2)}) %collective-permute-start.7) | collective-permute-done | bytes 81952 | tf_op jit(solution)/shard_map/ppermute | solution.py:649
  51.3 2.4 %collective-permute-start.9 = (bf16[20,16,128]{2,1,0:T(8,128)(2,1)S(1)}, bf16[20,16,128]{2,1,0:T(8,128)(2,1)S(1)}, u32[]{:S(2)}, u32[]{:S(2)}) collective-permute-start(bf16[20,16,128]{2,1,0:T(8,128)(2,1)S(1)} %get-tuple-element.77), channel_id=1, source_target_pairs={{0,6},{1,7},{2,4},{3,5},{4,2},{5,3},{6,0},{7,1},{8,14},{9,15},{10,... | collective-permute-start | bytes 245768 | tf_op jit(solution)/shard_map/ppermute | solution.py:649
  53.7 0.8 %input_rim.1.rim_ref = bf16[128,512]{1,0:T(8,128)(2,1)S(1)} custom-call(bf16[8,128,1152]{2,1,0:T(8,128)(2,1)S(1)} %get-tuple-element.57.dp0_ref, bf16[8,128,384]{2,1,0:T(8,128)(2,1)S(1)} %get-tuple-element.58.dp1_ref, bf16[8,128,512]{2,1,0:T(8,128)(2,1)S(1)} %get-tuple-element.59.x_ref, bf16[8,128,512]{2,1,0:T(8,128)(2,1)S(1)} %get-tuple-element.56.refs_6_.d_ref, ...), custom_call_target="tpu_custom_call" | custom-call | tf_op jit(solution)/shard_map/input_rim/pallas_call | solution.py:454
  54.5 3.6 %collective-permute-start.1 = (bf16[128,512]{1,0:T(8,128)(2,1)S(1)}, bf16[128,512]{1,0:T(8,128)(2,1)S(1)}, u32[]{:S(2)}, u32[]{:S(2)}) collective-permute-start(bf16[128,512]{1,0:T(8,128)(2,1)S(1)} %input_rim.1.rim_ref), channel_id=1, source_target_pairs={{0,28},{4,0},{8,4},{12,8},{16,12},{20,16},{24,20},{28,24},{1,29},{... | collective-permute-start | bytes 393224 | tf_op jit(solution)/shard_map/ppermute | solution.py:692
  58.8 2.6 %collective-permute-start.11 = (bf16[20,16,128]{2,1,0:T(8,128)(2,1)S(1)}, bf16[20,16,128]{2,1,0:T(8,128)(2,1)S(1)}, u32[]{:S(2)}, u32[]{:S(2)}) collective-permute-start(bf16[20,16,128]{2,1,0:T(8,128)(2,1)S(1)} %get-tuple-element.81), channel_id=1, source_target_pairs={{0,16},{1,17},{2,18},{3,19},{4,20},{5,21},{6,22},{7,23},{8,24},{9,... | collective-permute-start | bytes 245768 | tf_op jit(solution)/shard_map/ppermute | solution.py:649
  61.4 1.6 %collective-permute-start.12 = (bf16[20,16,128]{2,1,0:T(8,128)(2,1)S(1)}, bf16[20,16,128]{2,1,0:T(8,128)(2,1)S(1)}, u32[]{:S(2)}, u32[]{:S(2)}) collective-permute-start(bf16[20,16,128]{2,1,0:T(8,128)(2,1)S(1)} %get-tuple-element.82), channel_id=1, source_target_pairs={{0,24},{1,25},{2,26},{3,27},{4,28},{5,29},{6,30},{7,31},{8,16},{9,... | collective-permute-start | bytes 245768 | tf_op jit(solution)/shard_map/ppermute | solution.py:649
  63.1 3.7 %input_rest.1 = (bf16[8,128,512]{2,1,0:T(8,128)(2,1)}, bf16[128,512]{1,0:T(8,128)(2,1)S(1)}) custom-call(s32[1]{0:T(128)S(6)} %copy.25.shift_ref, bf16[8,128,1152]{2,1,0:T(8,128)(2,1)S(1)} %get-tuple-element.57.dp0_ref, bf16[8,128,384]{2,1,0:T(8,128)(2,1)S(1)} %get-tuple-element.58.dp1_ref, bf16[8,128,512]{2,1,0:T(8,128)(2,1)S(1)} %get-tuple-element.59.x_ref, ...), custom_call_target="tpu_custom_call" | custom-call | tf_op jit(solution)/shard_map/input_rest/pallas_call | solution.py:465
  66.7 0.8 %place_last.1 = bf16[8,128,512]{2,1,0:T(8,128)(2,1)} custom-call(s32[1]{0:T(128)S(6)} %copy.25.shift_ref, bf16[128,512]{1,0:T(8,128)(2,1)S(1)} %get-tuple-element.60.end_ref, bf16[128,512]{1,0:T(8,128)(2,1)S(1)} %collective-permute-done.1.rim_ref, bf16[8,128,512]{2,1,0:T(8,128)(2,1)} %get-tuple-element.61.grid_ref), custom_call_target="tpu_custom_call", output_to_operand_aliasing={{}: (3, {})} | custom-call | tf_op jit(solution)/shard_map/place_last/pallas_call | solution.py:482
  (32 shorter events, 4.5 us)
Async XLA Ops:
  1.7 14.7 %collective-permute-start = (bf16[2,8,16,512]{3,2,1,0:T(8,128)(2,1)S(1)}, bf16[2,8,16,512]{3,2,1,0:T(8,128)(2,1)S(1)}, u32[]{:S(2)}, u32[]{:S(2)}) collective-permute-start(bf16[2,8,16,512]{3,2,1,0:T(8,128)(2,1)S(1)} %pad_maximum_fusion), channel_id=1, source_target_pairs={{0,4},{4,8},{8,12},{12,16},{16,20},{20,24},{24,28},{28,0},{1,5},{5... | collective-permute-start | bytes 786440 | tf_op jit(solution)/shard_map/ppermute | solution.py:692
  5.4 0.8 %copy-start.5 = (s32[128,128]{1,0:T(8,128)S(1)}, s32[128,128]{1,0:T(8,128)}, u32[]{:S(2)}) copy-start(s32[128,128]{1,0:T(8,128)} %rel_ref.1) | copy-start | bytes 196612
  6.2 0.8 %copy-start.7 = (f32[465,16]{0,1:T(8,128)S(1)}, f32[465,16]{0,1:T(8,128)}, u32[]{:S(2)}) copy-start(f32[465,16]{0,1:T(8,128)} %param.13) | copy-start | bytes 89284
  8.0 1.4 %copy-start = (bf16[512,1536]{1,0:T(8,128)(2,1)S(1)}, bf16[512,1536]{1,0:T(8,128)(2,1)}, u32[]{:S(2)}) copy-start(bf16[512,1536]{1,0:T(8,128)(2,1)} %refs_6_.1) | copy-start | bytes 4718596
  9.4 1.2 %copy-start.2 = (bf16[8,128,512]{2,1,0:T(8,128)(2,1)S(1)}, bf16[8,128,512]{2,1,0:T(8,128)(2,1)}, u32[]{:S(2)}) copy-start(bf16[8,128,512]{2,1,0:T(8,128)(2,1)} %d_ref.1) | copy-start | bytes 3145732
  10.7 1.2 %copy-start.3 = (bf16[8,128,512]{2,1,0:T(8,128)(2,1)S(1)}, bf16[8,128,512]{2,1,0:T(8,128)(2,1)}, u32[]{:S(2)}) copy-start(bf16[8,128,512]{2,1,0:T(8,128)(2,1)} %x_ref.1) | copy-start | bytes 3145732
  11.9 1.0 %copy-start.4 = (bf16[512,512]{1,0:T(8,128)(2,1)S(1)}, bf16[512,512]{1,0:T(8,128)(2,1)}, u32[]{:S(2)}) copy-start(bf16[512,512]{1,0:T(8,128)(2,1)} %wp_ref.1) | copy-start | bytes 1572868
  12.9 0.7 copy-start.6
  30.8 6.7 %collective-permute-start.2 = (bf16[196,16,128]{2,1,0:T(8,128)(2,1)S(1)}, bf16[196,16,128]{2,1,0:T(8,128)(2,1)S(1)}, u32[]{:S(2)}, u32[]{:S(2)}) collective-permute-start(bf16[196,16,128]{2,1,0:T(8,128)(2,1)S(1)} %get-tuple-element.63), channel_id=1, source_target_pairs={{0,1},{1,0},{2,3},{3,2},{4,5},{5,4},{6,7},{7,6},{8,9},{9,8},{10,11... | collective-permute-start | bytes 2408456 | tf_op jit(solution)/shard_map/ppermute | solution.py:649
  36.9 16.8 %copy-start.1 = (bf16[512,1536]{1,0:T(8,128)(2,1)S(1)}, bf16[512,1536]{1,0:T(8,128)(2,1)}, u32[]{:S(2)}) copy-start(bf16[512,1536]{1,0:T(8,128)(2,1)} %refs_6_.1) | copy-start | bytes 4718596
  36.9 4.3 %collective-permute-start.6 = (bf16[68,16,128]{2,1,0:T(8,128)(2,1)S(1)}, bf16[68,16,128]{2,1,0:T(8,128)(2,1)S(1)}, u32[]{:S(2)}, u32[]{:S(2)}) collective-permute-start(bf16[68,16,128]{2,1,0:T(8,128)(2,1)S(1)} %get-tuple-element.71), channel_id=1, source_target_pairs={{0,1},{1,0},{2,3},{3,2},{4,5},{5,4},{6,7},{7,6},{8,9},{9,8},{10,11... | collective-permute-start | bytes 835592 | tf_op jit(solution)/shard_map/ppermute | solution.py:649
  37.7 20.5 %collective-permute-start.3 = (bf16[52,16,128]{2,1,0:T(8,128)(2,1)S(1)}, bf16[52,16,128]{2,1,0:T(8,128)(2,1)S(1)}, u32[]{:S(2)}, u32[]{:S(2)}) collective-permute-start(bf16[52,16,128]{2,1,0:T(8,128)(2,1)S(1)} %get-tuple-element.67), channel_id=1, source_target_pairs={{0,2},{1,3},{2,0},{3,1},{4,6},{5,7},{6,4},{7,5},{8,10},{9,11},{10,... | collective-permute-start | bytes 638984 | tf_op jit(solution)/shard_map/ppermute | solution.py:649
  39.2 18.9 %collective-permute-start.4 = (bf16[52,16,128]{2,1,0:T(8,128)(2,1)S(1)}, bf16[52,16,128]{2,1,0:T(8,128)(2,1)S(1)}, u32[]{:S(2)}, u32[]{:S(2)}) collective-permute-start(bf16[52,16,128]{2,1,0:T(8,128)(2,1)S(1)} %get-tuple-element.68), channel_id=1, source_target_pairs={{0,4},{1,5},{2,6},{3,7},{4,0},{5,1},{6,2},{7,3},{8,12},{9,13},{10,... | collective-permute-start | bytes 638984 | tf_op jit(solution)/shard_map/ppermute | solution.py:649
  40.7 17.4 %collective-permute-start.5 = (bf16[52,16,128]{2,1,0:T(8,128)(2,1)S(1)}, bf16[52,16,128]{2,1,0:T(8,128)(2,1)S(1)}, u32[]{:S(2)}, u32[]{:S(2)}) collective-permute-start(bf16[52,16,128]{2,1,0:T(8,128)(2,1)S(1)} %get-tuple-element.69), channel_id=1, source_target_pairs={{0,6},{1,7},{2,4},{3,5},{4,2},{5,3},{6,0},{7,1},{8,14},{9,15},{10,... | collective-permute-start | bytes 638984 | tf_op jit(solution)/shard_map/ppermute | solution.py:649
  41.3 10.0 %collective-permute-start.7 = (bf16[20,16,128]{2,1,0:T(8,128)(2,1)S(1)}, bf16[20,16,128]{2,1,0:T(8,128)(2,1)S(1)}, u32[]{:S(2)}, u32[]{:S(2)}) collective-permute-start(bf16[20,16,128]{2,1,0:T(8,128)(2,1)S(1)} %get-tuple-element.75), channel_id=1, source_target_pairs={{0,2},{1,3},{2,0},{3,1},{4,6},{5,7},{6,4},{7,5},{8,10},{9,11},{10,... | collective-permute-start | bytes 245768 | tf_op jit(solution)/shard_map/ppermute | solution.py:649
  42.9 11.6 %collective-permute-start.8 = (bf16[20,16,128]{2,1,0:T(8,128)(2,1)S(1)}, bf16[20,16,128]{2,1,0:T(8,128)(2,1)S(1)}, u32[]{:S(2)}, u32[]{:S(2)}) collective-permute-start(bf16[20,16,128]{2,1,0:T(8,128)(2,1)S(1)} %get-tuple-element.76), channel_id=1, source_target_pairs={{0,4},{1,5},{2,6},{3,7},{4,0},{5,1},{6,2},{7,3},{8,12},{9,13},{10,... | collective-permute-start | bytes 245768 | tf_op jit(solution)/shard_map/ppermute | solution.py:649
  51.3 6.8 %collective-permute-start.9 = (bf16[20,16,128]{2,1,0:T(8,128)(2,1)S(1)}, bf16[20,16,128]{2,1,0:T(8,128)(2,1)S(1)}, u32[]{:S(2)}, u32[]{:S(2)}) collective-permute-start(bf16[20,16,128]{2,1,0:T(8,128)(2,1)S(1)} %get-tuple-element.77), channel_id=1, source_target_pairs={{0,6},{1,7},{2,4},{3,5},{4,2},{5,3},{6,0},{7,1},{8,14},{9,15},{10,... | collective-permute-start | bytes 245768 | tf_op jit(solution)/shard_map/ppermute | solution.py:649
  54.5 12.2 %collective-permute-start.1 = (bf16[128,512]{1,0:T(8,128)(2,1)S(1)}, bf16[128,512]{1,0:T(8,128)(2,1)S(1)}, u32[]{:S(2)}, u32[]{:S(2)}) collective-permute-start(bf16[128,512]{1,0:T(8,128)(2,1)S(1)} %input_rim.1.rim_ref), channel_id=1, source_target_pairs={{0,28},{4,0},{8,4},{12,8},{16,12},{20,16},{24,20},{28,24},{1,29},{... | collective-permute-start | bytes 393224 | tf_op jit(solution)/shard_map/ppermute | solution.py:692
  58.6 9.0 %collective-permute-start.10 = (bf16[20,16,128]{2,1,0:T(8,128)(2,1)S(1)}, bf16[20,16,128]{2,1,0:T(8,128)(2,1)S(1)}, u32[]{:S(2)}, u32[]{:S(2)}) collective-permute-start(bf16[20,16,128]{2,1,0:T(8,128)(2,1)S(1)} %get-tuple-element.80), channel_id=1, source_target_pairs={{0,8},{1,9},{2,10},{3,11},{4,12},{5,13},{6,14},{7,15},{8,0},{9,1},... | collective-permute-start | bytes 245768 | tf_op jit(solution)/shard_map/ppermute | solution.py:649
  58.8 8.8 %collective-permute-start.11 = (bf16[20,16,128]{2,1,0:T(8,128)(2,1)S(1)}, bf16[20,16,128]{2,1,0:T(8,128)(2,1)S(1)}, u32[]{:S(2)}, u32[]{:S(2)}) collective-permute-start(bf16[20,16,128]{2,1,0:T(8,128)(2,1)S(1)} %get-tuple-element.81), channel_id=1, source_target_pairs={{0,16},{1,17},{2,18},{3,19},{4,20},{5,21},{6,22},{7,23},{8,24},{9,... | collective-permute-start | bytes 245768 | tf_op jit(solution)/shard_map/ppermute | solution.py:649
  61.4 6.3 %collective-permute-start.12 = (bf16[20,16,128]{2,1,0:T(8,128)(2,1)S(1)}, bf16[20,16,128]{2,1,0:T(8,128)(2,1)S(1)}, u32[]{:S(2)}, u32[]{:S(2)}) collective-permute-start(bf16[20,16,128]{2,1,0:T(8,128)(2,1)S(1)} %get-tuple-element.82), channel_id=1, source_target_pairs={{0,24},{1,25},{2,26},{3,27},{4,28},{5,29},{6,30},{7,31},{8,16},{9,... | collective-permute-start | bytes 245768 | tf_op jit(solution)/shard_map/ppermute | solution.py:649

commit v2 on v1

--- a/solution.py
+++ b/solution.py
@@ -17,11 +17,13 @@
 SLAB = LANES // HD
 SPANS = WH + 1
 UNIT = 16
+CHAINS = 12
 EPSILON = 1e-05
 LOG2E = math.log2(math.e)
 BF = jnp.bfloat16
 F32 = jnp.float32
 PARAMS = pltpu.CompilerParams(vmem_limit_bytes=24 * 2**20)
+FIRST_PARAMS = pltpu.CompilerParams(vmem_limit_bytes=49 * 2**20)
 
 
 def dot(left, right):
@@ -45,8 +47,12 @@
     return (value[:rows] + value[rows : 2 * rows]) + value[2 * rows :]
 
 
-def bits_of(me_ref, low, size):
-    return lax.shift_right_logical(me_ref[0], low) & ((1 << size) - 1)
+def device_index():
+    return lax.axis_index("lon") * lax.axis_size("lat") + lax.axis_index("lat")
+
+
+def device_bits(low, size):
+    return lax.shift_right_logical(device_index(), low) & ((1 << size) - 1)
 
 
 def odd_lanes(rows):
@@ -54,7 +60,7 @@
     return (lane // WW) % 2 == 1
 
 
-def bias_kernel(me_ref, rel_ref, table_ref, hot_ref, bias_ref, line_ref, span_ref):
+def fill_bias(rel_ref, table_ref, hot_ref, bias_ref, line_ref, span_ref):
     line_ref[...] = rel_ref[...].astype(F32).T
     slot = lax.broadcasted_iota(jnp.int32, (1, LANES), 1) % (2 * WW)
     codes = []
@@ -86,22 +92,6 @@
             bias_ref[h, row * WW : (row + 1) * WW, :] = jnp.where(odd, halves[1], halves[0])
 
 
-def expand_bias(me, rel_index, table):
-    width = SPANS * LANES
-    whole = pl.BlockSpec(memory_space=pltpu.VMEM)
-    return pl.pallas_call(
-        bias_kernel,
-        in_specs=[pl.BlockSpec(memory_space=pltpu.SMEM), whole, whole],
-        out_shape=(
-            jax.ShapeDtypeStruct((table.shape[1], width), BF),
-            jax.ShapeDtypeStruct((H, WIN, WIN), F32),
-        ),
-        scratch_shapes=[pltpu.VMEM((WIN, WIN), F32), pltpu.VMEM((H, width), F32)],
-        compiler_params=PARAMS,
-        name="expand_bias",
-    )(me, rel_index, table)
-
-
 def norm_stats(rows):
     centred = rows - jnp.mean(rows, axis=-1, keepdims=True)
     inv_std = lax.rsqrt(jnp.mean(centred * centred, axis=-1, keepdims=True) + EPSILON)
@@ -121,73 +111,124 @@
     return jnp.where(hit, 1.0, 0.0).astype(BF)
 
 
-def project_kernel(
-    shift_ref, rim_ref, x_ref, d_ref, wq_ref, wp_ref, gain_ref, *rest
-):
-    xw_ref, dw_ref, nt_ref, qkv_ref, dh_ref, norm_ref = rest[-6:]
-    rim = rim_ref is not None
-    count = 1 if rim else x_ref.shape[1] // WW - 1
-    c = x_ref.shape[-1]
+def project_windows(shift_ref, first, count, spans, wq_ref, wp_ref, gain_ref, outs, norm_ref):
+    xw_ref, dw_ref, nt_ref, qkv_ref, dh_ref = outs
+    c = wq_ref.shape[0]
     tokens = count * WIN
     select = shift_matrix(WW - shift_ref[0])
-
-    def spans(ref, n, halo):
-        if rim:
-            return pair_rows(rim_ref[halo], ref[...])
-        return pair_rows(ref[:, n * WW : (n + 1) * WW, :], ref[:, (n + 1) * WW : (n + 2) * WW, :])
-
-    first = 0 if rim else 1
     for n in range(count):
         rows = slice(n * WIN, (n + 1) * WIN)
-        values = dot(select, spans(x_ref, n, 0))
+        values = dot(select, spans(0, n))
         xw_ref[first + n] = values.astype(BF)
         normal, _ = norm_stats(values)
         normed = (normal * gain_ref[...]).astype(BF)
         norm_ref[rows, :] = normed
         nt_ref[:, (first + n) * WIN : (first + n + 1) * WIN] = normed.T
-        dw_ref[first + n] = dot(select, spans(d_ref, n, 1)).astype(BF)
+    yield
+    for n in range(count):
+        dw_ref[first + n] = dot(select, spans(1, n)).astype(BF)
+    yield
     step = 2 * LANES
     for n in range(3 * c // step):
         cols = slice(n * step, (n + 1) * step)
         part = dot(norm_ref[...], wq_ref[:, cols]).astype(BF)
         qkv_ref[first:, :, cols] = part.reshape(count, WIN, step)
+    yield
     grads = dw_ref[first:].reshape(tokens, c)
     for n in range(c // step):
         cols = slice(n * step, (n + 1) * step)
         part = dot_nt(grads, wp_ref[cols, :]).astype(BF)
         dh_ref[first:, :, cols] = part.reshape(count, WIN, step)
-
-
-def project(shift, x, d, w_qkv, w_proj, gain, halo=None, carried=None):
-    c = x.shape[-1]
-    count = x.shape[1] // WW
-    outs = [
+    yield
+
+
+def before_kernel(shift_ref, rel_ref, table_ref, gain_ref, x_hbm, d_hbm, wq_hbm, wp_hbm, *refs):
+    outs, (wq_ref, wp_ref, edge_ref, hot_ref, bias_ref) = refs[:5], refs[5:10]
+    x_ref, d_ref, norm_ref, line_ref, span_ref, sems = refs[10:]
+    pairs = ((x_hbm, x_ref), (d_hbm, d_ref), (wq_hbm, wq_ref), (wp_hbm, wp_ref))
+    copies = [
+        pltpu.make_async_copy(source, target, sems.at[n])
+        for n, (source, target) in enumerate(pairs)
+    ]
+    for copy in copies:
+        copy.start()
+    fill_bias(rel_ref, table_ref, hot_ref, bias_ref, line_ref, span_ref)
+    count = x_ref.shape[1] // WW - 1
+
+    def spans(which, n):
+        ref = (x_ref, d_ref)[which]
+        return pair_rows(ref[:, n * WW : (n + 1) * WW, :], ref[:, (n + 1) * WW : (n + 2) * WW, :])
+
+    stages = project_windows(shift_ref, 1, count, spans, wq_ref, wp_ref, gain_ref, outs, norm_ref)
+    for copy in copies:
+        copy.wait()
+        next(stages)
+    edge_ref[0] = x_ref[:, :WW, :]
+    edge_ref[1] = d_ref[:, :WW, :]
+
+
+def rim_kernel(shift_ref, halo_ref, edge_ref, wq_ref, wp_ref, gain_ref, *refs):
+    def spans(which, n):
+        return pair_rows(halo_ref[which], edge_ref[which])
+
+    for _ in project_windows(
+        shift_ref, 0, 1, spans, wq_ref, wp_ref, gain_ref, refs[-6:-1], refs[-1]
+    ):
+        pass
+
+
+def projected_shapes(count, c):
+    return [
         jax.ShapeDtypeStruct((count, WIN, c), BF),
         jax.ShapeDtypeStruct((count, WIN, c), BF),
         jax.ShapeDtypeStruct((c, count * WIN), BF),
         jax.ShapeDtypeStruct((count, WIN, 3 * c), BF),
         jax.ShapeDtypeStruct((count, WIN, c), BF),
     ]
+
+
+def before(shift, rel_index, table, gain, x, d, w_qkv, w_proj):
+    c = x.shape[-1]
+    count = x.shape[1] // WW
     scalar = pl.BlockSpec(memory_space=pltpu.SMEM)
-    if carried is None:
-        whole = pl.BlockSpec(memory_space=pltpu.VMEM)
-        return pl.pallas_call(
-            lambda shift_ref, *refs: project_kernel(shift_ref, None, *refs),
-            in_specs=[scalar] + [whole] * 5,
-            out_shape=outs,
-            scratch_shapes=[pltpu.VMEM(((count - 1) * WIN, c), BF)],
-            compiler_params=PARAMS,
-            name="project_rest",
-        )(shift, x, d, w_qkv, w_proj, gain)
-    block = pl.BlockSpec((WH, WW, c), lambda w: (0, 0, 0))
+    whole = pl.BlockSpec(memory_space=pltpu.VMEM)
+    far = pl.BlockSpec(memory_space=pltpu.HBM)
+    width = SPANS * LANES
+    return pl.pallas_call(
+        before_kernel,
+        in_specs=[scalar, whole, whole, whole, far, far, far, far],
+        out_shape=[pltpu.VMEM(o.shape, o.dtype) for o in projected_shapes(count, c)]
+        + [
+            pltpu.VMEM(w_qkv.shape, BF),
+            pltpu.VMEM(w_proj.shape, BF),
+            pltpu.VMEM((2, WH, WW, c), BF),
+            pltpu.VMEM((table.shape[1], width), BF),
+            pltpu.VMEM((H, WIN, WIN), F32),
+        ],
+        scratch_shapes=[
+            pltpu.VMEM(x.shape, BF),
+            pltpu.VMEM(d.shape, BF),
+            pltpu.VMEM(((count - 1) * WIN, c), BF),
+            pltpu.VMEM((WIN, WIN), F32),
+            pltpu.VMEM((H, width), F32),
+            pltpu.SemaphoreType.DMA((4,)),
+        ],
+        compiler_params=FIRST_PARAMS,
+        name="before",
+    )(shift, rel_index, table, gain, x, d, w_qkv, w_proj)
+
+
+def project_rim(shift, halo, edge, w_qkv, w_proj, gain, carried):
+    count, _, c = carried[0].shape
 
     def one(array):
         return pl.BlockSpec(array.shape, lambda w: (0,) * array.ndim)
 
     return pl.pallas_call(
-        project_kernel,
+        rim_kernel,
         grid=(1,),
-        in_specs=[scalar, one(halo), block, block, one(w_qkv), one(w_proj), one(gain)]
+        in_specs=[pl.BlockSpec(memory_space=pltpu.SMEM)]
+        + [one(a) for a in (halo, edge, w_qkv, w_proj, gain)]
         + [pl.BlockSpec(memory_space=pl.ANY) for _ in carried],
         out_specs=[
             pl.BlockSpec((1, WIN, c), lambda w: (0, 0, 0)),
@@ -196,12 +237,12 @@
             pl.BlockSpec((1, WIN, 3 * c), lambda w: (0, 0, 0)),
             pl.BlockSpec((1, WIN, c), lambda w: (0, 0, 0)),
         ],
-        out_shape=outs,
+        out_shape=projected_shapes(count, c),
         scratch_shapes=[pltpu.VMEM((WIN, c), BF)],
-        input_output_aliases={7 + n: n for n in range(5)},
+        input_output_aliases={6 + n: n for n in range(5)},
         compiler_params=PARAMS,
         name="project_rim",
-    )(shift, halo, x, d, w_qkv, w_proj, gain, *carried)
+    )(shift, halo, edge, w_qkv, w_proj, gain, *carried)
 
 
 def own_blocks(turned):
@@ -220,27 +261,34 @@
     )
 
 
-def attend_slab(q, k, v, dh, bias_ref, sum_ref, head, first):
+def attend_scores(q, k, v, dh):
+    return dot(k, own_blocks(q.T)), dot(v, own_blocks(dh.T))
+
+
+def attend_soft(scores, d_soft, bias_ref, sum_ref, head, first):
     factor = HD ** (-0.5)
-    k_turned, v_turned = k.T, v.T
-    scores = dot(k, own_blocks(q.T))
-    d_soft = dot(v, own_blocks(dh.T))
-    soft_all, d_all, att, dq = [], [], [], []
+    soft_all, d_all = [], []
     for a in range(SLAB):
         lanes = slice(a * WIN, (a + 1) * WIN)
-        part = slice(a * HD, (a + 1) * HD)
         score = scores[:, lanes] * (factor * LOG2E) + bias_ref[head + first + a]
         raised = jnp.exp2(score - jnp.max(score, axis=0, keepdims=True))
         attention = raised * (1.0 / jnp.sum(raised, axis=0, keepdims=True))
-        soft_low = attention.astype(BF)
+        soft_all.append(attention.astype(BF))
         soft = d_soft[:, lanes]
         d_score = attention * (soft - jnp.sum(attention * soft, axis=0, keepdims=True))
         sum_ref[first + a] += d_score
-        d_low = d_score.astype(BF)
-        soft_all.append(soft_low)
-        d_all.append(d_low)
-        att.append(dot(v_turned[part], soft_low))
-        dq.append(dot(k_turned[part], d_low))
+        d_all.append(d_score.astype(BF))
+    return soft_all, d_all
+
+
+def attend_grads(q, k, v, dh, soft_all, d_all):
+    factor = HD ** (-0.5)
+    k_turned, v_turned = k.T, v.T
+    att, dq = [], []
+    for a in range(SLAB):
+        part = slice(a * HD, (a + 1) * HD)
+        att.append(dot(v_turned[part], soft_all[a]))
+        dq.append(dot(k_turned[part], d_all[a]))
     att = jnp.concatenate(att, axis=0).astype(BF)
     dq = (jnp.concatenate(dq, axis=0) * factor).astype(BF).T
     dk = (dot(jnp.concatenate(d_all, axis=1), own_lanes(q)) * factor).astype(BF)
@@ -272,40 +320,68 @@
     return joined3(dot_nt(split3(jnp.concatenate(spans, axis=1)), hot_ref[...]))
 
 
-def attend_kernel(scales, slabs, base, split, *refs):
-    core_ref, qkv_ref, dh_ref, bias_ref, hot_ref, nt_ref, d_ref = refs[:7]
-    dp_ref, att_ref, sum_ref, row_ref = refs[7], refs[-3], refs[-2], refs[-1]
+def attend_windows(slabs, base, windows, qkv_ref, dh_ref, bias_ref, sum_ref, dp_ref, att_ref):
+    c = dh_ref.shape[-1]
+    wide = slabs * LANES
+    start, stop = windows
+    together = math.gcd(stop - start, max(1, CHAINS // slabs))
+
+    def some(n, carry):
+        pieces, operands = [], []
+        for m in range(together):
+            for s in range(slabs):
+                w = start + n * together + m
+                at = (base + s) * LANES
+                pieces.append((w, s))
+                operands.append(
+                    [qkv_ref[w, :, i * c + at : i * c + at + LANES] for i in range(3)]
+                    + [dh_ref[w, :, at : at + LANES]]
+                )
+        scores = [attend_scores(*o) for o in operands]
+        softs = [
+            attend_soft(*scores[i], bias_ref, sum_ref, base * SLAB, s * SLAB)
+            for i, (_, s) in enumerate(pieces)
+        ]
+        for i, (w, s) in enumerate(pieces):
+            att, dq, dk, dv = attend_grads(*operands[i], *softs[i])
+            lanes = slice(s * LANES, (s + 1) * LANES)
+            att_ref[lanes, pl.ds(pl.multiple_of(w * WIN, WIN), WIN)] = att
+            for k, part in enumerate((dq, dk, dv)):
+                dp_ref[w, :, k * wide + s * LANES : k * wide + (s + 1) * LANES] = part
+        return carry
+
+    lax.fori_loop(0, (stop - start) // together, some, 0)
+
+
+def attend_first_kernel(slabs, base, windows, qkv_ref, dh_ref, bias_ref, dp_ref, att_ref, sum_ref):
+    sum_ref[...] = jnp.zeros_like(sum_ref)
+    attend_windows(slabs, base, windows, qkv_ref, dh_ref, bias_ref, sum_ref, dp_ref, att_ref)
+
+
+def attend_kernel(scales, slabs, base, start, split, *refs):
+    qkv_ref, dh_ref, bias_ref, hot_ref, nt_ref, d_ref = refs[:6]
+    att_ref, sum_ref, row_ref = refs[-3:]
     count, _, c = dh_ref.shape
     heads = slabs * SLAB
-    wide = slabs * LANES
     tokens = count * WIN
-    sum_ref[...] = jnp.zeros_like(sum_ref)
-
-    def window(w, carry):
-        for s in range(slabs):
-            at = (base + s) * LANES
-            att, dq, dk, dv = attend_slab(
-                qkv_ref[w, :, at : at + LANES],
-                qkv_ref[w, :, c + at : c + at + LANES],
-                qkv_ref[w, :, 2 * c + at : 2 * c + at + LANES],
-                dh_ref[w, :, at : at + LANES],
-                bias_ref,
-                sum_ref,
-                base * SLAB,
-                s * SLAB,
-            )
-            lanes = slice(s * LANES, (s + 1) * LANES)
-            att_ref[lanes, pl.ds(pl.multiple_of(w * WIN, WIN), WIN)] = att
-            for n, part in enumerate((dq, dk, dv)):
-                dp_ref[w, :, n * wide + s * LANES : n * wide + (s + 1) * LANES] = part
-        return carry
-
-    lax.fori_loop(0, count, window, 0)
+    if start:
+        dp0_ref, att0_ref, sum0_ref = refs[6:9]
+        refs = refs[3:]
+        sum_ref[...] = sum0_ref[...]
+    else:
+        sum_ref[...] = jnp.zeros_like(sum_ref)
+    dp_ref = refs[6]
+    attend_windows(
+        slabs, base, (start, count), qkv_ref, dh_ref, bias_ref, sum_ref, dp_ref, att_ref
+    )
+    if start:
+        dp_ref[:start] = dp0_ref[...]
+        att_ref[:, : start * WIN] = att0_ref[...]
     grad_scale, table_scale = scales
     table = fold_table(sum_ref, hot_ref, row_ref, heads) * table_scale
     d_rows = d_ref[...].reshape(tokens, c)
     if not split:
-        grad_ref, proj_ref, table_ref = refs[8:11]
+        grad_ref, proj_ref, table_ref = refs[7:10]
         for n in range(3 * slabs):
             cols = slice(n * LANES, (n + 1) * LANES)
             part = dp_ref[:, :, cols].reshape(tokens, LANES)
@@ -313,8 +389,8 @@
         proj_ref[...] = (dot(att_ref[...], d_rows) * grad_scale).astype(BF)
         table_ref[...] = table
         return
-    kept_ref, sent_ref, table_ref, both_ref = refs[8:12]
-    core = bits_of(core_ref, 0, 1)
+    kept_ref, sent_ref, table_ref, both_ref = refs[7:11]
+    core = device_bits(0, 1)
     low = 2 * kept_ref.shape[0]
     top = c // (low * UNIT)
     per_top = 3 * slabs
@@ -339,35 +415,49 @@
                     row : row + UNIT, m * LANES : (m + 1) * LANES
                 ]
     table_ref[...] = jnp.zeros_like(table_ref)
-    rows = slice(base * SLAB, base * SLAB + heads)
     entries = table.shape[1]
-    for n in range(table_ref.shape[0]):
-        lanes = min(LANES, entries - n * LANES)
-        table_ref[n, rows, :lanes] = table[:, n * LANES : n * LANES + lanes]
+    for s in range(slabs):
+        for n in range(UNIT // SLAB):
+            lanes = min(LANES, entries - n * LANES)
+            table_ref[s, n * SLAB : (n + 1) * SLAB, :lanes] = table[
+                s * SLAB : (s + 1) * SLAB, n * LANES : n * LANES + lanes
+            ]
     kept_ref[...] = both_ref[0]
     units = kept_ref.shape[0] * kept_ref.shape[1]
     sent_ref[:units] = both_ref[1].reshape(units, UNIT, LANES)
     sent_ref[units:] = table_ref[...].astype(BF)
 
 
-def attend(base, slabs, qkv, dh, bias, hot, nt, d, scales, core, n_dev):
+def attend_first(base, slabs, stop, qkv, dh, bias):
+    heads = slabs * SLAB
+    wide = heads * HD
+    return pl.pallas_call(
+        lambda *refs: attend_first_kernel(slabs, base, (0, stop), *refs),
+        out_shape=(
+            jax.ShapeDtypeStruct((stop, WIN, 3 * wide), BF),
+            jax.ShapeDtypeStruct((wide, stop * WIN), BF),
+            jax.ShapeDtypeStruct((heads, WIN, WIN), F32),
+        ),
+        compiler_params=PARAMS,
+    )(qkv, dh, bias)
+
+
+def attend(base, slabs, qkv, dh, bias, hot, nt, d, scales, n_dev, split, early=()):
     count, _, c = dh.shape
     heads = slabs * SLAB
     wide = heads * HD
     tokens = count * WIN
     entries = hot.shape[0]
-    split = c // n_dev == UNIT
     outs = [jax.ShapeDtypeStruct((count, WIN, 3 * wide), BF)]
     scratch = []
     if split:
         top = c // LANES
         low = n_dev // top
         units = top * 3 * slabs + slabs * (c // LANES)
-        tables = -(-entries // LANES)
         outs += [
             jax.ShapeDtypeStruct((low // 2, units, UNIT, LANES), BF),
-            jax.ShapeDtypeStruct((low // 2 * units + tables, UNIT, LANES), BF),
-            jax.ShapeDtypeStruct((tables, UNIT, LANES), F32),
+            jax.ShapeDtypeStruct((low // 2 * units + slabs, UNIT, LANES), BF),
+            jax.ShapeDtypeStruct((slabs, UNIT, LANES), F32),
         ]
         scratch = [pltpu.VMEM((2, low // 2, units, UNIT, LANES), BF)]
     else:
@@ -377,9 +467,10 @@
             jax.ShapeDtypeStruct((heads, entries), F32),
         ]
     whole = pl.BlockSpec(memory_space=pltpu.VMEM)
-    return pl.pallas_call(
-        lambda *refs: attend_kernel(scales, slabs, base, split, *refs),
-        in_specs=[pl.BlockSpec(memory_space=pltpu.SMEM)] + [whole] * 6,
+    start = early[0].shape[0] if early else 0
+    return pl.pallas_call(
+        lambda *refs: attend_kernel(scales, slabs, base, start, split, *refs),
+        in_specs=[whole] * (6 + len(early)),
         out_shape=outs,
         scratch_shapes=scratch
         + [
@@ -388,7 +479,7 @@
             pltpu.VMEM((heads, 2 * WH, LANES), F32),
         ],
         compiler_params=PARAMS,
-    )(core, qkv, dh, bias, hot, nt, d)
+    )(qkv, dh, bias, hot, nt, d, *early)
 
 
 def input_rows(dp_refs, windows, x_ref, d_ref, w_ref, gain_ref, store):
@@ -502,11 +593,11 @@
     return (own + parts[0]) + (parts[1] + parts[2])
 
 
-def low_kernel(me_ref, kept_ref, got_ref, table_ref, own_ref, sent1_ref, sent2_ref, sent3_ref, out_ref):
+def low_kernel(kept_ref, got_ref, table_ref, own_ref, sent1_ref, sent2_ref, sent3_ref, out_ref):
     blocks, units = kept_ref.shape[:2]
     table = table_ref[...].astype(BF).astype(F32) + got_ref[blocks * units :].astype(F32)
     out_ref[...] = table
-    mine = bits_of(me_ref, 1, 2)
+    mine = device_bits(1, 2)
     for n, sent_ref in enumerate((None, sent1_ref, sent2_ref, sent3_ref)):
         b = mine ^ n
         total = kept_ref[b].astype(F32) + got_ref[pl.ds(b * units, units)].astype(F32)
@@ -517,14 +608,14 @@
             sent_ref[units:] = table.astype(BF)
 
 
-def low_stage(mine, kept, got, table):
+def low_stage(kept, got, table):
     _, units = kept.shape[:2]
     tables = table.shape[0]
     whole = pl.BlockSpec(memory_space=pltpu.VMEM)
     sent = jax.ShapeDtypeStruct((units + tables, UNIT, LANES), BF)
     return pl.pallas_call(
         low_kernel,
-        in_specs=[pl.BlockSpec(memory_space=pltpu.SMEM)] + [whole] * 3,
+        in_specs=[whole] * 3,
         out_shape=(
             jax.ShapeDtypeStruct((units, UNIT, LANES), F32),
             sent,
@@ -533,87 +624,82 @@
             jax.ShapeDtypeStruct(table.shape, F32),
         ),
         compiler_params=PARAMS,
-    )(mine, kept, got, table)
-
-
-def top_kernel(me_ref, *refs):
-    (own0, table0), got0 = refs[:2], refs[2:5]
-    (own1, table1), got1 = refs[5:7], refs[7:10]
-    own_ref, sent_refs, out_ref, sum0_ref, sum1_ref = refs[10], refs[11:14], refs[14], refs[15], refs[16]
-    table = None
-    for own, gots, sum_ref, part in ((own0, got0, sum0_ref, table0), (own1, got1, sum1_ref, table1)):
-        units = own.shape[0]
-        sum_ref[...] = pair_sum(own[...], [g[:units].astype(F32) for g in gots])
-        part = pair_sum(part[...].astype(BF).astype(F32), [g[units:].astype(F32) for g in gots])
-        table = part if table is None else table + part
+    )(kept, got, table)
+
+
+def top_kernel(base, slabs, own_ref, table_ref, got1, got2, got3, *refs):
+    kept_ref, sent_refs, out_ref, sum_ref = refs[0], refs[1:4], refs[4], refs[5]
+    gots = (got1, got2, got3)
+    units = own_ref.shape[0]
+    sum_ref[...] = pair_sum(own_ref[...], [g[:units].astype(F32) for g in gots])
+    table = pair_sum(table_ref[...].astype(BF).astype(F32), [g[units:].astype(F32) for g in gots])
     out_ref[...] = table
     top = 1 + len(sent_refs)
-    slabs0, slabs1 = (s.shape[0] // (4 * 4) for s in (own0, own1))
-    proj0 = own0.shape[0] - slabs0 * 4
-    proj1 = own1.shape[0] - slabs1 * 4
-    n0, n1 = proj0 // top, proj1 // top
-    mine = bits_of(me_ref, 3, 2)
+    per_top = 3 * slabs
+    tiles = kept_ref.shape[0] - per_top
+    mine = device_bits(3, 2)
     for n in range(top):
         t = mine ^ n
-        target = own_ref if n == 0 else sent_refs[n - 1]
+        target = kept_ref if n == 0 else sent_refs[n - 1]
         kind = F32 if n == 0 else BF
-        target[:n0] = sum0_ref[pl.ds(t * n0, n0)].astype(kind)
-        target[n0 : n0 + n1] = sum1_ref[pl.ds(t * n1, n1)].astype(kind)
-
-        @pl.when(t < slabs0)
-        def _():
-            target[n0 + n1 : n0 + n1 + 4] = sum0_ref[pl.ds(proj0 + t * 4, 4)].astype(kind)
-
-        @pl.when(t >= slabs0)
-        def _():
-            target[n0 + n1 : n0 + n1 + 4] = sum1_ref[pl.ds(proj1 + (t - slabs0) * 4, 4)].astype(kind)
-
+        target[:per_top] = sum_ref[pl.ds(t * per_top, per_top)].astype(kind)
+        here = (t >= base) & (t < base + slabs)
+        slab = jnp.clip(t - base, 0, slabs - 1)
+        proj = sum_ref[pl.ds(top * per_top + slab * tiles, tiles)]
+        target[per_top : per_top + tiles] = jnp.where(here, proj, 0.0).astype(kind)
         if n:
-            target[n0 + n1 + 4 :] = table.astype(BF)
-
-
-def top_stage(mine, first, second):
-    own0, got0, table0 = first
-    own1, got1, table1 = second
-    tables = table0.shape[0]
-    units = (own0.shape[0] + own1.shape[0]) // 4
+            target[per_top + tiles :] = table.astype(BF)
+
+
+def top_stage(base, slabs, tiles, own, table, gots):
+    units = 3 * slabs + tiles
     whole = pl.BlockSpec(memory_space=pltpu.VMEM)
-    sent = jax.ShapeDtypeStruct((units + tables, UNIT, LANES), BF)
-    return pl.pallas_call(
-        top_kernel,
-        in_specs=[pl.BlockSpec(memory_space=pltpu.SMEM)] + [whole] * 10,
+    sent = jax.ShapeDtypeStruct((units + slabs, UNIT, LANES), BF)
+    return pl.pallas_call(
+        lambda *refs: top_kernel(base, slabs, *refs),
+        in_specs=[whole] * 5,
         out_shape=(
             jax.ShapeDtypeStruct((units, UNIT, LANES), F32),
             sent,
             sent,
             sent,
-            jax.ShapeDtypeStruct(table0.shape, F32),
+            jax.ShapeDtypeStruct(table.shape, F32),
         ),
-        scratch_shapes=[pltpu.VMEM(own0.shape, F32), pltpu.VMEM(own1.shape, F32)],
+        scratch_shapes=[pltpu.VMEM(own.shape, F32)],
         compiler_params=PARAMS,
-        name="top_stage",
-    )(mine, own0, table0, *got0, own1, table1, *got1)
-
-
-def finish_kernel(
-    slabs, me_ref, own_ref, table_ref, got1, got2, got3, w_ref, gain_ref, qkv_ref, proj_ref, g_ref, t_ref
-):
-    gots = (got1, got2, got3)
-    units = own_ref.shape[0]
-    total = pair_sum(own_ref[...], [g[:units].astype(F32) for g in gots])
-    table = pair_sum(table_ref[...].astype(BF).astype(F32), [g[units:].astype(F32) for g in gots])
+    )(own, table, *gots)
+
+
+def finish_kernel(slabs, *refs):
+    w_ref, gain_ref, qkv_ref, proj_ref, g_ref, t_ref = refs[-6:]
     c = proj_ref.shape[1]
     tiles = c // LANES
-    unit = 0
-    for base, count in ((0, slabs[0]), (slabs[0], slabs[1])):
+    entries = t_ref.shape[1]
+    base, proj = 0, None
+    for group, count in enumerate(slabs):
+        own_ref, table_ref, *gots = refs[group * 5 : group * 5 + 5]
+        units = own_ref.shape[0]
+        total = pair_sum(own_ref[...], [g[:units].astype(F32) for g in gots])
+        table = pair_sum(
+            table_ref[...].astype(BF).astype(F32), [g[units:].astype(F32) for g in gots]
+        )
         for n in range(3):
             for s in range(count):
                 at = n * c + (base + s) * LANES
-                qkv_ref[:, at : at + LANES] = total[unit]
-                unit += 1
+                qkv_ref[:, at : at + LANES] = total[n * count + s]
+        part = total[3 * count :]
+        proj = part if proj is None else proj + part
+        for s in range(count):
+            rows = slice((base + s) * SLAB, (base + s + 1) * SLAB)
+            for n in range(UNIT // SLAB):
+                lanes = min(LANES, entries - n * LANES)
+                t_ref[rows, n * LANES : n * LANES + lanes] = table[
+                    s, n * SLAB : (n + 1) * SLAB, :lanes
+                ]
+        base += count
     for m in range(tiles):
-        proj_ref[:, m * LANES : (m + 1) * LANES] = total[unit + m]
-    start = pl.multiple_of(me_ref[0] * UNIT, UNIT)
+        proj_ref[:, m * LANES : (m + 1) * LANES] = proj[m]
+    start = pl.multiple_of(device_index() * UNIT, UNIT)
     rows = w_ref[pl.ds(start, UNIT), :].astype(F32)
     products = jnp.sum(rows * qkv_ref[...], axis=1, keepdims=True)
     lane = lax.broadcasted_iota(jnp.int32, (UNIT, c), 1)
@@ -621,18 +707,15 @@
     gains = jnp.where(lane == start + row, gain_ref[...], 0.0)
     column = products / jnp.sum(gains, axis=1, keepdims=True)
     g_ref[...] = jnp.broadcast_to(column, (UNIT, LANES)).T[:1, :]
-    entries = t_ref.shape[1]
-    for n in range(table.shape[0]):
-        lanes = min(LANES, entries - n * LANES)
-        t_ref[:, n * LANES : n * LANES + lanes] = table[n, :, :lanes]
-
-
-def finish(slabs, me, own, table, gots, w_qkv, gain, entries):
+
+
+def finish(slabs, groups, w_qkv, gain, entries):
     c = w_qkv.shape[0]
     whole = pl.BlockSpec(memory_space=pltpu.VMEM)
+    args = [a for own, table, gots in groups for a in (own, table, *gots)]
     return pl.pallas_call(
         lambda *refs: finish_kernel(slabs, *refs),
-        in_specs=[pl.BlockSpec(memory_space=pltpu.SMEM)] + [whole] * 7,
+        in_specs=[whole] * (len(args) + 2),
         out_shape=(
             jax.ShapeDtypeStruct((UNIT, 3 * c), F32),
             jax.ShapeDtypeStruct((UNIT, c), F32),
@@ -641,7 +724,7 @@
         ),
         compiler_params=PARAMS,
         name="finish",
-    )(me, own, table, *gots, w_qkv, gain)
+    )(*args, w_qkv, gain)
 
 
 def flat_permute(value, mask):
@@ -701,44 +784,47 @@
     scales = (tokens ** (-0.5), (tokens // WIN) ** (-0.5))
     entries = bias_table.shape[0]
     gain_row = gain.reshape(1, c)
-    me = (lax.axis_index("lon") * n_lat + lax.axis_index("lat")).astype(jnp.int32).reshape(1)
     split = c // n_dev == UNIT and n_lat == 4
     total = c // LANES
     slabs = (total - 1, 1)
 
     rim = jnp.stack([inputs[:, columns - WW :], d_out[:, columns - WW :]])
     halo = ring_shift(rim, 1)
-    hot, bias = expand_bias(me, rel_index, bias_table.T)
-    carried = project(shifts, inputs, d_out, w_qkv, w_proj, gain_row)
-    x, d, nt, qkv, dh = project(
-        shifts, inputs, d_out, w_qkv, w_proj, gain_row, halo=halo, carried=tuple(carried)
+    *carried, w_qkv, w_proj, edge, hot, bias = before(
+        shifts, rel_index, bias_table.T, gain_row, inputs, d_out, w_qkv, w_proj
     )
+    x, d, nt, qkv, dh = project_rim(shifts, halo, edge, w_qkv, w_proj, gain_row, carried)
 
     def three(values, low):
         return [flat_permute(value, n << low) for n, value in enumerate(values, 1)]
 
-    shared = (qkv, dh, bias, hot, nt, d, scales, me, n_dev)
+    tiles = c // LANES
+    shared = (qkv, dh, bias, hot, nt, d, scales, n_dev, split)
     dp0, *out0 = attend(0, slabs[0], *shared)
     if split:
         got0 = flat_permute(out0[1], 1)
-    dp1, *out1 = attend(slabs[0], slabs[1], *shared)
+    early = attend_first(slabs[0], slabs[1], x.shape[0] // 2, qkv, dh, bias)
+    if split:
+        own0, *sent0, table0 = low_stage(out0[0], got0, out0[2])
+        got0 = three(sent0, 1)
+    dp1, *out1 = attend(slabs[0], slabs[1], *shared, early=early)
     if split:
         got1 = flat_permute(out1[1], 1)
-        own0, *sent0, table0 = low_stage(me, out0[0], got0, out0[2])
-        got0 = three(sent0, 1)
     first = input_rim((dp0, dp1), x, d, w_qkv, gain_row)
     returned = ring_shift(first, -1)
     if split:
-        own1, *sent1, table1 = low_stage(me, out1[0], got1, out1[2])
+        own1, *sent1, table1 = low_stage(out1[0], got1, out1[2])
         got1 = three(sent1, 1)
+        own0, *sent0, table0 = top_stage(0, slabs[0], tiles, own0, table0, got0)
+        got0 = three(sent0, 3)
     grid, end = input_rest(shifts, (dp0, dp1), x, d, w_qkv, gain_row, first)
     if split:
-        own, *sent, table = top_stage(me, (own0, got0, table0), (own1, got1, table1))
-        got = three(sent, 3)
+        own1, *sent1, table1 = top_stage(slabs[0], slabs[1], tiles, own1, table1, got1)
+        got1 = three(sent1, 3)
     d_inputs = place_last(shifts, end, returned, grid)
     if split:
         g_qkv, g_proj, g_gain, g_table = finish(
-            slabs, me, own, table, got, w_qkv, gain_row, entries
+            slabs, ((own0, table0, got0), (own1, table1, got1)), w_qkv, gain_row, entries
         )
         return (d_inputs, g_qkv, g_proj, g_gain.reshape(UNIT), g_table.T)
 
@@ -751,8 +837,9 @@
     g_qkv, g_proj = own[:, : 3 * c], own[:, 3 * c :]
     g_table = full_sum(jnp.concatenate([out0[2], out1[2]], axis=0)).T
     rows = c // n_dev
-    w_rows = lax.dynamic_slice_in_dim(w_qkv, me[0] * rows, rows, 0).astype(F32)
-    gain_rows = lax.dynamic_slice_in_dim(gain, me[0] * rows, rows, 0)
+    me = device_index()
+    w_rows = lax.dynamic_slice_in_dim(w_qkv, me * rows, rows, 0).astype(F32)
+    gain_rows = lax.dynamic_slice_in_dim(gain, me * rows, rows, 0)
     g_gain = jnp.sum(w_rows * g_qkv, axis=1) / gain_rows
     return (d_inputs, g_qkv, g_proj, g_gain, g_table)
 

time: 69 us -> 63.8 us (0.925)
  local copies, waits for them, and re-layouts: 8.17 us -> 1 us
  waiting for transfers between devices: 7.14 us -> 14 us
  Pallas kernels: 31 us -> 27.4 us
  starting transfers between devices: 20.8 us -> 19.8 us
    unnamed x16 -> x2, local copies, waits for them, and re-layouts: 7.17 us -> 0.01 us
    ppermute x11 -> x14, waiting for transfers between devices: 7.13 us -> 11.2 us  [flat_permute(): lax.ppermute(value, ('lon', 'lat'), [(n, n ^ mask) for n in range(total)])]
    pallas_call x9 -> x10, Pallas kernels: 25.7 us -> 22.2 us  [the longest x2 12.8 us: attend(): pl.pallas_call(lambda *refs: attend_kernel(scales, slabs, base, start, sp...]
    ppermute x2, waiting for transfers between devices: 0.01 us -> 2.74 us  [ring_shift(): lax.ppermute(value, 'lon', [(n, (n + steps) % count) for n in range(count)])]
    ppermute x2, starting transfers between devices: 6.66 us -> 4.81 us  [ring_shift(): lax.ppermute(value, 'lon', [(n, (n + steps) % count) for n in range(count)])]
    ppermute x11 -> x14, starting transfers between devices: 14.1 us -> 14.9 us  [flat_permute(): lax.ppermute(value, ('lon', 'lat'), [(n, n ^ mask) for n in range(total)])]
  transfers between devices with their start and end apart: 13 -> 16, of which waited for: 2 -> 3; matrix products, arithmetic and copies ran while one was open for 0% -> 0% of each run, Pallas kernels for 23% -> 24%
where the time goes in v2:
time: 63.8 us; the launch traced here: 63.6 us
  Pallas kernels  27.4 us (43%)
  starting transfers between devices  19.8 us (31%)
  waiting for transfers between devices  14 us (22%)
  between operations  1.43 us (2%)
  local copies, waits for them, and re-layouts  1 us (2%)
    ppermute x14, starting transfers between devices, flat_permute(): lax.ppermute(value, ('lon', 'lat'), [(n, n ^ mask) for n in range(total)])  14.9 us
    pallas_call x2, Pallas kernels, attend(): pl.pallas_call(lambda *refs: attend_kernel(scales, slabs, base, start, sp...  12.8 us
    ppermute x14, waiting for transfers between devices, flat_permute(): lax.ppermute(value, ('lon', 'lat'), [(n, n ^ mask) for n in range(total)])  11.2 us
    pallas_call x1, Pallas kernels, before(): pl.pallas_call(before_kernel, in_specs=[scalar, whole, whole, whole, far,...  5.94 us
    ppermute x2, starting transfers between devices, ring_shift(): lax.ppermute(value, 'lon', [(n, (n + steps) % count) for n in range(count)])  4.81 us
    pallas_call x1, Pallas kernels, input_rest(): pl.pallas_call(input_rest_kernel, in_specs=[pl.BlockSpec(memory_space=plt...  3.64 us
    ppermute x2, waiting for transfers between devices, ring_shift(): lax.ppermute(value, 'lon', [(n, (n + steps) % count) for n in range(count)])  2.74 us
    pallas_call x1, Pallas kernels, attend_first(): pl.pallas_call(lambda *refs: attend_first_kernel(slabs, base, (0, stop),...  1.33 us
  transfers between devices with their start and end apart: 16, of which 3 were waited for; matrix products, arithmetic and copies ran while one was open for 0% of the time, Pallas kernels for 24%

profile of v2, /device:TPU:0, one launch (start us, length us, event | category | flops | bytes accessed | tf_op | source)
XLA Modules:
  0.0 63.6 jit_solution(15514641881628908363)
XLA Ops:
  0.6 1.0 %slice_bitcast_fusion = (bf16[1,8,16,512]{3,2,1,0:T(8,128)(2,1)S(1)}, bf16[1,8,16,512]{3,2,1,0:T(8,128)(2,1)S(1)}) fusion(bf16[8,128,512]{2,1,0:T(8,128)(2,1)} %d_hbm.1, bf16[8,128,512]{2,1,0:T(8,128)(2,1)} %x_hbm.1), kind=kLoop, calls=%fused_computation.1 | loop fusion | bytes 524288 | tf_op jit(solution)/shard_map/stack | solution.py:791
  1.7 3.0 %collective-permute-start = (bf16[2,8,16,512]{3,2,1,0:T(8,128)(2,1)S(1)}, bf16[2,8,16,512]{3,2,1,0:T(8,128)(2,1)S(1)}, u32[]{:S(2)}, u32[]{:S(2)}) collective-permute-start(bf16[2,8,16,512]{3,2,1,0:T(8,128)(2,1)S(1)} %pad_maximum_fusion), channel_id=1, source_target_pairs={{0,4},{4,8},{8,12},{12,16},{16,20},{20,24},{24,28},{28,0},{1,5},{5... | collective-permute-start | bytes 786440 | tf_op jit(solution)/shard_map/ppermute | solution.py:775
  5.4 5.9 %before.1 = (bf16[8,128,512]{2,1,0:T(8,128)(2,1)S(1)}, bf16[8,128,512]{2,1,0:T(8,128)(2,1)S(1)}, bf16[512,1024]{1,0:T(8,128)(2,1)S(1)}, bf16[8,128,1536]{2,1,0:T...) custom-call(s32[1]{0:T(128)S(6)} %copy.25.shift_ref, ...), custom_call_target="tpu_custom_call" | custom-call | tf_op jit(solution)/shard_map/before/pallas_call | solution.py:197
  11.3 2.7 %collective-permute-done.halo_ref = bf16[2,8,16,512]{3,2,1,0:T(8,128)(2,1)S(1)} collective-permute-done((bf16[2,8,16,512]{3,2,1,0:T(8,128)(2,1)S(1)}, bf16[2,8,16,512]{3,2,1,0:T(8,128)(2,1)S(1)}, u32[]{:S(2)}, u32[]{:S(2)}) %collective-permute-start) | collective-permute-done | bytes 262176 | tf_op jit(solution)/shard_map/ppermute | solution.py:775
  14.1 0.9 %project_rim.1 = (bf16[8,128,512]{2,1,0:T(8,128)(2,1)S(1)}, bf16[8,128,512]{2,1,0:T(8,128)(2,1)S(1)}, bf16[512,1024]{1,0:T(8,128)(2,1)S(1)}, bf16[8,128,1536]{2,1,0:T(8,128)(2,1)S(1)}, bf16[8,128,512]{2,1,0:T(8,128)(2,1)S(1)}) custom-call(s32[1]{0:T(128)S(6)} %copy.25.shift_ref, ...), custom_call_target="tpu_custom_call", output_to_operand_aliasing={{0}: (6, {}), {1}: (7, {}), {2}: (8, {}), {3}: (9, {}), {4}... | custom-call | tf_op jit(solution)/shard_map/project_rim/pallas_call | solution.py:227
  14.9 10.3 %shard_map.119 = (bf16[8,128,1152]{2,1,0:T(8,128)(2,1)S(1)}, bf16[4,48,16,128]{3,2,1,0:T(8,128)(2,1)S(1)}, bf16[195,16,128]{2,1,0:T(8,128)(2,1)S(1)}, f32[3,16,128]{2,1,0:T(8,128)S(1)}) custom-call(bf16[8,128,1536]{2,1,0:T(8,128)(2,1)S(1)} %get-tuple-element.65.refs_0_, bf16[8,128,512]{2,1,0:T(8,128)(2,1)S(1)} %get-tuple-element.66.refs_1_, ...), custom_call_target="tpu_custom_call" | custom-call | tf_op jit(solution)/shard_map/pallas_call | solution.py:471
  25.3 1.3 %shard_map.120 = (bf16[4,128,384]{2,1,0:T(8,128)(2,1)S(1)}, bf16[128,512]{1,0:T(8,128)(2,1)S(1)}, f32[4,128,128]{2,1,0:T(8,128)S(1)}) custom-call(bf16[8,128,1536]{2,1,0:T(8,128)(2,1)S(1)} %get-tuple-element.65.refs_0_, bf16[8,128,512]{2,1,0:T(8,128)(2,1)S(1)} %get-tuple-element.66.refs_1_, f32[16,128,128]{2,1,0:T(8,128)S(1)} %get-tuple-element.67.refs_2_), custom_call_target="tpu_custom_call" | custom-call | tf_op jit(solution)/shard_map/pallas_call | solution.py:434
  26.7 2.5 %shard_map.121 = (bf16[8,128,384]{2,1,0:T(8,128)(2,1)S(1)}, bf16[4,16,16,128]{3,2,1,0:T(8,128)(2,1)S(1)}, bf16[65,16,128]{2,1,0:T(8,128)(2,1)S(1)}, f32[1,16,128]{2,1,0:T(8,128)S(1)}) custom-call(bf16[8,128,1536]{2,1,0:T(8,128)(2,1)S(1)} %get-tuple-element.65.refs_0_, bf16[8,128,512]{2,1,0:T(8,128)(2,1)S(1)} %get-tuple-element.66.refs_1_, ...), custom_call_target="tpu_custom_call" | custom-call | tf_op jit(solution)/shard_map/pallas_call | solution.py:471
  29.1 0.6 collective-permute-start.9
  29.9 1.6 %collective-permute-start.3 = (bf16[51,16,128]{2,1,0:T(8,128)(2,1)S(1)}, bf16[51,16,128]{2,1,0:T(8,128)(2,1)S(1)}, u32[]{:S(2)}, u32[]{:S(2)}) collective-permute-start(bf16[51,16,128]{2,1,0:T(8,128)(2,1)S(1)} %get-tuple-element.84), channel_id=1, source_target_pairs={{0,2},{1,3},{2,0},{3,1},{4,6},{5,7},{6,4},{7,5},{8,10},{9,11},{10,... | collective-permute-start | bytes 626696 | tf_op jit(solution)/shard_map/ppermute | solution.py:732
  31.5 2.0 %collective-permute-start.5 = (bf16[51,16,128]{2,1,0:T(8,128)(2,1)S(1)}, bf16[51,16,128]{2,1,0:T(8,128)(2,1)S(1)}, u32[]{:S(2)}, u32[]{:S(2)}) collective-permute-start(bf16[51,16,128]{2,1,0:T(8,128)(2,1)S(1)} %get-tuple-element.86), channel_id=1, source_target_pairs={{0,6},{1,7},{2,4},{3,5},{4,2},{5,3},{6,0},{7,1},{8,14},{9,15},{10,... | collective-permute-start | bytes 626696 | tf_op jit(solution)/shard_map/ppermute | solution.py:732
  33.5 1.6 %collective-permute-start.10 = (bf16[17,16,128]{2,1,0:T(8,128)(2,1)S(1)}, bf16[17,16,128]{2,1,0:T(8,128)(2,1)S(1)}, u32[]{:S(2)}, u32[]{:S(2)}) collective-permute-start(bf16[17,16,128]{2,1,0:T(8,128)(2,1)S(1)} %get-tuple-element.97), channel_id=1, source_target_pairs={{0,2},{1,3},{2,0},{3,1},{4,6},{5,7},{6,4},{7,5},{8,10},{9,11},{10,... | collective-permute-start | bytes 208904 | tf_op jit(solution)/shard_map/ppermute | solution.py:732
  35.1 0.8 %input_rim.1.rim_ref = bf16[128,512]{1,0:T(8,128)(2,1)S(1)} custom-call(bf16[8,128,1152]{2,1,0:T(8,128)(2,1)S(1)} %get-tuple-element.71.dp0_ref, bf16[8,128,384]{2,1,0:T(8,128)(2,1)S(1)} %get-tuple-element.75.dp1_ref, bf16[8,128,512]{2,1,0:T(8,128)(2,1)S(1)} %get-tuple-element.76.x_ref, bf16[8,128,512]{2,1,0:T(8,128)(2,1)S(1)} %get-tuple-element.70.refs_5_.d_ref, ...), custom_call_target="tpu_custom_call" | custom-call | tf_op jit(solution)/shard_map/input_rim/pallas_call | solution.py:545
  35.9 7.2 %collective-permute-done.10.refs_2_ = bf16[17,16,128]{2,1,0:T(8,128)(2,1)S(1)} collective-permute-done((bf16[17,16,128]{2,1,0:T(8,128)(2,1)S(1)}, bf16[17,16,128]{2,1,0:T(8,128)(2,1)S(1)}, u32[]{:S(2)}, u32[]{:S(2)}) %collective-permute-start.10) | collective-permute-done | bytes 69664 | tf_op jit(solution)/shard_map/ppermute | solution.py:732
  43.1 1.8 %collective-permute-start.1 = (bf16[128,512]{1,0:T(8,128)(2,1)S(1)}, bf16[128,512]{1,0:T(8,128)(2,1)S(1)}, u32[]{:S(2)}, u32[]{:S(2)}) collective-permute-start(bf16[128,512]{1,0:T(8,128)(2,1)S(1)} %input_rim.1.rim_ref), channel_id=1, source_target_pairs={{0,28},{4,0},{8,4},{12,8},{16,12},{20,16},{24,20},{28,24},{1,29},{... | collective-permute-start | bytes 393224 | tf_op jit(solution)/shard_map/ppermute | solution.py:775
  44.8 1.2 %collective-permute-start.12 = (bf16[17,16,128]{2,1,0:T(8,128)(2,1)S(1)}, bf16[17,16,128]{2,1,0:T(8,128)(2,1)S(1)}, u32[]{:S(2)}, u32[]{:S(2)}) collective-permute-start(bf16[17,16,128]{2,1,0:T(8,128)(2,1)S(1)} %get-tuple-element.99), channel_id=1, source_target_pairs={{0,6},{1,7},{2,4},{3,5},{4,2},{5,3},{6,0},{7,1},{8,14},{9,15},{10,... | collective-permute-start | bytes 208904 | tf_op jit(solution)/shard_map/ppermute | solution.py:732
  46.0 4.0 %collective-permute-done.12.refs_4_ = bf16[17,16,128]{2,1,0:T(8,128)(2,1)S(1)} collective-permute-done((bf16[17,16,128]{2,1,0:T(8,128)(2,1)S(1)}, bf16[17,16,128]{2,1,0:T(8,128)(2,1)S(1)}, u32[]{:S(2)}, u32[]{:S(2)}) %collective-permute-start.12) | collective-permute-done | bytes 69664 | tf_op jit(solution)/shard_map/ppermute | solution.py:732
  50.4 2.1 %collective-permute-start.6 = (bf16[16,16,128]{2,1,0:T(8,128)(2,1)S(1)}, bf16[16,16,128]{2,1,0:T(8,128)(2,1)S(1)}, u32[]{:S(2)}, u32[]{:S(2)}) collective-permute-start(bf16[16,16,128]{2,1,0:T(8,128)(2,1)S(1)} %get-tuple-element.89), channel_id=1, source_target_pairs={{0,8},{1,9},{2,10},{3,11},{4,12},{5,13},{6,14},{7,15},{8,0},{9,1},... | collective-permute-start | bytes 196616 | tf_op jit(solution)/shard_map/ppermute | solution.py:732
  52.6 2.3 %collective-permute-start.8 = (bf16[16,16,128]{2,1,0:T(8,128)(2,1)S(1)}, bf16[16,16,128]{2,1,0:T(8,128)(2,1)S(1)}, u32[]{:S(2)}, u32[]{:S(2)}) collective-permute-start(bf16[16,16,128]{2,1,0:T(8,128)(2,1)S(1)} %get-tuple-element.91), channel_id=1, source_target_pairs={{0,24},{1,25},{2,26},{3,27},{4,28},{5,29},{6,30},{7,31},{8,16},{9,... | collective-permute-start | bytes 196616 | tf_op jit(solution)/shard_map/ppermute | solution.py:732
  54.9 0.7 %collective-permute-start.14 = (bf16[8,16,128]{2,1,0:T(8,128)(2,1)S(1)}, bf16[8,16,128]{2,1,0:T(8,128)(2,1)S(1)}, u32[]{:S(2)}, u32[]{:S(2)}) collective-permute-start(bf16[8,16,128]{2,1,0:T(8,128)(2,1)S(1)} %get-tuple-element.103), channel_id=1, source_target_pairs={{0,16},{1,17},{2,18},{3,19},{4,20},{5,21},{6,22},{7,23},{8,24},{9,... | collective-permute-start | bytes 98312 | tf_op jit(solution)/shard_map/ppermute | solution.py:732
  55.7 2.7 %collective-permute-start.15 = (bf16[8,16,128]{2,1,0:T(8,128)(2,1)S(1)}, bf16[8,16,128]{2,1,0:T(8,128)(2,1)S(1)}, u32[]{:S(2)}, u32[]{:S(2)}) collective-permute-start(bf16[8,16,128]{2,1,0:T(8,128)(2,1)S(1)} %get-tuple-element.104), channel_id=1, source_target_pairs={{0,24},{1,25},{2,26},{3,27},{4,28},{5,29},{6,30},{7,31},{8,16},{9,... | collective-permute-start | bytes 98312 | tf_op jit(solution)/shard_map/ppermute | solution.py:732
  58.3 3.6 %input_rest.1 = (bf16[8,128,512]{2,1,0:T(8,128)(2,1)}, bf16[128,512]{1,0:T(8,128)(2,1)S(1)}) custom-call(s32[1]{0:T(128)S(6)} %copy.25.shift_ref, bf16[8,128,1152]{2,1,0:T(8,128)(2,1)S(1)} %get-tuple-element.71.dp0_ref, bf16[8,128,384]{2,1,0:T(8,128)(2,1)S(1)} %get-tuple-element.75.dp1_ref, bf16[8,128,512]{2,1,0:T(8,128)(2,1)S(1)} %get-tuple-element.76.x_ref, ...), custom_call_target="tpu_custom_call" | custom-call | tf_op jit(solution)/shard_map/input_rest/pallas_call | solution.py:556
  62.0 0.8 %place_last.1 = bf16[8,128,512]{2,1,0:T(8,128)(2,1)} custom-call(s32[1]{0:T(128)S(6)} %copy.25.shift_ref, bf16[128,512]{1,0:T(8,128)(2,1)S(1)} %get-tuple-element.77.end_ref, bf16[128,512]{1,0:T(8,128)(2,1)S(1)} %collective-permute-done.1.rim_ref, bf16[8,128,512]{2,1,0:T(8,128)(2,1)} %get-tuple-element.78.grid_ref), custom_call_target="tpu_custom_call", output_to_operand_aliasing={{}: (3, {})} | custom-call | tf_op jit(solution)/shard_map/place_last/pallas_call | solution.py:573
  62.9 0.8 %finish.1 = (f32[16,1536]{1,0:T(8,128)}, f32[16,512]{1,0:T(8,128)}, f32[1,16]{1,0:T(1,128)}, f32[16,465]{1,0:T(8,128)}) custom-call(f32[13,16,128]{2,1,0:T(8,128)S(1)} %get-tuple-element.87.refs_0_, f32[3,16,128]{2,1,0:T(8,128)S(1)} %get-tuple-element.88.refs_1_, bf16[16,16,128]{2,1,0:T(8,128)(2,1)S(1)} %collective-permute-done.6.refs_2_, ...), custom_call_target="tpu_custom_call" | custom-call | tf_op jit(solution)/shard_map/finish/pallas_call | solution.py:716
  (25 shorter events, 0.9 us)
Async XLA Ops:
  1.6 12.4 %copy-start = (f32[512]{0:T(512)S(1)}, f32[512]{0:T(512)}, u32[]{:S(2)}) copy-start(f32[512]{0:T(512)} %param.12) | copy-start | bytes 6148
  1.7 12.4 %collective-permute-start = (bf16[2,8,16,512]{3,2,1,0:T(8,128)(2,1)S(1)}, bf16[2,8,16,512]{3,2,1,0:T(8,128)(2,1)S(1)}, u32[]{:S(2)}, u32[]{:S(2)}) collective-permute-start(bf16[2,8,16,512]{3,2,1,0:T(8,128)(2,1)S(1)} %pad_maximum_fusion), channel_id=1, source_target_pairs={{0,4},{4,8},{8,12},{12,16},{16,20},{20,24},{24,28},{28,0},{1,5},{5... | collective-permute-start | bytes 786440 | tf_op jit(solution)/shard_map/ppermute | solution.py:775
  25.2 4.4 %collective-permute-start.2 = (bf16[195,16,128]{2,1,0:T(8,128)(2,1)S(1)}, bf16[195,16,128]{2,1,0:T(8,128)(2,1)S(1)}, u32[]{:S(2)}, u32[]{:S(2)}) collective-permute-start(bf16[195,16,128]{2,1,0:T(8,128)(2,1)S(1)} %get-tuple-element.80), channel_id=1, source_target_pairs={{0,1},{1,0},{2,3},{3,2},{4,5},{5,4},{6,7},{7,6},{8,9},{9,8},{10,11... | collective-permute-start | bytes 2396168 | tf_op jit(solution)/shard_map/ppermute | solution.py:732
  29.1 4.3 %collective-permute-start.9 = (bf16[65,16,128]{2,1,0:T(8,128)(2,1)S(1)}, bf16[65,16,128]{2,1,0:T(8,128)(2,1)S(1)}, u32[]{:S(2)}, u32[]{:S(2)}) collective-permute-start(bf16[65,16,128]{2,1,0:T(8,128)(2,1)S(1)} %get-tuple-element.93), channel_id=1, source_target_pairs={{0,1},{1,0},{2,3},{3,2},{4,5},{5,4},{6,7},{7,6},{8,9},{9,8},{10,11... | collective-permute-start | bytes 798728 | tf_op jit(solution)/shard_map/ppermute | solution.py:732
  29.9 20.3 %collective-permute-start.3 = (bf16[51,16,128]{2,1,0:T(8,128)(2,1)S(1)}, bf16[51,16,128]{2,1,0:T(8,128)(2,1)S(1)}, u32[]{:S(2)}, u32[]{:S(2)}) collective-permute-start(bf16[51,16,128]{2,1,0:T(8,128)(2,1)S(1)} %get-tuple-element.84), channel_id=1, source_target_pairs={{0,2},{1,3},{2,0},{3,1},{4,6},{5,7},{6,4},{7,5},{8,10},{9,11},{10,... | collective-permute-start | bytes 626696 | tf_op jit(solution)/shard_map/ppermute | solution.py:732
  31.5 18.7 %collective-permute-start.4 = (bf16[51,16,128]{2,1,0:T(8,128)(2,1)S(1)}, bf16[51,16,128]{2,1,0:T(8,128)(2,1)S(1)}, u32[]{:S(2)}, u32[]{:S(2)}) collective-permute-start(bf16[51,16,128]{2,1,0:T(8,128)(2,1)S(1)} %get-tuple-element.85), channel_id=1, source_target_pairs={{0,4},{1,5},{2,6},{3,7},{4,0},{5,1},{6,2},{7,3},{8,12},{9,13},{10,... | collective-permute-start | bytes 626696 | tf_op jit(solution)/shard_map/ppermute | solution.py:732
  31.5 18.7 %collective-permute-start.5 = (bf16[51,16,128]{2,1,0:T(8,128)(2,1)S(1)}, bf16[51,16,128]{2,1,0:T(8,128)(2,1)S(1)}, u32[]{:S(2)}, u32[]{:S(2)}) collective-permute-start(bf16[51,16,128]{2,1,0:T(8,128)(2,1)S(1)} %get-tuple-element.86), channel_id=1, source_target_pairs={{0,6},{1,7},{2,4},{3,5},{4,2},{5,3},{6,0},{7,1},{8,14},{9,15},{10,... | collective-permute-start | bytes 626696 | tf_op jit(solution)/shard_map/ppermute | solution.py:732
  33.5 9.6 %collective-permute-start.10 = (bf16[17,16,128]{2,1,0:T(8,128)(2,1)S(1)}, bf16[17,16,128]{2,1,0:T(8,128)(2,1)S(1)}, u32[]{:S(2)}, u32[]{:S(2)}) collective-permute-start(bf16[17,16,128]{2,1,0:T(8,128)(2,1)S(1)} %get-tuple-element.97), channel_id=1, source_target_pairs={{0,2},{1,3},{2,0},{3,1},{4,6},{5,7},{6,4},{7,5},{8,10},{9,11},{10,... | collective-permute-start | bytes 208904 | tf_op jit(solution)/shard_map/ppermute | solution.py:732
  35.1 9.7 %collective-permute-start.11 = (bf16[17,16,128]{2,1,0:T(8,128)(2,1)S(1)}, bf16[17,16,128]{2,1,0:T(8,128)(2,1)S(1)}, u32[]{:S(2)}, u32[]{:S(2)}) collective-permute-start(bf16[17,16,128]{2,1,0:T(8,128)(2,1)S(1)} %get-tuple-element.98), channel_id=1, source_target_pairs={{0,4},{1,5},{2,6},{3,7},{4,0},{5,1},{6,2},{7,3},{8,12},{9,13},{10,... | collective-permute-start | bytes 208904 | tf_op jit(solution)/shard_map/ppermute | solution.py:732
  43.1 11.9 %collective-permute-start.1 = (bf16[128,512]{1,0:T(8,128)(2,1)S(1)}, bf16[128,512]{1,0:T(8,128)(2,1)S(1)}, u32[]{:S(2)}, u32[]{:S(2)}) collective-permute-start(bf16[128,512]{1,0:T(8,128)(2,1)S(1)} %input_rim.1.rim_ref), channel_id=1, source_target_pairs={{0,28},{4,0},{8,4},{12,8},{16,12},{20,16},{24,20},{28,24},{1,29},{... | collective-permute-start | bytes 393224 | tf_op jit(solution)/shard_map/ppermute | solution.py:775
  44.8 5.2 %collective-permute-start.12 = (bf16[17,16,128]{2,1,0:T(8,128)(2,1)S(1)}, bf16[17,16,128]{2,1,0:T(8,128)(2,1)S(1)}, u32[]{:S(2)}, u32[]{:S(2)}) collective-permute-start(bf16[17,16,128]{2,1,0:T(8,128)(2,1)S(1)} %get-tuple-element.99), channel_id=1, source_target_pairs={{0,6},{1,7},{2,4},{3,5},{4,2},{5,3},{6,0},{7,1},{8,14},{9,15},{10,... | collective-permute-start | bytes 208904 | tf_op jit(solution)/shard_map/ppermute | solution.py:732
  50.1 5.6 %collective-permute-start.13 = (bf16[8,16,128]{2,1,0:T(8,128)(2,1)S(1)}, bf16[8,16,128]{2,1,0:T(8,128)(2,1)S(1)}, u32[]{:S(2)}, u32[]{:S(2)}) collective-permute-start(bf16[8,16,128]{2,1,0:T(8,128)(2,1)S(1)} %get-tuple-element.102), channel_id=1, source_target_pairs={{0,8},{1,9},{2,10},{3,11},{4,12},{5,13},{6,14},{7,15},{8,0},{9,1},... | collective-permute-start | bytes 98312 | tf_op jit(solution)/shard_map/ppermute | solution.py:732
  50.4 12.4 %collective-permute-start.6 = (bf16[16,16,128]{2,1,0:T(8,128)(2,1)S(1)}, bf16[16,16,128]{2,1,0:T(8,128)(2,1)S(1)}, u32[]{:S(2)}, u32[]{:S(2)}) collective-permute-start(bf16[16,16,128]{2,1,0:T(8,128)(2,1)S(1)} %get-tuple-element.89), channel_id=1, source_target_pairs={{0,8},{1,9},{2,10},{3,11},{4,12},{5,13},{6,14},{7,15},{8,0},{9,1},... | collective-permute-start | bytes 196616 | tf_op jit(solution)/shard_map/ppermute | solution.py:732
  52.5 10.4 %collective-permute-start.7 = (bf16[16,16,128]{2,1,0:T(8,128)(2,1)S(1)}, bf16[16,16,128]{2,1,0:T(8,128)(2,1)S(1)}, u32[]{:S(2)}, u32[]{:S(2)}) collective-permute-start(bf16[16,16,128]{2,1,0:T(8,128)(2,1)S(1)} %get-tuple-element.90), channel_id=1, source_target_pairs={{0,16},{1,17},{2,18},{3,19},{4,20},{5,21},{6,22},{7,23},{8,24},{9,... | collective-permute-start | bytes 196616 | tf_op jit(solution)/shard_map/ppermute | solution.py:732
  52.6 10.2 %collective-permute-start.8 = (bf16[16,16,128]{2,1,0:T(8,128)(2,1)S(1)}, bf16[16,16,128]{2,1,0:T(8,128)(2,1)S(1)}, u32[]{:S(2)}, u32[]{:S(2)}) collective-permute-start(bf16[16,16,128]{2,1,0:T(8,128)(2,1)S(1)} %get-tuple-element.91), channel_id=1, source_target_pairs={{0,24},{1,25},{2,26},{3,27},{4,28},{5,29},{6,30},{7,31},{8,16},{9,... | collective-permute-start | bytes 196616 | tf_op jit(solution)/shard_map/ppermute | solution.py:732
  54.9 7.9 %collective-permute-start.14 = (bf16[8,16,128]{2,1,0:T(8,128)(2,1)S(1)}, bf16[8,16,128]{2,1,0:T(8,128)(2,1)S(1)}, u32[]{:S(2)}, u32[]{:S(2)}) collective-permute-start(bf16[8,16,128]{2,1,0:T(8,128)(2,1)S(1)} %get-tuple-element.103), channel_id=1, source_target_pairs={{0,16},{1,17},{2,18},{3,19},{4,20},{5,21},{6,22},{7,23},{8,24},{9,... | collective-permute-start | bytes 98312 | tf_op jit(solution)/shard_map/ppermute | solution.py:732
  55.7 7.2 %collective-permute-start.15 = (bf16[8,16,128]{2,1,0:T(8,128)(2,1)S(1)}, bf16[8,16,128]{2,1,0:T(8,128)(2,1)S(1)}, u32[]{:S(2)}, u32[]{:S(2)}) collective-permute-start(bf16[8,16,128]{2,1,0:T(8,128)(2,1)S(1)} %get-tuple-element.104), channel_id=1, source_target_pairs={{0,24},{1,25},{2,26},{3,27},{4,28},{5,29},{6,30},{7,31},{8,16},{9,... | collective-permute-start | bytes 98312 | tf_op jit(solution)/shard_map/ppermute | solution.py:732

commit v3 on v2

--- a/solution.py
+++ b/solution.py
@@ -17,7 +17,9 @@
 SLAB = LANES // HD
 SPANS = WH + 1
 UNIT = 16
-CHAINS = 12
+PIECES = 1
+EARLY = 2
+CHAINS = 16
 EPSILON = 1e-05
 LOG2E = math.log2(math.e)
 BF = jnp.bfloat16
@@ -143,15 +145,22 @@
 
 
 def before_kernel(shift_ref, rel_ref, table_ref, gain_ref, x_hbm, d_hbm, wq_hbm, wp_hbm, *refs):
-    outs, (wq_ref, wp_ref, edge_ref, hot_ref, bias_ref) = refs[:5], refs[5:10]
-    x_ref, d_ref, norm_ref, line_ref, span_ref, sems = refs[10:]
+    outs, (wq_ref, wp_ref, edge_ref, last_ref, hot_ref, bias_ref) = refs[:5], refs[5:11]
+    x_ref, d_ref, norm_ref, line_ref, span_ref, sems = refs[11:]
     pairs = ((x_hbm, x_ref), (d_hbm, d_ref), (wq_hbm, wq_ref), (wp_hbm, wp_ref))
-    copies = [
-        pltpu.make_async_copy(source, target, sems.at[n])
-        for n, (source, target) in enumerate(pairs)
-    ]
-    for copy in copies:
-        copy.start()
+    copies = []
+    for n, (source, target) in enumerate(pairs):
+        rows = source.shape[0] // PIECES
+        parts = [pl.ds(m * rows, rows) for m in range(PIECES)]
+        copies.append(
+            [
+                pltpu.make_async_copy(source.at[part], target.at[part], sems.at[n, m])
+                for m, part in enumerate(parts)
+            ]
+        )
+    for group in copies:
+        for copy in group:
+            copy.start()
     fill_bias(rel_ref, table_ref, hot_ref, bias_ref, line_ref, span_ref)
     count = x_ref.shape[1] // WW - 1
 
@@ -160,11 +169,13 @@
         return pair_rows(ref[:, n * WW : (n + 1) * WW, :], ref[:, (n + 1) * WW : (n + 2) * WW, :])
 
     stages = project_windows(shift_ref, 1, count, spans, wq_ref, wp_ref, gain_ref, outs, norm_ref)
-    for copy in copies:
-        copy.wait()
+    for group in copies:
+        for copy in group:
+            copy.wait()
         next(stages)
-    edge_ref[0] = x_ref[:, :WW, :]
-    edge_ref[1] = d_ref[:, :WW, :]
+    for n, ref in enumerate((x_ref, d_ref)):
+        edge_ref[n] = ref[:, :WW, :]
+        last_ref[n] = ref[:, count * WW :, :]
 
 
 def rim_kernel(shift_ref, halo_ref, edge_ref, wq_ref, wp_ref, gain_ref, *refs):
@@ -202,6 +213,7 @@
             pltpu.VMEM(w_qkv.shape, BF),
             pltpu.VMEM(w_proj.shape, BF),
             pltpu.VMEM((2, WH, WW, c), BF),
+            pltpu.VMEM((2, WH, WW, c), BF),
             pltpu.VMEM((table.shape[1], width), BF),
             pltpu.VMEM((H, WIN, WIN), F32),
         ],
@@ -211,14 +223,14 @@
             pltpu.VMEM(((count - 1) * WIN, c), BF),
             pltpu.VMEM((WIN, WIN), F32),
             pltpu.VMEM((H, width), F32),
-            pltpu.SemaphoreType.DMA((4,)),
+            pltpu.SemaphoreType.DMA((4, PIECES)),
         ],
         compiler_params=FIRST_PARAMS,
         name="before",
     )(shift, rel_index, table, gain, x, d, w_qkv, w_proj)
 
 
-def project_rim(shift, halo, edge, w_qkv, w_proj, gain, carried):
+def project_rim(shift, halo, edge, w_qkv, w_proj, gain, after, carried):
     count, _, c = carried[0].shape
 
     def one(array):
@@ -229,7 +241,7 @@
         grid=(1,),
         in_specs=[pl.BlockSpec(memory_space=pltpu.SMEM)]
         + [one(a) for a in (halo, edge, w_qkv, w_proj, gain)]
-        + [pl.BlockSpec(memory_space=pl.ANY) for _ in carried],
+        + [pl.BlockSpec(memory_space=pl.ANY) for _ in (after, *carried)],
         out_specs=[
             pl.BlockSpec((1, WIN, c), lambda w: (0, 0, 0)),
             pl.BlockSpec((1, WIN, c), lambda w: (0, 0, 0)),
@@ -239,10 +251,10 @@
         ],
         out_shape=projected_shapes(count, c),
         scratch_shapes=[pltpu.VMEM((WIN, c), BF)],
-        input_output_aliases={6 + n: n for n in range(5)},
+        input_output_aliases={7 + n: n for n in range(5)},
         compiler_params=PARAMS,
         name="project_rim",
-    )(shift, halo, edge, w_qkv, w_proj, gain, *carried)
+    )(shift, halo, edge, w_qkv, w_proj, gain, after, *carried)
 
 
 def own_blocks(turned):
@@ -265,12 +277,12 @@
     return dot(k, own_blocks(q.T)), dot(v, own_blocks(dh.T))
 
 
-def attend_soft(scores, d_soft, bias_ref, sum_ref, head, first):
+def attend_soft(scores, d_soft, bias_ref, sum_ref, first):
     factor = HD ** (-0.5)
     soft_all, d_all = [], []
     for a in range(SLAB):
         lanes = slice(a * WIN, (a + 1) * WIN)
-        score = scores[:, lanes] * (factor * LOG2E) + bias_ref[head + first + a]
+        score = scores[:, lanes] * (factor * LOG2E) + bias_ref[first + a]
         raised = jnp.exp2(score - jnp.max(score, axis=0, keepdims=True))
         attention = raised * (1.0 / jnp.sum(raised, axis=0, keepdims=True))
         soft_all.append(attention.astype(BF))
@@ -320,9 +332,9 @@
     return joined3(dot_nt(split3(jnp.concatenate(spans, axis=1)), hot_ref[...]))
 
 
-def attend_windows(slabs, base, windows, qkv_ref, dh_ref, bias_ref, sum_ref, dp_ref, att_ref):
+def attend_windows(windows, origin, qkv_ref, dh_ref, bias_ref, sum_ref, dp_ref, att_ref):
     c = dh_ref.shape[-1]
-    wide = slabs * LANES
+    slabs = c // LANES
     start, stop = windows
     together = math.gcd(stop - start, max(1, CHAINS // slabs))
 
@@ -331,7 +343,7 @@
         for m in range(together):
             for s in range(slabs):
                 w = start + n * together + m
-                at = (base + s) * LANES
+                at = s * LANES
                 pieces.append((w, s))
                 operands.append(
                     [qkv_ref[w, :, i * c + at : i * c + at + LANES] for i in range(3)]
@@ -339,44 +351,57 @@
                 )
         scores = [attend_scores(*o) for o in operands]
         softs = [
-            attend_soft(*scores[i], bias_ref, sum_ref, base * SLAB, s * SLAB)
+            attend_soft(*scores[i], bias_ref, sum_ref, s * SLAB)
             for i, (_, s) in enumerate(pieces)
         ]
         for i, (w, s) in enumerate(pieces):
             att, dq, dk, dv = attend_grads(*operands[i], *softs[i])
             lanes = slice(s * LANES, (s + 1) * LANES)
-            att_ref[lanes, pl.ds(pl.multiple_of(w * WIN, WIN), WIN)] = att
+            tokens = pl.ds(pl.multiple_of((w - origin) * WIN, WIN), WIN)
+            att_ref[lanes, tokens] = att
             for k, part in enumerate((dq, dk, dv)):
-                dp_ref[w, :, k * wide + s * LANES : k * wide + (s + 1) * LANES] = part
+                dp_ref[w - origin, :, k * c + s * LANES : k * c + (s + 1) * LANES] = part
         return carry
 
     lax.fori_loop(0, (stop - start) // together, some, 0)
 
 
-def attend_first_kernel(slabs, base, windows, qkv_ref, dh_ref, bias_ref, dp_ref, att_ref, sum_ref):
+def attend_first_kernel(start, qkv_ref, dh_ref, bias_ref, dp_ref, att_ref, sum_ref):
     sum_ref[...] = jnp.zeros_like(sum_ref)
-    attend_windows(slabs, base, windows, qkv_ref, dh_ref, bias_ref, sum_ref, dp_ref, att_ref)
-
-
-def attend_kernel(scales, slabs, base, start, split, *refs):
-    qkv_ref, dh_ref, bias_ref, hot_ref, nt_ref, d_ref = refs[:6]
+    windows = (start, dh_ref.shape[0])
+    attend_windows(windows, start, qkv_ref, dh_ref, bias_ref, sum_ref, dp_ref, att_ref)
+
+
+def attend_first(start, qkv, dh, bias):
+    count, _, c = dh.shape
+    whole = pl.BlockSpec(memory_space=pltpu.VMEM)
+    return pl.pallas_call(
+        lambda *refs: attend_first_kernel(start, *refs),
+        in_specs=[whole] * 3,
+        out_shape=(
+            jax.ShapeDtypeStruct((count - start, WIN, 3 * c), BF),
+            jax.ShapeDtypeStruct((c, (count - start) * WIN), BF),
+            jax.ShapeDtypeStruct(bias.shape, F32),
+        ),
+        compiler_params=PARAMS,
+        name="attend_first",
+    )(qkv, dh, bias)
+
+
+def attend_kernel(scales, split, *refs):
+    qkv_ref, dh_ref, bias_ref, hot_ref, nt_ref, d_ref, dp0_ref, att0_ref, sum0_ref = refs[:9]
+    refs = refs[3:]
+    dp_ref = refs[6]
     att_ref, sum_ref, row_ref = refs[-3:]
     count, _, c = dh_ref.shape
+    slabs = c // LANES
     heads = slabs * SLAB
     tokens = count * WIN
-    if start:
-        dp0_ref, att0_ref, sum0_ref = refs[6:9]
-        refs = refs[3:]
-        sum_ref[...] = sum0_ref[...]
-    else:
-        sum_ref[...] = jnp.zeros_like(sum_ref)
-    dp_ref = refs[6]
-    attend_windows(
-        slabs, base, (start, count), qkv_ref, dh_ref, bias_ref, sum_ref, dp_ref, att_ref
-    )
-    if start:
-        dp_ref[:start] = dp0_ref[...]
-        att_ref[:, : start * WIN] = att0_ref[...]
+    start = count - dp0_ref.shape[0]
+    sum_ref[...] = sum0_ref[...]
+    attend_windows((0, start), 0, qkv_ref, dh_ref, bias_ref, sum_ref, dp_ref, att_ref)
+    dp_ref[start:] = dp0_ref[...]
+    att_ref[:, start * WIN :] = att0_ref[...]
     grad_scale, table_scale = scales
     table = fold_table(sum_ref, hot_ref, row_ref, heads) * table_scale
     d_rows = d_ref[...].reshape(tokens, c)
@@ -428,32 +453,17 @@
     sent_ref[units:] = table_ref[...].astype(BF)
 
 
-def attend_first(base, slabs, stop, qkv, dh, bias):
+def attend(qkv, dh, bias, hot, nt, d, early, scales, n_dev, split):
+    count, _, c = dh.shape
+    slabs = c // LANES
     heads = slabs * SLAB
-    wide = heads * HD
-    return pl.pallas_call(
-        lambda *refs: attend_first_kernel(slabs, base, (0, stop), *refs),
-        out_shape=(
-            jax.ShapeDtypeStruct((stop, WIN, 3 * wide), BF),
-            jax.ShapeDtypeStruct((wide, stop * WIN), BF),
-            jax.ShapeDtypeStruct((heads, WIN, WIN), F32),
-        ),
-        compiler_params=PARAMS,
-    )(qkv, dh, bias)
-
-
-def attend(base, slabs, qkv, dh, bias, hot, nt, d, scales, n_dev, split, early=()):
-    count, _, c = dh.shape
-    heads = slabs * SLAB
-    wide = heads * HD
     tokens = count * WIN
     entries = hot.shape[0]
-    outs = [jax.ShapeDtypeStruct((count, WIN, 3 * wide), BF)]
+    outs = [jax.ShapeDtypeStruct((count, WIN, 3 * c), BF)]
     scratch = []
     if split:
-        top = c // LANES
-        low = n_dev // top
-        units = top * 3 * slabs + slabs * (c // LANES)
+        low = n_dev // slabs
+        units = slabs * 4 * slabs
         outs += [
             jax.ShapeDtypeStruct((low // 2, units, UNIT, LANES), BF),
             jax.ShapeDtypeStruct((low // 2 * units + slabs, UNIT, LANES), BF),
@@ -462,37 +472,33 @@
         scratch = [pltpu.VMEM((2, low // 2, units, UNIT, LANES), BF)]
     else:
         outs += [
-            jax.ShapeDtypeStruct((c, 3 * wide), BF),
-            jax.ShapeDtypeStruct((wide, c), BF),
+            jax.ShapeDtypeStruct((c, 3 * c), BF),
+            jax.ShapeDtypeStruct((c, c), BF),
             jax.ShapeDtypeStruct((heads, entries), F32),
         ]
     whole = pl.BlockSpec(memory_space=pltpu.VMEM)
-    start = early[0].shape[0] if early else 0
     return pl.pallas_call(
-        lambda *refs: attend_kernel(scales, slabs, base, start, split, *refs),
-        in_specs=[whole] * (6 + len(early)),
+        lambda *refs: attend_kernel(scales, split, *refs),
+        in_specs=[whole] * 9,
         out_shape=outs,
         scratch_shapes=scratch
         + [
-            pltpu.VMEM((wide, tokens), BF),
+            pltpu.VMEM((c, tokens), BF),
             pltpu.VMEM((heads, WIN, WIN), F32),
             pltpu.VMEM((heads, 2 * WH, LANES), F32),
         ],
         compiler_params=PARAMS,
+        name="attend",
     )(qkv, dh, bias, hot, nt, d, *early)
 
 
-def input_rows(dp_refs, windows, x_ref, d_ref, w_ref, gain_ref, store):
+def input_rows(dp_ref, windows, x_ref, d_ref, w_ref, gain_ref, store):
     c = x_ref.shape[-1]
     start, stop = windows
     d_normed = None
     for n in range(3):
-        parts = []
-        for dp_ref in dp_refs:
-            wide = dp_ref.shape[-1] // 3
-            part = dp_ref[start:stop, :, n * wide : (n + 1) * wide]
-            parts.append(part.reshape((stop - start) * WIN, wide))
-        part = dot_nt(jnp.concatenate(parts, axis=1), w_ref[:, n * c : (n + 1) * c])
+        part = dp_ref[start:stop, :, n * c : (n + 1) * c].reshape((stop - start) * WIN, c)
+        part = dot_nt(part, w_ref[:, n * c : (n + 1) * c])
         d_normed = part if d_normed is None else d_normed + part
     for w in range(start, stop):
         grad = d_normed[(w - start) * WIN : (w - start + 1) * WIN]
@@ -506,11 +512,11 @@
         store(w, (d_ref[w].astype(F32) + branch).astype(BF))
 
 
-def input_rim_kernel(dp0_ref, dp1_ref, x_ref, d_ref, w_ref, gain_ref, out_ref):
+def input_rim_kernel(dp_ref, x_ref, d_ref, w_ref, gain_ref, out_ref):
     def store(w, value):
         out_ref[...] = value
 
-    input_rows((dp0_ref, dp1_ref), (0, 1), x_ref, d_ref, w_ref, gain_ref, store)
+    input_rows(dp_ref, (0, 1), x_ref, d_ref, w_ref, gain_ref, store)
 
 
 def placed(select, first, second):
@@ -520,7 +526,7 @@
 
 
 def input_rest_kernel(
-    shift_ref, dp0_ref, dp1_ref, x_ref, d_ref, w_ref, gain_ref, rim_ref, out_ref, end_ref, row_ref
+    shift_ref, dp_ref, x_ref, d_ref, w_ref, gain_ref, rim_ref, out_ref, end_ref, row_ref
 ):
     count = x_ref.shape[0]
     select = shift_matrix(shift_ref[0])
@@ -531,7 +537,7 @@
 
     half = (count + 1) // 2
     for windows in ((1, half), (half, count)):
-        input_rows((dp0_ref, dp1_ref), windows, x_ref, d_ref, w_ref, gain_ref, store)
+        input_rows(dp_ref, windows, x_ref, d_ref, w_ref, gain_ref, store)
         for w in range(windows[0], windows[1]):
             out_ref[:, (w - 1) * WW : w * WW, :] = placed(select, row_ref[w - 1], row_ref[w])
     end_ref[...] = row_ref[count - 1]
@@ -541,21 +547,21 @@
     out_ref[...] = placed(shift_matrix(shift_ref[0]), end_ref[...], rim_ref[...])
 
 
-def input_rim(dps, x, d, w_qkv, gain):
+def input_rim(dp, x, d, w_qkv, gain):
     return pl.pallas_call(
         input_rim_kernel,
         out_shape=jax.ShapeDtypeStruct(x.shape[1:], BF),
         compiler_params=PARAMS,
         name="input_rim",
-    )(*dps, x, d, w_qkv, gain)
-
-
-def input_rest(shift, dps, x, d, w_qkv, gain, rim):
+    )(dp, x, d, w_qkv, gain)
+
+
+def input_rest(shift, dp, x, d, w_qkv, gain, rim):
     count, _, c = x.shape
     whole = pl.BlockSpec(memory_space=pltpu.VMEM)
     return pl.pallas_call(
         input_rest_kernel,
-        in_specs=[pl.BlockSpec(memory_space=pltpu.SMEM)] + [whole] * 7,
+        in_specs=[pl.BlockSpec(memory_space=pltpu.SMEM)] + [whole] * 6,
         out_shape=(
             jax.ShapeDtypeStruct((WH, count * WW, c), BF),
             jax.ShapeDtypeStruct((WIN, c), BF),
@@ -563,7 +569,7 @@
         scratch_shapes=[pltpu.VMEM((count, WIN, c), BF)],
         compiler_params=PARAMS,
         name="input_rest",
-    )(shift, *dps, x, d, w_qkv, gain, rim)
+    )(shift, dp, x, d, w_qkv, gain, rim)
 
 
 def place_last(shift, end, rim, grid):
@@ -593,112 +599,128 @@
     return (own + parts[0]) + (parts[1] + parts[2])
 
 
-def low_kernel(kept_ref, got_ref, table_ref, own_ref, sent1_ref, sent2_ref, sent3_ref, out_ref):
-    blocks, units = kept_ref.shape[:2]
-    table = table_ref[...].astype(BF).astype(F32) + got_ref[blocks * units :].astype(F32)
+def shape_of(*shape, kind=BF):
+    return jax.ShapeDtypeStruct((*shape, UNIT, LANES), kind)
+
+
+def stage_call(kernel, outs, *args, scratch=()):
+    whole = pl.BlockSpec(memory_space=pltpu.VMEM)
+    return pl.pallas_call(
+        kernel,
+        in_specs=[whole] * len(args),
+        out_shape=outs,
+        scratch_shapes=scratch,
+        compiler_params=PARAMS,
+    )(*args)
+
+
+def core_kernel(kept_ref, got_ref, table_ref, own_a, sent_a, own_b, sent_b, out_ref):
+    units = kept_ref.shape[1]
+    half = units // 2
+    table = table_ref[...].astype(BF).astype(F32) + got_ref[4 * units :].astype(F32)
     out_ref[...] = table
-    mine = device_bits(1, 2)
-    for n, sent_ref in enumerate((None, sent1_ref, sent2_ref, sent3_ref)):
-        b = mine ^ n
-        total = kept_ref[b].astype(F32) + got_ref[pl.ds(b * units, units)].astype(F32)
-        if n == 0:
-            own_ref[...] = total
-        else:
-            sent_ref[:units] = total.astype(BF)
-            sent_ref[units:] = table.astype(BF)
-
-
-def low_stage(kept, got, table):
-    _, units = kept.shape[:2]
-    tables = table.shape[0]
-    whole = pl.BlockSpec(memory_space=pltpu.VMEM)
-    sent = jax.ShapeDtypeStruct((units + tables, UNIT, LANES), BF)
-    return pl.pallas_call(
-        low_kernel,
-        in_specs=[whole] * 3,
-        out_shape=(
-            jax.ShapeDtypeStruct((units, UNIT, LANES), F32),
-            sent,
-            sent,
-            sent,
-            jax.ShapeDtypeStruct(table.shape, F32),
-        ),
-        compiler_params=PARAMS,
-    )(kept, got, table)
-
-
-def top_kernel(base, slabs, own_ref, table_ref, got1, got2, got3, *refs):
-    kept_ref, sent_refs, out_ref, sum_ref = refs[0], refs[1:4], refs[4], refs[5]
+    x, y = device_bits(1, 1), device_bits(2, 1)
+
+    def total(y, x, start):
+        b = 2 * y + x
+        got = got_ref[pl.ds(b * units + start, half)]
+        return kept_ref[b, start : start + half].astype(F32) + got.astype(F32)
+
+    for n in range(2):
+        own_a[n] = total(n, x, 0)
+        sent_a[n * half : (n + 1) * half] = total(n, 1 - x, 0).astype(BF)
+        own_b[n] = total(y, n, half)
+        sent_b[n * half : (n + 1) * half] = total(1 - y, n, half).astype(BF)
+    sent_a[2 * half :] = table.astype(BF)
+
+
+def core_stage(kept, got, table):
+    half, tables = kept.shape[1] // 2, table.shape[0]
+    outs = (
+        shape_of(2, half, kind=F32),
+        shape_of(2 * half + tables),
+        shape_of(2, half, kind=F32),
+        shape_of(2 * half),
+        shape_of(tables, kind=F32),
+    )
+    return stage_call(core_kernel, outs, kept, got, table)
+
+
+def pair_kernel(own_a, got_a, own_b, got_b, table_ref, keep_a, sent_a, keep_b, sent_b, out_ref):
+    half = own_a.shape[1]
+    table = table_ref[...].astype(BF).astype(F32) + got_a[2 * half :].astype(F32)
+    out_ref[...] = table
+    for own, got, keep, sent, mine in (
+        (own_a, got_a, keep_a, sent_a, device_bits(2, 1)),
+        (own_b, got_b, keep_b, sent_b, device_bits(1, 1)),
+    ):
+        keep[...] = own[mine] + got[pl.ds(mine * half, half)].astype(F32)
+        other = 1 - mine
+        total = own[other] + got[pl.ds(other * half, half)].astype(F32)
+        sent[:half] = total.astype(BF)
+    sent_a[half:] = table.astype(BF)
+
+
+def pair_stage(own_a, got_a, own_b, got_b, table):
+    half, tables = own_a.shape[1], table.shape[0]
+    outs = (
+        shape_of(half, kind=F32),
+        shape_of(half + tables),
+        shape_of(half, kind=F32),
+        shape_of(half),
+        shape_of(tables, kind=F32),
+    )
+    return stage_call(pair_kernel, outs, own_a, got_a, own_b, got_b, table)
+
+
+def top_kernel(own_a, got_a, own_b, got_b, table_ref, kept_ref, sent1, sent2, sent3, out_ref, sum_ref):
+    half = own_a.shape[0]
+    sum_ref[:half] = own_a[...] + got_a[:half].astype(F32)
+    sum_ref[half:] = own_b[...] + got_b[...].astype(F32)
+    table = table_ref[...].astype(BF).astype(F32) + got_a[half:].astype(F32)
+    out_ref[...] = table
+    top = 4
+    count = kept_ref.shape[0]
+    tiles = count // 4
+    mine = device_bits(3, 2)
+    for n, target in enumerate((kept_ref, sent1, sent2, sent3)):
+        t = mine ^ n
+        kind = target.dtype
+        target[: 3 * tiles] = sum_ref[pl.ds(t * 3 * tiles, 3 * tiles)].astype(kind)
+        proj = sum_ref[pl.ds(top * 3 * tiles + t * tiles, tiles)]
+        target[3 * tiles : count] = proj.astype(kind)
+        if n:
+            target[count:] = table.astype(BF)
+
+
+def top_stage(own_a, got_a, own_b, got_b, table):
+    units, tables = 2 * own_a.shape[0], table.shape[0]
+    sent = shape_of(units // 4 + tables)
+    outs = (shape_of(units // 4, kind=F32), sent, sent, sent, shape_of(tables, kind=F32))
+    scratch = [pltpu.VMEM((units, UNIT, LANES), F32)]
+    return stage_call(top_kernel, outs, own_a, got_a, own_b, got_b, table, scratch=scratch)
+
+
+def finish_kernel(
+    own_ref, table_ref, got1, got2, got3, w_ref, gain_ref, qkv_ref, proj_ref, g_ref, t_ref
+):
     gots = (got1, got2, got3)
     units = own_ref.shape[0]
-    sum_ref[...] = pair_sum(own_ref[...], [g[:units].astype(F32) for g in gots])
-    table = pair_sum(table_ref[...].astype(BF).astype(F32), [g[units:].astype(F32) for g in gots])
-    out_ref[...] = table
-    top = 1 + len(sent_refs)
-    per_top = 3 * slabs
-    tiles = kept_ref.shape[0] - per_top
-    mine = device_bits(3, 2)
-    for n in range(top):
-        t = mine ^ n
-        target = kept_ref if n == 0 else sent_refs[n - 1]
-        kind = F32 if n == 0 else BF
-        target[:per_top] = sum_ref[pl.ds(t * per_top, per_top)].astype(kind)
-        here = (t >= base) & (t < base + slabs)
-        slab = jnp.clip(t - base, 0, slabs - 1)
-        proj = sum_ref[pl.ds(top * per_top + slab * tiles, tiles)]
-        target[per_top : per_top + tiles] = jnp.where(here, proj, 0.0).astype(kind)
-        if n:
-            target[per_top + tiles :] = table.astype(BF)
-
-
-def top_stage(base, slabs, tiles, own, table, gots):
-    units = 3 * slabs + tiles
-    whole = pl.BlockSpec(memory_space=pltpu.VMEM)
-    sent = jax.ShapeDtypeStruct((units + slabs, UNIT, LANES), BF)
-    return pl.pallas_call(
-        lambda *refs: top_kernel(base, slabs, *refs),
-        in_specs=[whole] * 5,
-        out_shape=(
-            jax.ShapeDtypeStruct((units, UNIT, LANES), F32),
-            sent,
-            sent,
-            sent,
-            jax.ShapeDtypeStruct(table.shape, F32),
-        ),
-        scratch_shapes=[pltpu.VMEM(own.shape, F32)],
-        compiler_params=PARAMS,
-    )(own, table, *gots)
-
-
-def finish_kernel(slabs, *refs):
-    w_ref, gain_ref, qkv_ref, proj_ref, g_ref, t_ref = refs[-6:]
     c = proj_ref.shape[1]
     tiles = c // LANES
     entries = t_ref.shape[1]
-    base, proj = 0, None
-    for group, count in enumerate(slabs):
-        own_ref, table_ref, *gots = refs[group * 5 : group * 5 + 5]
-        units = own_ref.shape[0]
-        total = pair_sum(own_ref[...], [g[:units].astype(F32) for g in gots])
-        table = pair_sum(
-            table_ref[...].astype(BF).astype(F32), [g[units:].astype(F32) for g in gots]
-        )
-        for n in range(3):
-            for s in range(count):
-                at = n * c + (base + s) * LANES
-                qkv_ref[:, at : at + LANES] = total[n * count + s]
-        part = total[3 * count :]
-        proj = part if proj is None else proj + part
-        for s in range(count):
-            rows = slice((base + s) * SLAB, (base + s + 1) * SLAB)
-            for n in range(UNIT // SLAB):
-                lanes = min(LANES, entries - n * LANES)
-                t_ref[rows, n * LANES : n * LANES + lanes] = table[
-                    s, n * SLAB : (n + 1) * SLAB, :lanes
-                ]
-        base += count
-    for m in range(tiles):
-        proj_ref[:, m * LANES : (m + 1) * LANES] = proj[m]
+    total = pair_sum(own_ref[...], [g[:units].astype(F32) for g in gots])
+    table = pair_sum(table_ref[...].astype(BF).astype(F32), [g[units:].astype(F32) for g in gots])
+    for n in range(3 * tiles):
+        qkv_ref[:, n * LANES : (n + 1) * LANES] = total[n]
+    for n in range(tiles):
+        proj_ref[:, n * LANES : (n + 1) * LANES] = total[3 * tiles + n]
+    for s in range(table.shape[0]):
+        for n in range(UNIT // SLAB):
+            lanes = min(LANES, entries - n * LANES)
+            t_ref[s * SLAB : (s + 1) * SLAB, n * LANES : n * LANES + lanes] = table[
+                s, n * SLAB : (n + 1) * SLAB, :lanes
+            ]
     start = pl.multiple_of(device_index() * UNIT, UNIT)
     rows = w_ref[pl.ds(start, UNIT), :].astype(F32)
     products = jnp.sum(rows * qkv_ref[...], axis=1, keepdims=True)
@@ -709,22 +731,15 @@
     g_ref[...] = jnp.broadcast_to(column, (UNIT, LANES)).T[:1, :]
 
 
-def finish(slabs, groups, w_qkv, gain, entries):
+def finish(own, table, gots, w_qkv, gain, entries):
     c = w_qkv.shape[0]
-    whole = pl.BlockSpec(memory_space=pltpu.VMEM)
-    args = [a for own, table, gots in groups for a in (own, table, *gots)]
-    return pl.pallas_call(
-        lambda *refs: finish_kernel(slabs, *refs),
-        in_specs=[whole] * (len(args) + 2),
-        out_shape=(
-            jax.ShapeDtypeStruct((UNIT, 3 * c), F32),
-            jax.ShapeDtypeStruct((UNIT, c), F32),
-            jax.ShapeDtypeStruct((1, UNIT), F32),
-            jax.ShapeDtypeStruct((H, entries), F32),
-        ),
-        compiler_params=PARAMS,
-        name="finish",
-    )(*args, w_qkv, gain)
+    outs = (
+        jax.ShapeDtypeStruct((UNIT, 3 * c), F32),
+        jax.ShapeDtypeStruct((UNIT, c), F32),
+        jax.ShapeDtypeStruct((1, UNIT), F32),
+        jax.ShapeDtypeStruct((H, entries), F32),
+    )
+    return stage_call(finish_kernel, outs, own, table, *gots, w_qkv, gain)
 
 
 def flat_permute(value, mask):
@@ -785,57 +800,36 @@
     entries = bias_table.shape[0]
     gain_row = gain.reshape(1, c)
     split = c // n_dev == UNIT and n_lat == 4
-    total = c // LANES
-    slabs = (total - 1, 1)
-
-    rim = jnp.stack([inputs[:, columns - WW :], d_out[:, columns - WW :]])
-    halo = ring_shift(rim, 1)
-    *carried, w_qkv, w_proj, edge, hot, bias = before(
+
+    *carried, w_qkv, w_proj, edge, last, hot, bias = before(
         shifts, rel_index, bias_table.T, gain_row, inputs, d_out, w_qkv, w_proj
     )
-    x, d, nt, qkv, dh = project_rim(shifts, halo, edge, w_qkv, w_proj, gain_row, carried)
-
-    def three(values, low):
-        return [flat_permute(value, n << low) for n, value in enumerate(values, 1)]
-
-    tiles = c // LANES
-    shared = (qkv, dh, bias, hot, nt, d, scales, n_dev, split)
-    dp0, *out0 = attend(0, slabs[0], *shared)
+    halo = ring_shift(last, 1)
+    early = attend_first(EARLY, carried[3], carried[4], bias)
+    x, d, nt, qkv, dh = project_rim(shifts, halo, edge, w_qkv, w_proj, gain_row, early[2], carried)
+    dp, *out = attend(qkv, dh, bias, hot, nt, d, early, scales, n_dev, split)
     if split:
-        got0 = flat_permute(out0[1], 1)
-    early = attend_first(slabs[0], slabs[1], x.shape[0] // 2, qkv, dh, bias)
-    if split:
-        own0, *sent0, table0 = low_stage(out0[0], got0, out0[2])
-        got0 = three(sent0, 1)
-    dp1, *out1 = attend(slabs[0], slabs[1], *shared, early=early)
-    if split:
-        got1 = flat_permute(out1[1], 1)
-    first = input_rim((dp0, dp1), x, d, w_qkv, gain_row)
+        kept, sent, table = out
+        got = flat_permute(sent, 1)
+    first = input_rim(dp, x, d, w_qkv, gain_row)
     returned = ring_shift(first, -1)
     if split:
-        own1, *sent1, table1 = low_stage(out1[0], got1, out1[2])
-        got1 = three(sent1, 1)
-        own0, *sent0, table0 = top_stage(0, slabs[0], tiles, own0, table0, got0)
-        got0 = three(sent0, 3)
-    grid, end = input_rest(shifts, (dp0, dp1), x, d, w_qkv, gain_row, first)
+        own_a, sent_a, own_b, sent_b, table = core_stage(kept, got, table)
+        got_a, got_b = flat_permute(sent_a, 2), flat_permute(sent_b, 4)
+    grid, end = input_rest(shifts, dp, x, d, w_qkv, gain_row, first)
     if split:
-        own1, *sent1, table1 = top_stage(slabs[0], slabs[1], tiles, own1, table1, got1)
-        got1 = three(sent1, 3)
+        own_a, sent_a, own_b, sent_b, table = pair_stage(own_a, got_a, own_b, got_b, table)
+        got_a, got_b = flat_permute(sent_a, 4), flat_permute(sent_b, 2)
     d_inputs = place_last(shifts, end, returned, grid)
     if split:
-        g_qkv, g_proj, g_gain, g_table = finish(
-            slabs, ((own0, table0, got0), (own1, table1, got1)), w_qkv, gain_row, entries
-        )
+        own, *sent, table = top_stage(own_a, got_a, own_b, got_b, table)
+        gots = [flat_permute(value, n << 3) for n, value in enumerate(sent, 1)]
+        g_qkv, g_proj, g_gain, g_table = finish(own, table, gots, w_qkv, gain_row, entries)
         return (d_inputs, g_qkv, g_proj, g_gain.reshape(UNIT), g_table.T)
 
-    parts = []
-    for n in range(3):
-        for out, count in ((out0, slabs[0]), (out1, slabs[1])):
-            parts.append(out[0][:, n * count * LANES : (n + 1) * count * LANES])
-    parts.append(jnp.concatenate([out0[1], out1[1]], axis=0))
-    own = scatter_sum(jnp.concatenate(parts, axis=1))
+    own = scatter_sum(jnp.concatenate(out[:2], axis=1))
     g_qkv, g_proj = own[:, : 3 * c], own[:, 3 * c :]
-    g_table = full_sum(jnp.concatenate([out0[2], out1[2]], axis=0)).T
+    g_table = full_sum(out[2]).T
     rows = c // n_dev
     me = device_index()
     w_rows = lax.dynamic_slice_in_dim(w_qkv, me * rows, rows, 0).astype(F32)

time: 63.8 us -> 55.1 us (0.86)
  starting transfers between devices: 19.8 us -> 13.2 us
  Pallas kernels: 27.4 us -> 26.1 us
  local copies, waits for them, and re-layouts: 1 us -> 0.01 us
    ppermute x14 -> x8, starting transfers between devices: 14.9 us -> 6.96 us  [flat_permute(): lax.ppermute(value, ('lon', 'lat'), [(n, n ^ mask) for n in range(total)])]
    ppermute x2, starting transfers between devices: 4.81 us -> 6.21 us  [ring_shift(): lax.ppermute(value, 'lon', [(n, (n + steps) % count) for n in range(count)])]
    pallas_call x8 -> x6, Pallas kernels: 15.4 us -> 14.1 us  [the longest x1 7.39 us: attend_first(): pl.pallas_call(lambda *refs: attend_first_kernel(start, *refs), in_specs=...]
    ppermute x14 -> x8, waiting for transfers between devices: 11.2 us -> 12.3 us  [flat_permute(): lax.ppermute(value, ('lon', 'lat'), [(n, n ^ mask) for n in range(total)])]
    another operation x1 -> x0, local copies, waits for them, and re-layouts: 1 us -> none  [step(): rim = jnp.stack([inputs[:, columns - WW:], d_out[:, columns - WW:]])]
    ppermute x2, waiting for transfers between devices: 2.74 us -> 1.95 us  [ring_shift(): lax.ppermute(value, 'lon', [(n, (n + steps) % count) for n in range(count)])]
  transfers between devices with their start and end apart: 16 -> 10, of which waited for: 3 -> 5; matrix products, arithmetic and copies ran while one was open for 0% -> 0% of each run, Pallas kernels for 24% -> 23%
where the time goes in v3:
time: 55.1 us; the launch traced here: 54.9 us
  Pallas kernels  26.1 us (47%)
  waiting for transfers between devices  14.3 us (26%)
  starting transfers between devices  13.2 us (24%)
  between operations  1.37 us (2%)
    ppermute x8, waiting for transfers between devices, flat_permute(): lax.ppermute(value, ('lon', 'lat'), [(n, n ^ mask) for n in range(total)])  12.3 us
    pallas_call x1, Pallas kernels, attend_first(): pl.pallas_call(lambda *refs: attend_first_kernel(start, *refs), in_specs=...  7.39 us
    ppermute x8, starting transfers between devices, flat_permute(): lax.ppermute(value, ('lon', 'lat'), [(n, n ^ mask) for n in range(total)])  6.96 us
    ppermute x2, starting transfers between devices, ring_shift(): lax.ppermute(value, 'lon', [(n, (n + steps) % count) for n in range(count)])  6.21 us
    pallas_call x1, Pallas kernels, before(): pl.pallas_call(before_kernel, in_specs=[scalar, whole, whole, whole, far,...  5.97 us
    pallas_call x1, Pallas kernels, attend(): pl.pallas_call(lambda *refs: attend_kernel(scales, split, *refs), in_spec...  5.52 us
    pallas_call x1, Pallas kernels, input_rest(): pl.pallas_call(input_rest_kernel, in_specs=[pl.BlockSpec(memory_space=plt...  3.59 us
    ppermute x2, waiting for transfers between devices, ring_shift(): lax.ppermute(value, 'lon', [(n, (n + steps) % count) for n in range(count)])  1.95 us
  transfers between devices with their start and end apart: 10, of which 5 were waited for; matrix products, arithmetic and copies ran while one was open for 0% of the time, Pallas kernels for 23%

profile of v3, /device:TPU:0, one launch (start us, length us, event | category | flops | bytes accessed | tf_op | source)
XLA Modules:
  0.0 54.9 jit_solution(5843121399244694109)
XLA Ops:
  1.3 6.0 %before.1 = (bf16[8,128,512]{2,1,0:T(8,128)(2,1)S(1)}, bf16[8,128,512]{2,1,0:T(8,128)(2,1)S(1)}, bf16[512,1024]{1,0:T(8,128)(2,1)S(1)}, bf16[8,128,1536]{2,1,0:T...) custom-call(s32[1]{0:T(128)S(6)} %copy.25.shift_ref, ...), custom_call_target="tpu_custom_call" | custom-call | tf_op jit(solution)/shard_map/before/pallas_call | solution.py:208
  7.3 3.2 %collective-permute-start = (bf16[2,8,16,512]{3,2,1,0:T(8,128)(2,1)S(1)}, bf16[2,8,16,512]{3,2,1,0:T(8,128)(2,1)S(1)}, u32[]{:S(2)}, u32[]{:S(2)}) collective-permute-start(bf16[2,8,16,512]{3,2,1,0:T(8,128)(2,1)S(1)} %get-tuple-element.49), channel_id=1, source_target_pairs={{0,4},{4,8},{8,12},{12,16},{16,20},{20,24},{24,28},{28,0},{1,5},{5... | collective-permute-start | bytes 786440 | tf_op jit(solution)/shard_map/ppermute | solution.py:790
  10.5 7.4 %attend_first.1 = (bf16[6,128,1536]{2,1,0:T(8,128)(2,1)S(1)}, bf16[512,768]{1,0:T(8,128)(2,1)S(1)}, f32[16,128,128]{2,1,0:T(8,128)S(1)}) custom-call(bf16[8,128,1536]{2,1,0:T(8,128)(2,1)S(1)} %get-tuple-element.53.refs_0_.refs_4_, bf16[8,128,512]{2,1,0:T(8,128)(2,1)S(1)} %get-tuple-element.54.refs_1_.refs_5_, f32[16,128,128]{2,1,0:T(8,128)S(1)} %get-tuple-element.55.refs_2_), custom_call_target="tpu_custom_call" | custom-call | tf_op jit(solution)/shard_map/attend_first/pallas_call | solution.py:378
  17.9 1.9 %collective-permute-done.halo_ref = bf16[2,8,16,512]{3,2,1,0:T(8,128)(2,1)S(1)} collective-permute-done((bf16[2,8,16,512]{3,2,1,0:T(8,128)(2,1)S(1)}, bf16[2,8,16,512]{3,2,1,0:T(8,128)(2,1)S(1)}, u32[]{:S(2)}, u32[]{:S(2)}) %collective-permute-start) | collective-permute-done | bytes 262176 | tf_op jit(solution)/shard_map/ppermute | solution.py:790
  19.8 0.9 %project_rim.1 = (bf16[8,128,512]{2,1,0:T(8,128)(2,1)S(1)}, bf16[8,128,512]{2,1,0:T(8,128)(2,1)S(1)}, bf16[512,1024]{1,0:T(8,128)(2,1)S(1)}, bf16[8,128,1536]{2,1,0:T(8,128)(2,1)S(1)}, bf16[8,128,512]{2,1,0:T(8,128)(2,1)S(1)}) custom-call(s32[1]{0:T(128)S(6)} %copy.25.shift_ref, ...), custom_call_target="tpu_custom_call", output_to_operand_aliasing={{0}: (7, {}), {1}: (8, {}), {2}: (9, {}), {3}: (10, {}), {4... | custom-call | tf_op jit(solution)/shard_map/project_rim/pallas_call | solution.py:239
  20.7 5.5 %attend.1 = (bf16[8,128,1536]{2,1,0:T(8,128)(2,1)S(1)}, bf16[4,64,16,128]{3,2,1,0:T(8,128)(2,1)S(1)}, bf16[260,16,128]{2,1,0:T(8,128)(2,1)S(1)}, f32[4,16,128]{2,1,0:T(8,128)S(1)}) custom-call(bf16[8,128,1536]{2,1,0:T(8,128)(2,1)S(1)} %get-tuple-element.60.refs_0_, bf16[8,128,512]{2,1,0:T(8,128)(2,1)S(1)} %get-tuple-element.61.refs_1_, ...), custom_call_target="tpu_custom_call" | custom-call | tf_op jit(solution)/shard_map/attend/pallas_call | solution.py:480
  26.2 0.1 collective-permute-start.2
  26.3 2.7 %collective-permute-done.2.got_ref = bf16[260,16,128]{2,1,0:T(8,128)(2,1)S(1)} collective-permute-done((bf16[260,16,128]{2,1,0:T(8,128)(2,1)S(1)}, bf16[260,16,128]{2,1,0:T(8,128)(2,1)S(1)}, u32[]{:S(2)}, u32[]{:S(2)}) %collective-permute-start.2) | collective-permute-done | bytes 1064992 | tf_op jit(solution)/shard_map/ppermute | solution.py:747
  29.0 0.2 shard_map.119
  29.2 1.5 %collective-permute-start.3 = (bf16[68,16,128]{2,1,0:T(8,128)(2,1)S(1)}, bf16[68,16,128]{2,1,0:T(8,128)(2,1)S(1)}, u32[]{:S(2)}, u32[]{:S(2)}) collective-permute-start(bf16[68,16,128]{2,1,0:T(8,128)(2,1)S(1)} %get-tuple-element.75), channel_id=1, source_target_pairs={{0,2},{1,3},{2,0},{3,1},{4,6},{5,7},{6,4},{7,5},{8,10},{9,11},{10,... | collective-permute-start | bytes 835592 | tf_op jit(solution)/shard_map/ppermute | solution.py:747
  30.8 8.1 %collective-permute-done.4.got_b = bf16[64,16,128]{2,1,0:T(8,128)(2,1)S(1)} collective-permute-done((bf16[64,16,128]{2,1,0:T(8,128)(2,1)S(1)}, bf16[64,16,128]{2,1,0:T(8,128)(2,1)S(1)}, u32[]{:S(2)}, u32[]{:S(2)}) %collective-permute-start.4) | collective-permute-done | bytes 262176 | tf_op jit(solution)/shard_map/ppermute | solution.py:747
  38.8 0.1 shard_map.120
  38.9 0.3 collective-permute-start.5
  39.3 0.6 %collective-permute-start.6 = (bf16[32,16,128]{2,1,0:T(8,128)(2,1)S(1)}, bf16[32,16,128]{2,1,0:T(8,128)(2,1)S(1)}, u32[]{:S(2)}, u32[]{:S(2)}) collective-permute-start(bf16[32,16,128]{2,1,0:T(8,128)(2,1)S(1)} %get-tuple-element.82), channel_id=1, source_target_pairs={{0,2},{1,3},{2,0},{3,1},{4,6},{5,7},{6,4},{7,5},{8,10},{9,11},{10,... | collective-permute-start | bytes 393224 | tf_op jit(solution)/shard_map/ppermute | solution.py:747
  39.8 0.8 %input_rim.1.rim_ref = bf16[128,512]{1,0:T(8,128)(2,1)S(1)} custom-call(bf16[8,128,1536]{2,1,0:T(8,128)(2,1)S(1)} %get-tuple-element.67.dp_ref, bf16[8,128,512]{2,1,0:T(8,128)(2,1)S(1)} %get-tuple-element.68.x_ref, bf16[8,128,512]{2,1,0:T(8,128)(2,1)S(1)} %get-tuple-element.64.refs_5_.d_ref, bf16[512,1536]{1,0:T(8,128)(2,1)S(1)} %get-tuple-element.51.wq_ref.w_ref, ...), custom_call_target="tpu_custom_call" | custom-call | tf_op jit(solution)/shard_map/input_rim/pallas_call | solution.py:551
  40.6 3.0 %collective-permute-start.1 = (bf16[128,512]{1,0:T(8,128)(2,1)S(1)}, bf16[128,512]{1,0:T(8,128)(2,1)S(1)}, u32[]{:S(2)}, u32[]{:S(2)}) collective-permute-start(bf16[128,512]{1,0:T(8,128)(2,1)S(1)} %input_rim.1.rim_ref), channel_id=1, source_target_pairs={{0,28},{4,0},{8,4},{12,8},{16,12},{20,16},{24,20},{28,24},{1,29},{... | collective-permute-start | bytes 393224 | tf_op jit(solution)/shard_map/ppermute | solution.py:790
  43.6 0.7 %collective-permute-done.6.got_b = bf16[32,16,128]{2,1,0:T(8,128)(2,1)S(1)} collective-permute-done((bf16[32,16,128]{2,1,0:T(8,128)(2,1)S(1)}, bf16[32,16,128]{2,1,0:T(8,128)(2,1)S(1)}, u32[]{:S(2)}, u32[]{:S(2)}) %collective-permute-start.6) | collective-permute-done | bytes 131104 | tf_op jit(solution)/shard_map/ppermute | solution.py:747
  44.3 0.9 %collective-permute-done.5.got_a = bf16[36,16,128]{2,1,0:T(8,128)(2,1)S(1)} collective-permute-done((bf16[36,16,128]{2,1,0:T(8,128)(2,1)S(1)}, bf16[36,16,128]{2,1,0:T(8,128)(2,1)S(1)}, u32[]{:S(2)}, u32[]{:S(2)}) %collective-permute-start.5) | collective-permute-done | bytes 147488 | tf_op jit(solution)/shard_map/ppermute | solution.py:747
  45.2 0.1 shard_map.121
  45.3 2.4 %collective-permute-start.8 = (bf16[20,16,128]{2,1,0:T(8,128)(2,1)S(1)}, bf16[20,16,128]{2,1,0:T(8,128)(2,1)S(1)}, u32[]{:S(2)}, u32[]{:S(2)}) collective-permute-start(bf16[20,16,128]{2,1,0:T(8,128)(2,1)S(1)} %get-tuple-element.87), channel_id=1, source_target_pairs={{0,16},{1,17},{2,18},{3,19},{4,20},{5,21},{6,22},{7,23},{8,24},{9,... | collective-permute-start | bytes 245768 | tf_op jit(solution)/shard_map/ppermute | solution.py:747
  47.8 1.9 %collective-permute-start.9 = (bf16[20,16,128]{2,1,0:T(8,128)(2,1)S(1)}, bf16[20,16,128]{2,1,0:T(8,128)(2,1)S(1)}, u32[]{:S(2)}, u32[]{:S(2)}) collective-permute-start(bf16[20,16,128]{2,1,0:T(8,128)(2,1)S(1)} %get-tuple-element.88), channel_id=1, source_target_pairs={{0,24},{1,25},{2,26},{3,27},{4,28},{5,29},{6,30},{7,31},{8,16},{9,... | collective-permute-start | bytes 245768 | tf_op jit(solution)/shard_map/ppermute | solution.py:747
  49.7 3.6 %input_rest.1 = (bf16[8,128,512]{2,1,0:T(8,128)(2,1)}, bf16[128,512]{1,0:T(8,128)(2,1)S(1)}) custom-call(s32[1]{0:T(128)S(6)} %copy.25.shift_ref, bf16[8,128,1536]{2,1,0:T(8,128)(2,1)S(1)} %get-tuple-element.67.dp_ref, bf16[8,128,512]{2,1,0:T(8,128)(2,1)S(1)} %get-tuple-element.68.x_ref, bf16[8,128,512]{2,1,0:T(8,128)(2,1)S(1)} %get-tuple-element.64.refs_5_.d_ref, ...), custom_call_target="tpu_custom_call" | custom-call | tf_op jit(solution)/shard_map/input_rest/pallas_call | solution.py:562
  53.3 0.8 %place_last.1 = bf16[8,128,512]{2,1,0:T(8,128)(2,1)} custom-call(s32[1]{0:T(128)S(6)} %copy.25.shift_ref, bf16[128,512]{1,0:T(8,128)(2,1)S(1)} %get-tuple-element.69.end_ref, bf16[128,512]{1,0:T(8,128)(2,1)S(1)} %collective-permute-done.1.rim_ref, bf16[8,128,512]{2,1,0:T(8,128)(2,1)} %get-tuple-element.70.grid_ref), custom_call_target="tpu_custom_call", output_to_operand_aliasing={{}: (3, {})} | custom-call | tf_op jit(solution)/shard_map/place_last/pallas_call | solution.py:579
  54.2 0.7 %shard_map.122 = (f32[16,1536]{1,0:T(8,128)}, f32[16,512]{1,0:T(8,128)}, f32[1,16]{1,0:T(1,128)}, f32[16,465]{1,0:T(8,128)}) custom-call(f32[16,16,128]{2,1,0:T(8,128)S(1)} %get-tuple-element.84.own_ref, f32[4,16,128]{2,1,0:T(8,128)S(1)} %get-tuple-element.85.table_ref, bf16[20,16,128]{2,1,0:T(8,128)(2,1)S(1)} %collective-permute-done.7.got1, ...), custom_call_target="tpu_custom_call" | custom-call | tf_op jit(solution)/shard_map/pallas_call | solution.py:608
  (9 shorter events, 0.1 us)
Async XLA Ops:
  7.3 12.6 %collective-permute-start = (bf16[2,8,16,512]{3,2,1,0:T(8,128)(2,1)S(1)}, bf16[2,8,16,512]{3,2,1,0:T(8,128)(2,1)S(1)}, u32[]{:S(2)}, u32[]{:S(2)}) collective-permute-start(bf16[2,8,16,512]{3,2,1,0:T(8,128)(2,1)S(1)} %get-tuple-element.49), channel_id=1, source_target_pairs={{0,4},{4,8},{8,12},{12,16},{16,20},{20,24},{24,28},{28,0},{1,5},{5... | collective-permute-start | bytes 786440 | tf_op jit(solution)/shard_map/ppermute | solution.py:790
  10.5 9.3 %copy-start = (f32[512]{0:T(512)S(1)}, f32[512]{0:T(512)}, u32[]{:S(2)}) copy-start(f32[512]{0:T(512)} %param.12) | copy-start | bytes 6148
  26.2 2.7 %collective-permute-start.2 = (bf16[260,16,128]{2,1,0:T(8,128)(2,1)S(1)}, bf16[260,16,128]{2,1,0:T(8,128)(2,1)S(1)}, u32[]{:S(2)}, u32[]{:S(2)}) collective-permute-start(bf16[260,16,128]{2,1,0:T(8,128)(2,1)S(1)} %get-tuple-element.72), channel_id=1, source_target_pairs={{0,1},{1,0},{2,3},{3,2},{4,5},{5,4},{6,7},{7,6},{8,9},{9,8},{10,11... | collective-permute-start | bytes 3194888 | tf_op jit(solution)/shard_map/ppermute | solution.py:747
  29.2 9.6 %collective-permute-start.3 = (bf16[68,16,128]{2,1,0:T(8,128)(2,1)S(1)}, bf16[68,16,128]{2,1,0:T(8,128)(2,1)S(1)}, u32[]{:S(2)}, u32[]{:S(2)}) collective-permute-start(bf16[68,16,128]{2,1,0:T(8,128)(2,1)S(1)} %get-tuple-element.75), channel_id=1, source_target_pairs={{0,2},{1,3},{2,0},{3,1},{4,6},{5,7},{6,4},{7,5},{8,10},{9,11},{10,... | collective-permute-start | bytes 835592 | tf_op jit(solution)/shard_map/ppermute | solution.py:747
  30.8 8.1 %collective-permute-start.4 = (bf16[64,16,128]{2,1,0:T(8,128)(2,1)S(1)}, bf16[64,16,128]{2,1,0:T(8,128)(2,1)S(1)}, u32[]{:S(2)}, u32[]{:S(2)}) collective-permute-start(bf16[64,16,128]{2,1,0:T(8,128)(2,1)S(1)} %get-tuple-element.77), channel_id=1, source_target_pairs={{0,4},{1,5},{2,6},{3,7},{4,0},{5,1},{6,2},{7,3},{8,12},{9,13},{10,... | collective-permute-start | bytes 786440 | tf_op jit(solution)/shard_map/ppermute | solution.py:747
  38.9 6.2 %collective-permute-start.5 = (bf16[36,16,128]{2,1,0:T(8,128)(2,1)S(1)}, bf16[36,16,128]{2,1,0:T(8,128)(2,1)S(1)}, u32[]{:S(2)}, u32[]{:S(2)}) collective-permute-start(bf16[36,16,128]{2,1,0:T(8,128)(2,1)S(1)} %get-tuple-element.80), channel_id=1, source_target_pairs={{0,4},{1,5},{2,6},{3,7},{4,0},{5,1},{6,2},{7,3},{8,12},{9,13},{10,... | collective-permute-start | bytes 442376 | tf_op jit(solution)/shard_map/ppermute | solution.py:747
  39.3 5.0 %collective-permute-start.6 = (bf16[32,16,128]{2,1,0:T(8,128)(2,1)S(1)}, bf16[32,16,128]{2,1,0:T(8,128)(2,1)S(1)}, u32[]{:S(2)}, u32[]{:S(2)}) collective-permute-start(bf16[32,16,128]{2,1,0:T(8,128)(2,1)S(1)} %get-tuple-element.82), channel_id=1, source_target_pairs={{0,2},{1,3},{2,0},{3,1},{4,6},{5,7},{6,4},{7,5},{8,10},{9,11},{10,... | collective-permute-start | bytes 393224 | tf_op jit(solution)/shard_map/ppermute | solution.py:747
  40.6 12.7 %collective-permute-start.1 = (bf16[128,512]{1,0:T(8,128)(2,1)S(1)}, bf16[128,512]{1,0:T(8,128)(2,1)S(1)}, u32[]{:S(2)}, u32[]{:S(2)}) collective-permute-start(bf16[128,512]{1,0:T(8,128)(2,1)S(1)} %input_rim.1.rim_ref), channel_id=1, source_target_pairs={{0,28},{4,0},{8,4},{12,8},{16,12},{20,16},{24,20},{28,24},{1,29},{... | collective-permute-start | bytes 393224 | tf_op jit(solution)/shard_map/ppermute | solution.py:790
  45.3 8.9 %collective-permute-start.7 = (bf16[20,16,128]{2,1,0:T(8,128)(2,1)S(1)}, bf16[20,16,128]{2,1,0:T(8,128)(2,1)S(1)}, u32[]{:S(2)}, u32[]{:S(2)}) collective-permute-start(bf16[20,16,128]{2,1,0:T(8,128)(2,1)S(1)} %get-tuple-element.86), channel_id=1, source_target_pairs={{0,8},{1,9},{2,10},{3,11},{4,12},{5,13},{6,14},{7,15},{8,0},{9,1},... | collective-permute-start | bytes 245768 | tf_op jit(solution)/shard_map/ppermute | solution.py:747
  45.3 8.8 %collective-permute-start.8 = (bf16[20,16,128]{2,1,0:T(8,128)(2,1)S(1)}, bf16[20,16,128]{2,1,0:T(8,128)(2,1)S(1)}, u32[]{:S(2)}, u32[]{:S(2)}) collective-permute-start(bf16[20,16,128]{2,1,0:T(8,128)(2,1)S(1)} %get-tuple-element.87), channel_id=1, source_target_pairs={{0,16},{1,17},{2,18},{3,19},{4,20},{5,21},{6,22},{7,23},{8,24},{9,... | collective-permute-start | bytes 245768 | tf_op jit(solution)/shard_map/ppermute | solution.py:747
  47.8 6.4 %collective-permute-start.9 = (bf16[20,16,128]{2,1,0:T(8,128)(2,1)S(1)}, bf16[20,16,128]{2,1,0:T(8,128)(2,1)S(1)}, u32[]{:S(2)}, u32[]{:S(2)}) collective-permute-start(bf16[20,16,128]{2,1,0:T(8,128)(2,1)S(1)} %get-tuple-element.88), channel_id=1, source_target_pairs={{0,24},{1,25},{2,26},{3,27},{4,28},{5,29},{6,30},{7,31},{8,16},{9,... | collective-permute-start | bytes 245768 | tf_op jit(solution)/shard_map/ppermute | solution.py:747

commit v4 on v3

--- a/solution.py
+++ b/solution.py
@@ -19,6 +19,7 @@
 UNIT = 16
 PIECES = 1
 EARLY = 2
+SHARE = 5
 CHAINS = 16
 EPSILON = 1e-05
 LOG2E = math.log2(math.e)
@@ -616,31 +617,34 @@
 
 def core_kernel(kept_ref, got_ref, table_ref, own_a, sent_a, own_b, sent_b, out_ref):
     units = kept_ref.shape[1]
-    half = units // 2
+    half = own_a.shape[1]
     table = table_ref[...].astype(BF).astype(F32) + got_ref[4 * units :].astype(F32)
     out_ref[...] = table
     x, y = device_bits(1, 1), device_bits(2, 1)
 
-    def total(y, x, start):
+    rest = units - half
+
+    def total(y, x, start, size):
         b = 2 * y + x
-        got = got_ref[pl.ds(b * units + start, half)]
-        return kept_ref[b, start : start + half].astype(F32) + got.astype(F32)
+        got = got_ref[pl.ds(b * units + start, size)]
+        return kept_ref[b, start : start + size].astype(F32) + got.astype(F32)
 
     for n in range(2):
-        own_a[n] = total(n, x, 0)
-        sent_a[n * half : (n + 1) * half] = total(n, 1 - x, 0).astype(BF)
-        own_b[n] = total(y, n, half)
-        sent_b[n * half : (n + 1) * half] = total(1 - y, n, half).astype(BF)
+        own_a[n] = total(n, x, 0, half)
+        sent_a[n * half : (n + 1) * half] = total(n, 1 - x, 0, half).astype(BF)
+        own_b[n] = total(y, n, half, rest)
+        sent_b[n * rest : (n + 1) * rest] = total(1 - y, n, half, rest).astype(BF)
     sent_a[2 * half :] = table.astype(BF)
 
 
 def core_stage(kept, got, table):
-    half, tables = kept.shape[1] // 2, table.shape[0]
+    units, tables = kept.shape[1], table.shape[0]
+    half = units * SHARE // 8
     outs = (
         shape_of(2, half, kind=F32),
         shape_of(2 * half + tables),
-        shape_of(2, half, kind=F32),
-        shape_of(2 * half),
+        shape_of(2, units - half, kind=F32),
+        shape_of(2 * (units - half)),
         shape_of(tables, kind=F32),
     )
     return stage_call(core_kernel, outs, kept, got, table)
@@ -654,20 +658,21 @@
         (own_a, got_a, keep_a, sent_a, device_bits(2, 1)),
         (own_b, got_b, keep_b, sent_b, device_bits(1, 1)),
     ):
-        keep[...] = own[mine] + got[pl.ds(mine * half, half)].astype(F32)
+        size = own.shape[1]
+        keep[...] = own[mine] + got[pl.ds(mine * size, size)].astype(F32)
         other = 1 - mine
-        total = own[other] + got[pl.ds(other * half, half)].astype(F32)
-        sent[:half] = total.astype(BF)
+        total = own[other] + got[pl.ds(other * size, size)].astype(F32)
+        sent[:size] = total.astype(BF)
     sent_a[half:] = table.astype(BF)
 
 
 def pair_stage(own_a, got_a, own_b, got_b, table):
-    half, tables = own_a.shape[1], table.shape[0]
+    half, rest, tables = own_a.shape[1], own_b.shape[1], table.shape[0]
     outs = (
         shape_of(half, kind=F32),
         shape_of(half + tables),
-        shape_of(half, kind=F32),
-        shape_of(half),
+        shape_of(rest, kind=F32),
+        shape_of(rest),
         shape_of(tables, kind=F32),
     )
     return stage_call(pair_kernel, outs, own_a, got_a, own_b, got_b, table)
@@ -694,7 +699,7 @@
 
 
 def top_stage(own_a, got_a, own_b, got_b, table):
-    units, tables = 2 * own_a.shape[0], table.shape[0]
+    units, tables = own_a.shape[0] + own_b.shape[0], table.shape[0]
     sent = shape_of(units // 4 + tables)
     outs = (shape_of(units // 4, kind=F32), sent, sent, sent, shape_of(tables, kind=F32))
     scratch = [pltpu.VMEM((units, UNIT, LANES), F32)]

time: 55.1 us -> 56.6 us (1.027)
  starting transfers between devices: 13.2 us -> 14 us
  waiting for transfers between devices: 14.3 us -> 15 us
    ppermute x8, starting transfers between devices: 6.96 us -> 7.66 us  [flat_permute(): lax.ppermute(value, ('lon', 'lat'), [(n, n ^ mask) for n in range(total)])]
    ppermute x8, waiting for transfers between devices: 12.3 us -> 13 us  [flat_permute(): lax.ppermute(value, ('lon', 'lat'), [(n, n ^ mask) for n in range(total)])]
  transfers between devices with their start and end apart: 10 -> 10, of which waited for: 5 -> 5; matrix products, arithmetic and copies ran while one was open for 0% -> 0% of each run, Pallas kernels for 23% -> 22%
where the time goes in v4:
time: 56.6 us; the launch traced here: 56.5 us
  Pallas kernels  26.1 us (46%)
  waiting for transfers between devices  15 us (27%)
  starting transfers between devices  14 us (25%)
  between operations  1.37 us (2%)
    ppermute x8, waiting for transfers between devices, flat_permute(): lax.ppermute(value, ('lon', 'lat'), [(n, n ^ mask) for n in range(total)])  13 us
    ppermute x8, starting transfers between devices, flat_permute(): lax.ppermute(value, ('lon', 'lat'), [(n, n ^ mask) for n in range(total)])  7.66 us
    pallas_call x1, Pallas kernels, attend_first(): pl.pallas_call(lambda *refs: attend_first_kernel(start, *refs), in_specs=...  7.39 us
    ppermute x2, starting transfers between devices, ring_shift(): lax.ppermute(value, 'lon', [(n, (n + steps) % count) for n in range(count)])  6.34 us
    pallas_call x1, Pallas kernels, before(): pl.pallas_call(before_kernel, in_specs=[scalar, whole, whole, whole, far,...  5.97 us
    pallas_call x1, Pallas kernels, attend(): pl.pallas_call(lambda *refs: attend_kernel(scales, split, *refs), in_spec...  5.52 us
    pallas_call x1, Pallas kernels, input_rest(): pl.pallas_call(input_rest_kernel, in_specs=[pl.BlockSpec(memory_space=plt...  3.59 us
    ppermute x2, waiting for transfers between devices, ring_shift(): lax.ppermute(value, 'lon', [(n, (n + steps) % count) for n in range(count)])  1.95 us
  transfers between devices with their start and end apart: 10, of which 5 were waited for; matrix products, arithmetic and copies ran while one was open for 0% of the time, Pallas kernels for 22%

profile of v4, /device:TPU:0, one launch (start us, length us, event | category | flops | bytes accessed | tf_op | source)
XLA Modules:
  0.0 56.5 jit_solution(10353634992135106001)
XLA Ops:
  1.3 6.0 %before.1 = (bf16[8,128,512]{2,1,0:T(8,128)(2,1)S(1)}, bf16[8,128,512]{2,1,0:T(8,128)(2,1)S(1)}, bf16[512,1024]{1,0:T(8,128)(2,1)S(1)}, bf16[8,128,1536]{2,1,0:T...) custom-call(s32[1]{0:T(128)S(6)} %copy.25.shift_ref, ...), custom_call_target="tpu_custom_call" | custom-call | tf_op jit(solution)/shard_map/before/pallas_call | solution.py:209
  7.3 3.2 %collective-permute-start = (bf16[2,8,16,512]{3,2,1,0:T(8,128)(2,1)S(1)}, bf16[2,8,16,512]{3,2,1,0:T(8,128)(2,1)S(1)}, u32[]{:S(2)}, u32[]{:S(2)}) collective-permute-start(bf16[2,8,16,512]{3,2,1,0:T(8,128)(2,1)S(1)} %get-tuple-element.49), channel_id=1, source_target_pairs={{0,4},{4,8},{8,12},{12,16},{16,20},{20,24},{24,28},{28,0},{1,5},{5... | collective-permute-start | bytes 786440 | tf_op jit(solution)/shard_map/ppermute | solution.py:795
  10.5 7.4 %attend_first.1 = (bf16[6,128,1536]{2,1,0:T(8,128)(2,1)S(1)}, bf16[512,768]{1,0:T(8,128)(2,1)S(1)}, f32[16,128,128]{2,1,0:T(8,128)S(1)}) custom-call(bf16[8,128,1536]{2,1,0:T(8,128)(2,1)S(1)} %get-tuple-element.53.refs_0_.refs_4_, bf16[8,128,512]{2,1,0:T(8,128)(2,1)S(1)} %get-tuple-element.54.refs_1_.refs_5_, f32[16,128,128]{2,1,0:T(8,128)S(1)} %get-tuple-element.55.refs_2_), custom_call_target="tpu_custom_call" | custom-call | tf_op jit(solution)/shard_map/attend_first/pallas_call | solution.py:379
  17.9 1.9 %collective-permute-done.halo_ref = bf16[2,8,16,512]{3,2,1,0:T(8,128)(2,1)S(1)} collective-permute-done((bf16[2,8,16,512]{3,2,1,0:T(8,128)(2,1)S(1)}, bf16[2,8,16,512]{3,2,1,0:T(8,128)(2,1)S(1)}, u32[]{:S(2)}, u32[]{:S(2)}) %collective-permute-start) | collective-permute-done | bytes 262176 | tf_op jit(solution)/shard_map/ppermute | solution.py:795
  19.8 0.9 %project_rim.1 = (bf16[8,128,512]{2,1,0:T(8,128)(2,1)S(1)}, bf16[8,128,512]{2,1,0:T(8,128)(2,1)S(1)}, bf16[512,1024]{1,0:T(8,128)(2,1)S(1)}, bf16[8,128,1536]{2,1,0:T(8,128)(2,1)S(1)}, bf16[8,128,512]{2,1,0:T(8,128)(2,1)S(1)}) custom-call(s32[1]{0:T(128)S(6)} %copy.25.shift_ref, ...), custom_call_target="tpu_custom_call", output_to_operand_aliasing={{0}: (7, {}), {1}: (8, {}), {2}: (9, {}), {3}: (10, {}), {4... | custom-call | tf_op jit(solution)/shard_map/project_rim/pallas_call | solution.py:240
  20.7 5.5 %attend.1 = (bf16[8,128,1536]{2,1,0:T(8,128)(2,1)S(1)}, bf16[4,64,16,128]{3,2,1,0:T(8,128)(2,1)S(1)}, bf16[260,16,128]{2,1,0:T(8,128)(2,1)S(1)}, f32[4,16,128]{2,1,0:T(8,128)S(1)}) custom-call(bf16[8,128,1536]{2,1,0:T(8,128)(2,1)S(1)} %get-tuple-element.60.refs_0_, bf16[8,128,512]{2,1,0:T(8,128)(2,1)S(1)} %get-tuple-element.61.refs_1_, ...), custom_call_target="tpu_custom_call" | custom-call | tf_op jit(solution)/shard_map/attend/pallas_call | solution.py:481
  26.3 2.7 %collective-permute-done.2.got_ref = bf16[260,16,128]{2,1,0:T(8,128)(2,1)S(1)} collective-permute-done((bf16[260,16,128]{2,1,0:T(8,128)(2,1)S(1)}, bf16[260,16,128]{2,1,0:T(8,128)(2,1)S(1)}, u32[]{:S(2)}, u32[]{:S(2)}) %collective-permute-start.2) | collective-permute-done | bytes 1064992 | tf_op jit(solution)/shard_map/ppermute | solution.py:752
  29.0 0.2 shard_map.119
  29.2 1.5 %collective-permute-start.3 = (bf16[84,16,128]{2,1,0:T(8,128)(2,1)S(1)}, bf16[84,16,128]{2,1,0:T(8,128)(2,1)S(1)}, u32[]{:S(2)}, u32[]{:S(2)}) collective-permute-start(bf16[84,16,128]{2,1,0:T(8,128)(2,1)S(1)} %get-tuple-element.75), channel_id=1, source_target_pairs={{0,2},{1,3},{2,0},{3,1},{4,6},{5,7},{6,4},{7,5},{8,10},{9,11},{10,... | collective-permute-start | bytes 1032200 | tf_op jit(solution)/shard_map/ppermute | solution.py:752
  30.8 6.7 %collective-permute-done.4.got_b = bf16[48,16,128]{2,1,0:T(8,128)(2,1)S(1)} collective-permute-done((bf16[48,16,128]{2,1,0:T(8,128)(2,1)S(1)}, bf16[48,16,128]{2,1,0:T(8,128)(2,1)S(1)}, u32[]{:S(2)}, u32[]{:S(2)}) %collective-permute-start.4) | collective-permute-done | bytes 196640 | tf_op jit(solution)/shard_map/ppermute | solution.py:752
  37.4 2.0 %collective-permute-done.3.got_a = bf16[84,16,128]{2,1,0:T(8,128)(2,1)S(1)} collective-permute-done((bf16[84,16,128]{2,1,0:T(8,128)(2,1)S(1)}, bf16[84,16,128]{2,1,0:T(8,128)(2,1)S(1)}, u32[]{:S(2)}, u32[]{:S(2)}) %collective-permute-start.3) | collective-permute-done | bytes 344096 | tf_op jit(solution)/shard_map/ppermute | solution.py:752
  39.4 0.1 shard_map.120
  39.5 0.1 collective-permute-start.5
  39.6 1.5 %collective-permute-start.6 = (bf16[24,16,128]{2,1,0:T(8,128)(2,1)S(1)}, bf16[24,16,128]{2,1,0:T(8,128)(2,1)S(1)}, u32[]{:S(2)}, u32[]{:S(2)}) collective-permute-start(bf16[24,16,128]{2,1,0:T(8,128)(2,1)S(1)} %get-tuple-element.82), channel_id=1, source_target_pairs={{0,2},{1,3},{2,0},{3,1},{4,6},{5,7},{6,4},{7,5},{8,10},{9,11},{10,... | collective-permute-start | bytes 294920 | tf_op jit(solution)/shard_map/ppermute | solution.py:752
  41.1 0.8 %input_rim.1.rim_ref = bf16[128,512]{1,0:T(8,128)(2,1)S(1)} custom-call(bf16[8,128,1536]{2,1,0:T(8,128)(2,1)S(1)} %get-tuple-element.67.dp_ref, bf16[8,128,512]{2,1,0:T(8,128)(2,1)S(1)} %get-tuple-element.68.x_ref, bf16[8,128,512]{2,1,0:T(8,128)(2,1)S(1)} %get-tuple-element.64.refs_5_.d_ref, bf16[512,1536]{1,0:T(8,128)(2,1)S(1)} %get-tuple-element.51.wq_ref.w_ref, ...), custom_call_target="tpu_custom_call" | custom-call | tf_op jit(solution)/shard_map/input_rim/pallas_call | solution.py:552
  41.9 3.1 %collective-permute-start.1 = (bf16[128,512]{1,0:T(8,128)(2,1)S(1)}, bf16[128,512]{1,0:T(8,128)(2,1)S(1)}, u32[]{:S(2)}, u32[]{:S(2)}) collective-permute-start(bf16[128,512]{1,0:T(8,128)(2,1)S(1)} %input_rim.1.rim_ref), channel_id=1, source_target_pairs={{0,28},{4,0},{8,4},{12,8},{16,12},{20,16},{24,20},{28,24},{1,29},{... | collective-permute-start | bytes 393224 | tf_op jit(solution)/shard_map/ppermute | solution.py:795
  45.0 1.7 %collective-permute-done.5.got_a = bf16[44,16,128]{2,1,0:T(8,128)(2,1)S(1)} collective-permute-done((bf16[44,16,128]{2,1,0:T(8,128)(2,1)S(1)}, bf16[44,16,128]{2,1,0:T(8,128)(2,1)S(1)}, u32[]{:S(2)}, u32[]{:S(2)}) %collective-permute-start.5) | collective-permute-done | bytes 180256 | tf_op jit(solution)/shard_map/ppermute | solution.py:752
  46.7 0.1 shard_map.121
  46.8 0.1 collective-permute-start.7
  46.9 2.2 %collective-permute-start.8 = (bf16[20,16,128]{2,1,0:T(8,128)(2,1)S(1)}, bf16[20,16,128]{2,1,0:T(8,128)(2,1)S(1)}, u32[]{:S(2)}, u32[]{:S(2)}) collective-permute-start(bf16[20,16,128]{2,1,0:T(8,128)(2,1)S(1)} %get-tuple-element.87), channel_id=1, source_target_pairs={{0,16},{1,17},{2,18},{3,19},{4,20},{5,21},{6,22},{7,23},{8,24},{9,... | collective-permute-start | bytes 245768 | tf_op jit(solution)/shard_map/ppermute | solution.py:752
  49.1 2.1 %collective-permute-start.9 = (bf16[20,16,128]{2,1,0:T(8,128)(2,1)S(1)}, bf16[20,16,128]{2,1,0:T(8,128)(2,1)S(1)}, u32[]{:S(2)}, u32[]{:S(2)}) collective-permute-start(bf16[20,16,128]{2,1,0:T(8,128)(2,1)S(1)} %get-tuple-element.88), channel_id=1, source_target_pairs={{0,24},{1,25},{2,26},{3,27},{4,28},{5,29},{6,30},{7,31},{8,16},{9,... | collective-permute-start | bytes 245768 | tf_op jit(solution)/shard_map/ppermute | solution.py:752
  51.2 3.6 %input_rest.1 = (bf16[8,128,512]{2,1,0:T(8,128)(2,1)}, bf16[128,512]{1,0:T(8,128)(2,1)S(1)}) custom-call(s32[1]{0:T(128)S(6)} %copy.25.shift_ref, bf16[8,128,1536]{2,1,0:T(8,128)(2,1)S(1)} %get-tuple-element.67.dp_ref, bf16[8,128,512]{2,1,0:T(8,128)(2,1)S(1)} %get-tuple-element.68.x_ref, bf16[8,128,512]{2,1,0:T(8,128)(2,1)S(1)} %get-tuple-element.64.refs_5_.d_ref, ...), custom_call_target="tpu_custom_call" | custom-call | tf_op jit(solution)/shard_map/input_rest/pallas_call | solution.py:563
  54.8 0.8 %place_last.1 = bf16[8,128,512]{2,1,0:T(8,128)(2,1)} custom-call(s32[1]{0:T(128)S(6)} %copy.25.shift_ref, bf16[128,512]{1,0:T(8,128)(2,1)S(1)} %get-tuple-element.69.end_ref, bf16[128,512]{1,0:T(8,128)(2,1)S(1)} %collective-permute-done.1.rim_ref, bf16[8,128,512]{2,1,0:T(8,128)(2,1)} %get-tuple-element.70.grid_ref), custom_call_target="tpu_custom_call", output_to_operand_aliasing={{}: (3, {})} | custom-call | tf_op jit(solution)/shard_map/place_last/pallas_call | solution.py:580
  55.7 0.7 %shard_map.122 = (f32[16,1536]{1,0:T(8,128)}, f32[16,512]{1,0:T(8,128)}, f32[1,16]{1,0:T(1,128)}, f32[16,465]{1,0:T(8,128)}) custom-call(f32[16,16,128]{2,1,0:T(8,128)S(1)} %get-tuple-element.84.own_ref, f32[4,16,128]{2,1,0:T(8,128)S(1)} %get-tuple-element.85.table_ref, bf16[20,16,128]{2,1,0:T(8,128)(2,1)S(1)} %collective-permute-done.7.got1, ...), custom_call_target="tpu_custom_call" | custom-call | tf_op jit(solution)/shard_map/pallas_call | solution.py:609
  (9 shorter events, 0.1 us)
Async XLA Ops:
  7.3 12.6 %collective-permute-start = (bf16[2,8,16,512]{3,2,1,0:T(8,128)(2,1)S(1)}, bf16[2,8,16,512]{3,2,1,0:T(8,128)(2,1)S(1)}, u32[]{:S(2)}, u32[]{:S(2)}) collective-permute-start(bf16[2,8,16,512]{3,2,1,0:T(8,128)(2,1)S(1)} %get-tuple-element.49), channel_id=1, source_target_pairs={{0,4},{4,8},{8,12},{12,16},{16,20},{20,24},{24,28},{28,0},{1,5},{5... | collective-permute-start | bytes 786440 | tf_op jit(solution)/shard_map/ppermute | solution.py:795
  10.5 9.3 %copy-start = (f32[512]{0:T(512)S(1)}, f32[512]{0:T(512)}, u32[]{:S(2)}) copy-start(f32[512]{0:T(512)} %param.12) | copy-start | bytes 6148
  26.2 2.7 %collective-permute-start.2 = (bf16[260,16,128]{2,1,0:T(8,128)(2,1)S(1)}, bf16[260,16,128]{2,1,0:T(8,128)(2,1)S(1)}, u32[]{:S(2)}, u32[]{:S(2)}) collective-permute-start(bf16[260,16,128]{2,1,0:T(8,128)(2,1)S(1)} %get-tuple-element.72), channel_id=1, source_target_pairs={{0,1},{1,0},{2,3},{3,2},{4,5},{5,4},{6,7},{7,6},{8,9},{9,8},{10,11... | collective-permute-start | bytes 3194888 | tf_op jit(solution)/shard_map/ppermute | solution.py:752
  29.2 10.2 %collective-permute-start.3 = (bf16[84,16,128]{2,1,0:T(8,128)(2,1)S(1)}, bf16[84,16,128]{2,1,0:T(8,128)(2,1)S(1)}, u32[]{:S(2)}, u32[]{:S(2)}) collective-permute-start(bf16[84,16,128]{2,1,0:T(8,128)(2,1)S(1)} %get-tuple-element.75), channel_id=1, source_target_pairs={{0,2},{1,3},{2,0},{3,1},{4,6},{5,7},{6,4},{7,5},{8,10},{9,11},{10,... | collective-permute-start | bytes 1032200 | tf_op jit(solution)/shard_map/ppermute | solution.py:752
  30.8 6.7 %collective-permute-start.4 = (bf16[48,16,128]{2,1,0:T(8,128)(2,1)S(1)}, bf16[48,16,128]{2,1,0:T(8,128)(2,1)S(1)}, u32[]{:S(2)}, u32[]{:S(2)}) collective-permute-start(bf16[48,16,128]{2,1,0:T(8,128)(2,1)S(1)} %get-tuple-element.77), channel_id=1, source_target_pairs={{0,4},{1,5},{2,6},{3,7},{4,0},{5,1},{6,2},{7,3},{8,12},{9,13},{10,... | collective-permute-start | bytes 589832 | tf_op jit(solution)/shard_map/ppermute | solution.py:752
  39.5 7.2 %collective-permute-start.5 = (bf16[44,16,128]{2,1,0:T(8,128)(2,1)S(1)}, bf16[44,16,128]{2,1,0:T(8,128)(2,1)S(1)}, u32[]{:S(2)}, u32[]{:S(2)}) collective-permute-start(bf16[44,16,128]{2,1,0:T(8,128)(2,1)S(1)} %get-tuple-element.80), channel_id=1, source_target_pairs={{0,4},{1,5},{2,6},{3,7},{4,0},{5,1},{6,2},{7,3},{8,12},{9,13},{10,... | collective-permute-start | bytes 540680 | tf_op jit(solution)/shard_map/ppermute | solution.py:752
  39.6 5.4 %collective-permute-start.6 = (bf16[24,16,128]{2,1,0:T(8,128)(2,1)S(1)}, bf16[24,16,128]{2,1,0:T(8,128)(2,1)S(1)}, u32[]{:S(2)}, u32[]{:S(2)}) collective-permute-start(bf16[24,16,128]{2,1,0:T(8,128)(2,1)S(1)} %get-tuple-element.82), channel_id=1, source_target_pairs={{0,2},{1,3},{2,0},{3,1},{4,6},{5,7},{6,4},{7,5},{8,10},{9,11},{10,... | collective-permute-start | bytes 294920 | tf_op jit(solution)/shard_map/ppermute | solution.py:752
  41.9 13.0 %collective-permute-start.1 = (bf16[128,512]{1,0:T(8,128)(2,1)S(1)}, bf16[128,512]{1,0:T(8,128)(2,1)S(1)}, u32[]{:S(2)}, u32[]{:S(2)}) collective-permute-start(bf16[128,512]{1,0:T(8,128)(2,1)S(1)} %input_rim.1.rim_ref), channel_id=1, source_target_pairs={{0,28},{4,0},{8,4},{12,8},{16,12},{20,16},{24,20},{28,24},{1,29},{... | collective-permute-start | bytes 393224 | tf_op jit(solution)/shard_map/ppermute | solution.py:795
  46.8 8.9 %collective-permute-start.7 = (bf16[20,16,128]{2,1,0:T(8,128)(2,1)S(1)}, bf16[20,16,128]{2,1,0:T(8,128)(2,1)S(1)}, u32[]{:S(2)}, u32[]{:S(2)}) collective-permute-start(bf16[20,16,128]{2,1,0:T(8,128)(2,1)S(1)} %get-tuple-element.86), channel_id=1, source_target_pairs={{0,8},{1,9},{2,10},{3,11},{4,12},{5,13},{6,14},{7,15},{8,0},{9,1},... | collective-permute-start | bytes 245768 | tf_op jit(solution)/shard_map/ppermute | solution.py:752
  46.9 8.8 %collective-permute-start.8 = (bf16[20,16,128]{2,1,0:T(8,128)(2,1)S(1)}, bf16[20,16,128]{2,1,0:T(8,128)(2,1)S(1)}, u32[]{:S(2)}, u32[]{:S(2)}) collective-permute-start(bf16[20,16,128]{2,1,0:T(8,128)(2,1)S(1)} %get-tuple-element.87), channel_id=1, source_target_pairs={{0,16},{1,17},{2,18},{3,19},{4,20},{5,21},{6,22},{7,23},{8,24},{9,... | collective-permute-start | bytes 245768 | tf_op jit(solution)/shard_map/ppermute | solution.py:752
  49.1 6.6 %collective-permute-start.9 = (bf16[20,16,128]{2,1,0:T(8,128)(2,1)S(1)}, bf16[20,16,128]{2,1,0:T(8,128)(2,1)S(1)}, u32[]{:S(2)}, u32[]{:S(2)}) collective-permute-start(bf16[20,16,128]{2,1,0:T(8,128)(2,1)S(1)} %get-tuple-element.88), channel_id=1, source_target_pairs={{0,24},{1,25},{2,26},{3,27},{4,28},{5,29},{6,30},{7,31},{8,16},{9,... | collective-permute-start | bytes 245768 | tf_op jit(solution)/shard_map/ppermute | solution.py:752
